TPU v7x, 128 devices: a whole 4x4x4 slice. The times are simulated.
128 devices in a mesh: seq: 16 (over x, z), head: 4 (over y), batch: 2 (over core).
Axes of the slice: x: 4, y: 4, z: 4, core: 2. Of those that a mesh axis runs over, the one named last changes fastest.
Arguments:
- queries: bfloat16 [2, 8192, 32, 128], P('batch', 'seq', 'head'), may hold values from -200 to 200
- key_states: bfloat16 [2, 8192, 8, 128], P('batch', 'seq', 'head'), may hold values from -7 to 7
- value_vectors: bfloat16 [2, 8192, 8, 128], P('batch', 'seq', 'head'), may hold values from -6 to 6
- block_doc: int32 [2, 64], P('batch'), may hold values from 0 to 15, never falling along the last dimension, each value on 1 to 36 neighbouring positions
- out_weight: bfloat16 [4096, 8192], P('head', 'batch'), may hold values from -0.5 to 0.5
Outputs:
- projected: bfloat16 [8192, 2, 8192], P(('seq', 'head'), None, 'batch')
Inputs may be any that keep to these rules, and one draw needn't show every extreme that they name: block_doc[b, j] never falls along j, starts at 0 and skips no number; every document covers 1 to 36 whole blocks, and some document covers exactly 36.
All inputs are finite; a program needn't handle non-finite values.
Results may differ from a plain program's by a relative error of at most 0.0095.
Values may be sent and summed in bfloat16 or wider, within the bound.
No kernel may reach another device: no remote copies, remote signals or barrier semaphores. Data moves between devices by JAX's collectives and lax.ppermute only.
A program may use at most 128 MiB of HBM per device.

v0:
```python
import functools
import math

import jax
import jax.numpy as jnp
from jax import lax
from jax.experimental import pallas as pl
from jax.experimental.pallas import tpu as pltpu
from jax.sharding import PartitionSpec as P


XN = 4
ZN = 4
TOK = 512
BLK = 128
HD = 128
GRP = 4
BPD = TOK // BLK
REACH = 9
SLOTS = REACH + 1
SCALE = math.log2(math.e) / math.sqrt(HD)
NEG = -1e30


NAMES = (
    "own",
    "x1",
    "x2",
    "below_own",
    "below_x1",
    "below_x2",
    "above_mixed",
    "above_x1",
    "far_mixed",
    "far_x1",
    "corner",
)


def unit_source(name, x, z):
    below, above, far = (z + ZN - 1) % ZN, (z + 1) % ZN, (z + 2) % ZN
    at = {
        "own": (x, z),
        "x1": (x - 1, z),
        "x2": (x - 2, z),
        "below_own": (x, below),
        "below_x1": (x - 1, below),
        "below_x2": (x - 2, below),
        "above_mixed": (jnp.where(z == ZN - 1, x, x - 2), above),
        "above_x1": (x - 1, above),
        "far_mixed": (jnp.where(z >= 2, x, x - 2), far),
        "far_x1": (x - 1, far),
        "corner": (jnp.where(z == 0, x - 3, -1), ZN - 1),
    }[name]
    return ZN * at[0] + at[1]


APART = tuple((i, None) for i in range(len(NAMES)))
STACKED = (
    (0, 0),
    (0, 1),
    (0, 2),
    (1, 0),
    (1, 1),
    (1, 2),
    (2, 0),
    (2, 1),
    (3, None),
    (4, None),
    (5, None),
)


def attn_kernel(spec, n, span, doc_ref, q_ref, *refs):
    unit_refs = refs[:n]
    o_ref = refs[n]
    kv, qs, m_ref, l_ref, acc_ref, s_a, s_b, p_a, p_b, a_a, a_b, sems = refs[n + 1 :]
    s_idx = lax.axis_index("seq")
    x_idx = s_idx // ZN
    z_idx = s_idx % ZN
    first_doc = doc_ref[0, BPD * s_idx]

    copies = []
    for i, (operand, at) in enumerate(spec):
        src = unit_source(NAMES[i], x_idx, z_idx)
        delta = s_idx - src
        safe = jnp.maximum(src, 0)
        need = (
            (src >= 0)
            & (delta >= 0)
            & (delta <= REACH)
            & (doc_ref[0, BPD * safe + BPD - 1] >= first_doc)
        )
        slot = jnp.clip(delta, 0, REACH)
        unit = unit_refs[operand]
        if at is not None:
            unit = unit.at[at]
        copy = pltpu.make_async_copy(unit, kv.at[slot], sems.at[i])
        copies.append((need, copy))
    for need, copy in copies:
        pl.when(need)(copy.start)
    for need, copy in copies:
        pl.when(need)(copy.wait)

    def score(dst, slot, mask=None):
        s = lax.dot_general(
            qs[...], kv[slot, 0], (((1,), (1,)), ((), ())), preferred_element_type=jnp.float32
        )
        if mask is None:
            dst[...] = s
        else:
            for h in range(GRP):
                rows = slice(h * BLK, (h + 1) * BLK)
                dst[rows] = jnp.where(mask, s[rows], NEG)

    def soften(src, p_dst, a_dst):
        for h in range(GRP):
            rows = slice(h * BLK, (h + 1) * BLK)
            sh = src[rows]
            m_prev = m_ref[rows]
            m_new = jnp.maximum(m_prev, jnp.max(sh, axis=1, keepdims=True))
            m_wide = jnp.concatenate([m_new] * (TOK // HD), axis=1)
            p = jnp.exp2((sh - m_wide) * SCALE)
            alpha = jnp.exp2((m_prev - m_new) * SCALE)
            part_sum = p[:, 0:HD]
            for c in range(1, TOK // HD):
                part_sum = part_sum + p[:, c * HD : (c + 1) * HD]
            l_ref[rows] = l_ref[rows] * alpha + part_sum
            m_ref[rows] = m_new
            a_dst[rows] = alpha
            p_dst[rows] = p.astype(jnp.bfloat16)

    def mix(p_src, a_src, slot):
        pv = jnp.dot(p_src[...], kv[slot, 1], preferred_element_type=jnp.float32)
        acc_ref[...] = acc_ref[...] * a_src[...] + pv

    @pl.loop(span[0], span[1])
    def _(j):
        for h in range(GRP):
            qs[h * BLK : (h + 1) * BLK] = q_ref[
                pl.ds(pl.multiple_of(j * BLK, BLK), BLK), h * HD : (h + 1) * HD
            ]
        m_ref[...] = jnp.full_like(m_ref, NEG)
        l_ref[...] = jnp.zeros_like(l_ref)
        acc_ref[...] = jnp.zeros_like(acc_ref)
        doc_q = doc_ref[0, BPD * s_idx + j]
        full = jnp.int32(0)
        some = jnp.int32(0)
        for d in range(1, REACH + 1):
            src = s_idx - d
            safe = jnp.maximum(src, 0)
            valid = src >= 0
            full = full + (valid & (doc_ref[0, BPD * safe] == doc_q)).astype(jnp.int32)
            some = some + (valid & (doc_ref[0, BPD * safe + BPD - 1] == doc_q)).astype(jnp.int32)
        key_pos = lax.broadcasted_iota(jnp.int32, (BLK, TOK), 1)
        row_pos = lax.broadcasted_iota(jnp.int32, (BLK, TOK), 0) + j * BLK

        def hidden_keys(unit):
            hidden = jnp.int32(0)
            for b in range(BPD - 1):
                hidden = hidden + (doc_ref[0, BPD * unit + b] < doc_q).astype(jnp.int32)
            return hidden * BLK

        score(s_b, 0, (key_pos <= row_pos) & (key_pos >= hidden_keys(s_idx)))
        soften(s_b, p_b, a_b)

        edge = jnp.minimum(full + 1, REACH)

        @pl.when(some > full)
        def _():
            score(s_a, edge, key_pos >= hidden_keys(jnp.maximum(s_idx - edge, 0)))
            mix(p_b, a_b, 0)
            soften(s_a, p_b, a_b)

        pend = jnp.where(some > full, edge, 0)
        odd = full % 2

        @pl.when(odd == 1)
        def _():
            score(s_a, 1)
            mix(p_b, a_b, pend)
            soften(s_a, p_b, a_b)

        pend = jnp.where(odd == 1, 1, pend)

        @pl.when(full > 1)
        def _():
            score(s_a, 1 + odd)

        @pl.loop(0, full // 2)
        def _(i):
            t = 1 + odd + 2 * i
            score(s_b, t + 1)
            soften(s_a, p_a, a_a)
            mix(p_b, a_b, jnp.where(i == 0, pend, t - 1))
            score(s_a, jnp.minimum(t + 2, full))
            soften(s_b, p_b, a_b)
            mix(p_a, a_a, t)

        mix(p_b, a_b, jnp.where(full > 1, full, pend))

        for h in range(GRP):
            rows = slice(h * BLK, (h + 1) * BLK)
            total = jnp.sum(l_ref[rows], axis=1, keepdims=True)
            o_ref[pl.ds(pl.multiple_of((j - span[0]) * BLK, BLK), BLK), h * HD : (h + 1) * HD] = (
                acc_ref[rows] / total
            ).astype(o_ref.dtype)


def attention(doc, q, units, spec, span):
    n = len(units)
    return pl.pallas_call(
        functools.partial(attn_kernel, spec, n, span),
        name="attend",
        out_shape=jax.ShapeDtypeStruct(((span[1] - span[0]) * BLK, GRP * HD), jnp.bfloat16),
        in_specs=[
            pl.BlockSpec(memory_space=pltpu.SMEM),
            pl.BlockSpec(memory_space=pltpu.VMEM),
        ]
        + [pl.BlockSpec(memory_space=pl.ANY)] * n,
        out_specs=pl.BlockSpec(memory_space=pltpu.VMEM),
        scratch_shapes=[
            pltpu.VMEM((SLOTS, 2, TOK, HD), jnp.bfloat16),
            pltpu.VMEM((GRP * BLK, HD), jnp.bfloat16),
            pltpu.VMEM((GRP * BLK, HD), jnp.float32),
            pltpu.VMEM((GRP * BLK, HD), jnp.float32),
            pltpu.VMEM((GRP * BLK, HD), jnp.float32),
            pltpu.VMEM((GRP * BLK, TOK), jnp.float32),
            pltpu.VMEM((GRP * BLK, TOK), jnp.float32),
            pltpu.VMEM((GRP * BLK, TOK), jnp.bfloat16),
            pltpu.VMEM((GRP * BLK, TOK), jnp.bfloat16),
            pltpu.VMEM((GRP * BLK, HD), jnp.float32),
            pltpu.VMEM((GRP * BLK, HD), jnp.float32),
            pltpu.SemaphoreType.DMA((len(spec),)),
        ],
        compiler_params=pltpu.CompilerParams(vmem_limit_bytes=16 << 20),
        cost_estimate=pl.CostEstimate(
            flops=(span[1] - span[0]) * 1_500_000_000,
            bytes_accessed=4_000_000,
            transcendentals=(span[1] - span[0]) * 2_000_000,
        ),
    )(doc, q, *units)


def along_z(v, step):
    pairs = [(ZN * x + z, ZN * x + (z + step) % ZN) for x in range(XN) for z in range(ZN)]
    return lax.ppermute(v, "seq", pairs)


def along_x(v, first_row):
    pairs = [(ZN * x + z, ZN * (x + 1) + z) for x in range(first_row, XN - 1) for z in range(ZN)]
    return lax.ppermute(v, "seq", pairs)


def from_corner(own):
    return lax.ppermute(own, "seq", [(ZN - 1, ZN * (XN - 1))])


def gather_apart(own, z):
    x1 = along_x(own, 0)
    below_own = along_z(own, 1)
    corner = from_corner(own)
    x2 = along_x(x1, 1)
    below_x1 = along_z(x1, 1)
    above_x1 = along_z(x1, -1)
    below_x2 = along_z(x2, 1)
    above_mixed = along_z(jnp.where(z == 0, own, x2), -1)
    far_x1 = along_z(above_x1, -1)
    far_mixed = along_z(jnp.where((z == 1) | (z == 2), below_own, below_x2), 1)
    return [
        own,
        x1,
        x2,
        below_own,
        below_x1,
        below_x2,
        above_mixed,
        above_x1,
        far_mixed,
        far_x1,
        corner,
    ]


def add_kernel(turn, ra_ref, rb_ref, p_ref, na_ref, nb_ref):
    rows, half = ra_ref.shape
    n = lax.axis_size("head")
    me = lax.axis_index("head")
    ka = pl.multiple_of((me + 2 * n - 2 - turn) % n * rows, rows)
    kb = pl.multiple_of((me + 2 + turn) % n * rows, rows)
    na_ref[...] = ra_ref[...] + p_ref[pl.ds(ka, rows), :half]
    nb_ref[...] = rb_ref[...] + p_ref[pl.ds(kb, rows), half:]


def ring_add(turn, ra, rb, partial):
    return pl.pallas_call(
        functools.partial(add_kernel, turn),
        name="ring_add",
        out_shape=[jax.ShapeDtypeStruct(ra.shape, ra.dtype)] * 2,
        in_specs=[pl.BlockSpec(memory_space=pltpu.VMEM)] * 3,
        out_specs=[pl.BlockSpec(memory_space=pltpu.VMEM)] * 2,
        compiler_params=pltpu.CompilerParams(vmem_limit_bytes=16 << 20),
        cost_estimate=pl.CostEstimate(
            flops=100_000_000, bytes_accessed=12 * ra.size, transcendentals=0
        ),
    )(ra, rb, partial)


def around(v, step):
    n = lax.axis_size("head")
    return lax.ppermute(v, "head", [(i, (i + step) % n) for i in range(n)])


def first_blocks(partial):
    me = lax.axis_index("head")
    n = lax.axis_size("head")
    rows = partial.shape[0] // n
    half = partial.shape[1] // 2
    a = lax.dynamic_slice(partial, ((me + n - 1) % n * rows, 0), (rows, half))
    b = lax.dynamic_slice(partial, ((me + 1) % n * rows, half), (rows, half))
    return a, b


def ring_step(turn, a, b, partial):
    a = around(a, 1)
    b = around(b, -1)
    return ring_add(turn, a, b, partial)


def swapped(v):
    return lax.ppermute(v, "batch", [(0, 1), (1, 0)])


def on_device(queries, key_states, value_vectors, block_doc, out_weight):
    core = lax.axis_index("batch")
    first = core == 0
    q2 = queries[0].reshape(TOK, 2 * GRP * HD)
    halves_q = (q2[:, : GRP * HD], q2[:, GRP * HD :])
    halves_kv = tuple(
        jnp.stack([key_states[0, :, h], value_vectors[0, :, h]], axis=0) for h in range(2)
    )
    kv_mine = jnp.where(first, halves_kv[0], halves_kv[1])
    kv_theirs = swapped(jnp.where(first, halves_kv[1], halves_kv[0]))
    q_mine = jnp.where(first, halves_q[0], halves_q[1])
    q_theirs = swapped(jnp.where(first, halves_q[1], halves_q[0]))
    doc_theirs = swapped(block_doc)

    def of(sequence, mine, theirs):
        return jnp.where(core == sequence, mine, theirs)

    def project(attended):
        other = swapped(attended)
        both = jnp.where(
            first,
            jnp.concatenate([attended, other], axis=1),
            jnp.concatenate([other, attended], axis=1),
        )
        return jnp.dot(both, out_weight, preferred_element_type=jnp.float32).astype(jnp.bfloat16)

    tie = lax.optimization_barrier
    z = lax.axis_index("seq") % ZN
    units0 = gather_apart(of(0, kv_mine, kv_theirs), z)

    own1, units0[2] = tie((of(1, kv_mine, kv_theirs), units0[2]))
    y1 = along_x(own1, 0)
    y2 = along_x(y1, 1)
    stack1 = jnp.stack([own1, y1, y2])
    up1 = jnp.stack([jnp.where(z == 0, own1, y2), y1])
    units0, stack1, up1 = tie((units0, stack1, up1))
    below1 = along_z(stack1, 1)
    above1 = along_z(up1, -1)
    corner1 = from_corner(own1)
    attended0 = attention(
        of(0, block_doc, doc_theirs), of(0, q_mine, q_theirs), units0, APART, (0, BPD)
    )
    partial0 = project(attended0)
    a0, b0 = first_blocks(partial0)

    (below1, above1), _ = tie(((below1, above1), (a0, b0)))
    far_mixed1 = along_z(jnp.where((z == 1) | (z == 2), below1[0], below1[2]), 1)
    far_x1 = along_z(above1[1], -1)
    units1 = [stack1, below1, above1, far_mixed1, far_x1, corner1]
    doc1, q1 = of(1, block_doc, doc_theirs), of(1, q_mine, q_theirs)
    a0, b0 = ring_step(0, a0, b0, partial0)
    upper = attention(doc1, q1, units1, STACKED, (0, BPD // 2))
    a0, b0 = ring_step(1, a0, b0, partial0)
    lower = attention(doc1, q1, units1, STACKED, (BPD // 2, BPD))
    a0, b0 = ring_step(2, a0, b0, partial0)
    partial1 = project(jnp.concatenate([upper, lower], axis=0))
    a1, b1 = first_blocks(partial1)
    for turn in range(3):
        a1, b1 = ring_step(turn, a1, b1, partial1)
    sum0 = jnp.concatenate([a0, b0], axis=1)
    sum1 = jnp.concatenate([a1, b1], axis=1)
    return jnp.stack([sum0, sum1], axis=1)


def solution(mesh):
    return jax.shard_map(
        on_device,
        mesh=mesh,
        in_specs=(
            P("batch", "seq", "head", None),
            P("batch", "seq", "head", None),
            P("batch", "seq", "head", None),
            P("batch", None),
            P("head", "batch"),
        ),
        out_specs=P(("seq", "head"), None, "batch"),
        check_vma=False,
    )
```

profile of v0, /device:TPU:36, one launch (start us, length us, event | category | flops | bytes accessed | tf_op | source)
XLA Modules:
  0.0 198.2 jit_solution(7733789174322065486)
XLA Ops:
  5.0 3.1 %collective-permute-start.3 = (bf16[2,512,128]{2,1,0:T(8,128)(2,1)S(1)}, bf16[2,512,128]{2,1,0:T(8,128)(2,1)S(1)}, u32[]{:S(2)}, u32[]{:S(2)}) collective-permute-start(bf16[2,512,128]{2,1,0:T(8,128)(2,1)S(1)} %get-tuple-element.36.refs_0_), channel_id=1, source_target_pairs={{0,32},{8,40},{16,48},{24,56},{32,64},{40,72},{48,80},{56,88},{64,... | collective-permute-start | bytes 786440 | tf_op jit(solution)/shard_map/ppermute | solution.py:252
  8.2 7.0 %collective-permute-done.3.refs_1_ = bf16[2,512,128]{2,1,0:T(8,128)(2,1)S(1)} collective-permute-done((bf16[2,512,128]{2,1,0:T(8,128)(2,1)S(1)}, bf16[2,512,128]{2,1,0:T(8,128)(2,1)S(1)}, u32[]{:S(2)}, u32[]{:S(2)}) %collective-permute-start.3) | collective-permute-done | bytes 262176 | tf_op jit(solution)/shard_map/ppermute | solution.py:252
  15.2 3.1 %collective-permute-start.4 = (bf16[2,512,128]{2,1,0:T(8,128)(2,1)S(1)}, bf16[2,512,128]{2,1,0:T(8,128)(2,1)S(1)}, u32[]{:S(2)}, u32[]{:S(2)}) collective-permute-start(bf16[2,512,128]{2,1,0:T(8,128)(2,1)S(1)} %collective-permute-done.3.refs_1_), channel_id=1, source_target_pairs={{32,64},{40,72},{48,80},{56,88},{64,96},{72,104},{80,112},{88,120}... | collective-permute-start | bytes 786440 | tf_op jit(solution)/shard_map/ppermute | solution.py:252
  24.6 3.1 %collective-permute-start.13 = (bf16[2,512,128]{2,1,0:T(8,128)(2,1)S(1)}, bf16[2,512,128]{2,1,0:T(8,128)(2,1)S(1)}, u32[]{:S(2)}, u32[]{:S(2)}) collective-permute-start(bf16[2,512,128]{2,1,0:T(8,128)(2,1)S(1)} %get-tuple-element.35), channel_id=1, source_target_pairs={{0,32},{8,40},{16,48},{24,56},{32,64},{40,72},{48,80},{56,88},{64,... | collective-permute-start | bytes 786440 | tf_op jit(solution)/shard_map/ppermute | solution.py:252
  29.8 3.3 %collective-permute-done.13 = bf16[2,512,128]{2,1,0:T(8,128)(2,1)S(1)} collective-permute-done((bf16[2,512,128]{2,1,0:T(8,128)(2,1)S(1)}, bf16[2,512,128]{2,1,0:T(8,128)(2,1)S(1)}, u32[]{:S(2)}, u32[]{:S(2)}) %collective-permute-start.13) | collective-permute-done | bytes 262176 | tf_op jit(solution)/shard_map/ppermute | solution.py:252
  33.1 3.1 %collective-permute-start.14 = (bf16[2,512,128]{2,1,0:T(8,128)(2,1)S(1)}, bf16[2,512,128]{2,1,0:T(8,128)(2,1)S(1)}, u32[]{:S(2)}, u32[]{:S(2)}) collective-permute-start(bf16[2,512,128]{2,1,0:T(8,128)(2,1)S(1)} %collective-permute-done.13), channel_id=1, source_target_pairs={{32,64},{40,72},{48,80},{56,88},{64,96},{72,104},{80,112},{88,120}... | collective-permute-start | bytes 786440 | tf_op jit(solution)/shard_map/ppermute | solution.py:252
  44.4 4.6 %collective-permute-done.11.refs_9_ = bf16[2,512,128]{2,1,0:T(8,128)(2,1)S(1)} collective-permute-done((bf16[2,512,128]{2,1,0:T(8,128)(2,1)S(1)}, bf16[2,512,128]{2,1,0:T(8,128)(2,1)S(1)}, u32[]{:S(2)}, u32[]{:S(2)}) %collective-permute-start.11) | collective-permute-done | bytes 262176 | tf_op jit(solution)/shard_map/ppermute | solution.py:247
  49.1 13.8 %attend.3 = bf16[512,512]{1,0:T(8,128)(2,1)S(1)} custom-call(s32[1,64]{1,0:T(1,128)S(1)} %get-tuple-element.75.doc_ref, bf16[512,512]{1,0:T(8,128)(2,1)S(1)} %get-tuple-element.67.q_ref, bf16[2,512,128]{2,1,0:T(8,128)(2,1)S(1)} %get-tuple-element.36.refs_0_, bf16[2,512,128]{2,1,0:T(8,128)(2,1)S(1)} %collective-permute-done.3.refs_1_, ...), custom_call_target="tpu_custom_call" | custom-call | flops 6000000000 | bytes 4000000 | tf_op jit(solution)/shard_map/attend/pallas_call | solution.py:212
  64.5 3.1 %collective-permute-start.22 = (bf16[3,2,512,128]{3,2,1,0:T(8,128)(2,1)S(1)}, bf16[3,2,512,128]{3,2,1,0:T(8,128)(2,1)S(1)}, u32[]{:S(2)}, u32[]{:S(2)}) collective-permute-start(bf16[3,2,512,128]{3,2,1,0:T(8,128)(2,1)S(1)} %pad_maximum_fusion.1.refs_0_), channel_id=1, source_target_pairs={{0,8},{8,16},{16,24},{24,0},{32,40},{40,48},{48,56},{56,32},{64,72... | collective-permute-start | bytes 2359304 | tf_op jit(solution)/shard_map/ppermute | solution.py:247
  67.7 8.2 %convolution_convert_fusion.1.p_ref = bf16[512,4096]{1,0:T(8,128)(2,1)S(1)} fusion(bf16[1024,4096]{1,0:T(8,128)(2,1)} %param.9, bf16[512,512]{1,0:T(8,128)(2,1)} %collective-permute-done.15, bf16[512,512]{1,0:T(8,128)(2,1)S(1)} %attend.3, pred[]{:T(512)S(6)} %eq.29), kind=kOutput, calls=%fused_computation.1 | convolution fusion | flops 4301783040 | bytes 13631489 | tf_op jit(solution)/shard_map/dot_general | solution.py:358
  76.0 3.9 %collective-permute-done.23.refs_2_ = bf16[2,2,512,128]{3,2,1,0:T(8,128)(2,1)S(1)} collective-permute-done((bf16[2,2,512,128]{3,2,1,0:T(8,128)(2,1)S(1)}, bf16[2,2,512,128]{3,2,1,0:T(8,128)(2,1)S(1)}, u32[]{:S(2)}, u32[]{:S(2)}) %collective-permute-start.23) | collective-permute-done | bytes 524320 | tf_op jit(solution)/shard_map/ppermute | solution.py:247
  79.9 9.3 %collective-permute-done.22.refs_1_ = bf16[3,2,512,128]{3,2,1,0:T(8,128)(2,1)S(1)} collective-permute-done((bf16[3,2,512,128]{3,2,1,0:T(8,128)(2,1)S(1)}, bf16[3,2,512,128]{3,2,1,0:T(8,128)(2,1)S(1)}, u32[]{:S(2)}, u32[]{:S(2)}) %collective-permute-start.22) | collective-permute-done | bytes 786464 | tf_op jit(solution)/shard_map/ppermute | solution.py:247
  89.3 3.0 %collective-permute-start.25 = (bf16[2,512,128]{2,1,0:T(8,128)(2,1)S(1)}, bf16[2,512,128]{2,1,0:T(8,128)(2,1)S(1)}, u32[]{:S(2)}, u32[]{:S(2)}) collective-permute-start(bf16[2,512,128]{2,1,0:T(8,128)(2,1)S(1)} %slice_bitcast_fusion), channel_id=1, source_target_pairs={{0,24},{8,0},{16,8},{24,16},{32,56},{40,32},{48,40},{56,48},{64,88... | collective-permute-start | bytes 786440 | tf_op jit(solution)/shard_map/ppermute | solution.py:247
  92.4 5.0 %collective-permute-done.25.refs_4_ = bf16[2,512,128]{2,1,0:T(8,128)(2,1)S(1)} collective-permute-done((bf16[2,512,128]{2,1,0:T(8,128)(2,1)S(1)}, bf16[2,512,128]{2,1,0:T(8,128)(2,1)S(1)}, u32[]{:S(2)}, u32[]{:S(2)}) %collective-permute-start.25) | collective-permute-done | bytes 262176 | tf_op jit(solution)/shard_map/ppermute | solution.py:247
  99.6 10.0 %attend.5 = bf16[256,512]{1,0:T(8,128)(2,1)S(1)} custom-call(s32[1,64]{1,0:T(1,128)S(1)} %get-tuple-element.76.doc_ref, bf16[512,512]{1,0:T(8,128)(2,1)S(1)} %get-tuple-element.68.q_ref, bf16[3,2,512,128]{3,2,1,0:T(8,128)(2,1)S(1)} %pad_maximum_fusion.1.refs_0_, bf16[3,2,512,128]{3,2,1,0:T(8,128)(2,1)S(1)} %collective-permute-done.22.refs_1_, ...), custom_call_target="tpu_custom_call" | custom-call | flops 3000000000 | bytes 4000000 | tf_op jit(solution)/shard_map/attend/pallas_call | solution.py:212
  109.6 10.0 %attend.4 = bf16[256,512]{1,0:T(8,128)(2,1)S(1)} custom-call(s32[1,64]{1,0:T(1,128)S(1)} %get-tuple-element.76.doc_ref, bf16[512,512]{1,0:T(8,128)(2,1)S(1)} %get-tuple-element.68.q_ref, bf16[3,2,512,128]{3,2,1,0:T(8,128)(2,1)S(1)} %pad_maximum_fusion.1.refs_0_, bf16[3,2,512,128]{3,2,1,0:T(8,128)(2,1)S(1)} %collective-permute-done.22.refs_1_, ...), custom_call_target="tpu_custom_call" | custom-call | flops 3000000000 | bytes 4000000 | tf_op jit(solution)/shard_map/attend/pallas_call | solution.py:212
  119.8 3.1 %collective-permute-start.17 = (bf16[128,2048]{1,0:T(8,128)(2,1)S(1)}, bf16[128,2048]{1,0:T(8,128)(2,1)S(1)}, u32[]{:S(2)}, u32[]{:S(2)}) collective-permute-start(bf16[128,2048]{1,0:T(8,128)(2,1)S(1)} %get-tuple-element.65), channel_id=1, source_target_pairs={{0,6},{2,0},{4,2},{6,4},{1,7},{3,1},{5,3},{7,5},{8,14},{10,8},{12,... | collective-permute-start | bytes 1572872 | tf_op jit(solution)/shard_map/ppermute | solution.py:311
  122.9 4.8 %convolution_convert_fusion.p_ref = bf16[512,4096]{1,0:T(8,128)(2,1)S(1)} fusion(bf16[1024,4096]{1,0:T(8,128)(2,1)S(1)} %bitcast.36, bf16[512,512]{1,0:T(8,128)(2,1)S(1)} %collective-permute-done.27, bf16[256,512]{1,0:T(8,128)(2,1)S(1)} %attend.5, bf16[256,512]{1,0:T(8,128)(2,1)S(1)} %attend.4, pred[]{:T(512)S(6)} %eq.29), kind=kOutput, calls=%fused_computation | convolution fusion | flops 4303880192 | bytes 13631489 | tf_op jit(solution)/shard_map/dot_general | solution.py:358
  127.8 3.3 %collective-permute-start.29 = (bf16[128,2048]{1,0:T(8,128)(2,1)S(1)}, bf16[128,2048]{1,0:T(8,128)(2,1)S(1)}, u32[]{:S(2)}, u32[]{:S(2)}) collective-permute-start(bf16[128,2048]{1,0:T(8,128)(2,1)S(1)} %get-tuple-element.63), channel_id=1, source_target_pairs={{0,6},{2,0},{4,2},{6,4},{1,7},{3,1},{5,3},{7,5},{8,14},{10,8},{12,... | collective-permute-start | bytes 1572872 | tf_op jit(solution)/shard_map/ppermute | solution.py:311
  131.1 4.1 %collective-permute-done.17.rb_ref = bf16[128,2048]{1,0:T(8,128)(2,1)S(1)} collective-permute-done((bf16[128,2048]{1,0:T(8,128)(2,1)S(1)}, bf16[128,2048]{1,0:T(8,128)(2,1)S(1)}, u32[]{:S(2)}, u32[]{:S(2)}) %collective-permute-start.17) | collective-permute-done | bytes 524320 | tf_op jit(solution)/shard_map/ppermute | solution.py:311
  135.2 3.7 %collective-permute-done.16.ra_ref = bf16[128,2048]{1,0:T(8,128)(2,1)S(1)} collective-permute-done((bf16[128,2048]{1,0:T(8,128)(2,1)S(1)}, bf16[128,2048]{1,0:T(8,128)(2,1)S(1)}, u32[]{:S(2)}, u32[]{:S(2)}) %collective-permute-start.16) | collective-permute-done | bytes 524320 | tf_op jit(solution)/shard_map/ppermute | solution.py:311
  139.1 3.2 %collective-permute-start.19 = (bf16[128,2048]{1,0:T(8,128)(2,1)S(1)}, bf16[128,2048]{1,0:T(8,128)(2,1)S(1)}, u32[]{:S(2)}, u32[]{:S(2)}) collective-permute-start(bf16[128,2048]{1,0:T(8,128)(2,1)S(1)} %get-tuple-element.48), channel_id=1, source_target_pairs={{0,6},{2,0},{4,2},{6,4},{1,7},{3,1},{5,3},{7,5},{8,14},{10,8},{12,... | collective-permute-start | bytes 1572872 | tf_op jit(solution)/shard_map/ppermute | solution.py:311
  142.3 4.1 %collective-permute-done.29.rb_ref = bf16[128,2048]{1,0:T(8,128)(2,1)S(1)} collective-permute-done((bf16[128,2048]{1,0:T(8,128)(2,1)S(1)}, bf16[128,2048]{1,0:T(8,128)(2,1)S(1)}, u32[]{:S(2)}, u32[]{:S(2)}) %collective-permute-start.29) | collective-permute-done | bytes 524320 | tf_op jit(solution)/shard_map/ppermute | solution.py:311
  146.4 3.7 %collective-permute-done.28.ra_ref = bf16[128,2048]{1,0:T(8,128)(2,1)S(1)} collective-permute-done((bf16[128,2048]{1,0:T(8,128)(2,1)S(1)}, bf16[128,2048]{1,0:T(8,128)(2,1)S(1)}, u32[]{:S(2)}, u32[]{:S(2)}) %collective-permute-start.28) | collective-permute-done | bytes 524320 | tf_op jit(solution)/shard_map/ppermute | solution.py:311
  150.3 3.2 %collective-permute-start.31 = (bf16[128,2048]{1,0:T(8,128)(2,1)S(1)}, bf16[128,2048]{1,0:T(8,128)(2,1)S(1)}, u32[]{:S(2)}, u32[]{:S(2)}) collective-permute-start(bf16[128,2048]{1,0:T(8,128)(2,1)S(1)} %get-tuple-element.58), channel_id=1, source_target_pairs={{0,6},{2,0},{4,2},{6,4},{1,7},{3,1},{5,3},{7,5},{8,14},{10,8},{12,... | collective-permute-start | bytes 1572872 | tf_op jit(solution)/shard_map/ppermute | solution.py:311
  153.5 7.8 %collective-permute-done.18.ra_ref = bf16[128,2048]{1,0:T(8,128)(2,1)S(1)} collective-permute-done((bf16[128,2048]{1,0:T(8,128)(2,1)S(1)}, bf16[128,2048]{1,0:T(8,128)(2,1)S(1)}, u32[]{:S(2)}, u32[]{:S(2)}) %collective-permute-start.18) | collective-permute-done | bytes 524320 | tf_op jit(solution)/shard_map/ppermute | solution.py:311
  161.6 3.2 %collective-permute-start.21 = (bf16[128,2048]{1,0:T(8,128)(2,1)S(1)}, bf16[128,2048]{1,0:T(8,128)(2,1)S(1)}, u32[]{:S(2)}, u32[]{:S(2)}) collective-permute-start(bf16[128,2048]{1,0:T(8,128)(2,1)S(1)} %get-tuple-element.50), channel_id=1, source_target_pairs={{0,6},{2,0},{4,2},{6,4},{1,7},{3,1},{5,3},{7,5},{8,14},{10,8},{12,... | collective-permute-start | bytes 1572872 | tf_op jit(solution)/shard_map/ppermute | solution.py:311
  164.8 7.8 %collective-permute-done.30.ra_ref = bf16[128,2048]{1,0:T(8,128)(2,1)S(1)} collective-permute-done((bf16[128,2048]{1,0:T(8,128)(2,1)S(1)}, bf16[128,2048]{1,0:T(8,128)(2,1)S(1)}, u32[]{:S(2)}, u32[]{:S(2)}) %collective-permute-start.30) | collective-permute-done | bytes 524320 | tf_op jit(solution)/shard_map/ppermute | solution.py:311
  172.8 3.2 %collective-permute-start.33 = (bf16[128,2048]{1,0:T(8,128)(2,1)S(1)}, bf16[128,2048]{1,0:T(8,128)(2,1)S(1)}, u32[]{:S(2)}, u32[]{:S(2)}) collective-permute-start(bf16[128,2048]{1,0:T(8,128)(2,1)S(1)} %get-tuple-element.60), channel_id=1, source_target_pairs={{0,6},{2,0},{4,2},{6,4},{1,7},{3,1},{5,3},{7,5},{8,14},{10,8},{12,... | collective-permute-start | bytes 1572872 | tf_op jit(solution)/shard_map/ppermute | solution.py:311
  176.0 7.8 %collective-permute-done.20.ra_ref = bf16[128,2048]{1,0:T(8,128)(2,1)S(1)} collective-permute-done((bf16[128,2048]{1,0:T(8,128)(2,1)S(1)}, bf16[128,2048]{1,0:T(8,128)(2,1)S(1)}, u32[]{:S(2)}, u32[]{:S(2)}) %collective-permute-start.20) | collective-permute-done | bytes 524320 | tf_op jit(solution)/shard_map/ppermute | solution.py:311
  184.0 10.2 %collective-permute-done.32.ra_ref = bf16[128,2048]{1,0:T(8,128)(2,1)S(1)} collective-permute-done((bf16[128,2048]{1,0:T(8,128)(2,1)S(1)}, bf16[128,2048]{1,0:T(8,128)(2,1)S(1)}, u32[]{:S(2)}, u32[]{:S(2)}) %collective-permute-start.32) | collective-permute-done | bytes 524320 | tf_op jit(solution)/shard_map/ppermute | solution.py:311
  194.7 3.5 %copy.10 = bf16[128,2,4096]{2,1,0:T(2,128)(2,1)} copy(bf16[128,2,4096]{2,0,1:T(8,128)(2,1)S(1)} %pad_maximum_fusion) | data formatting | bytes 4194304 | tf_op jit(solution)/shard_map/stack | solution.py:395
  (80 shorter events, 27.1 us)
Async XLA Ops:
  5.0 10.2 %collective-permute-start.3 = (bf16[2,512,128]{2,1,0:T(8,128)(2,1)S(1)}, bf16[2,512,128]{2,1,0:T(8,128)(2,1)S(1)}, u32[]{:S(2)}, u32[]{:S(2)}) collective-permute-start(bf16[2,512,128]{2,1,0:T(8,128)(2,1)S(1)} %get-tuple-element.36.refs_0_), channel_id=1, source_target_pairs={{0,32},{8,40},{16,48},{24,56},{32,64},{40,72},{48,80},{56,88},{64,... | collective-permute-start | bytes 786440 | tf_op jit(solution)/shard_map/ppermute | solution.py:252
  8.1 19.5 %collective-permute-start.1 = (bf16[512,512]{1,0:T(8,128)(2,1)S(1)}, bf16[512,512]{1,0:T(8,128)(2,1)S(1)}, u32[]{:S(2)}, u32[]{:S(2)}) collective-permute-start(bf16[512,512]{1,0:T(8,128)(2,1)S(1)} %broadcast_select_fusion.2), channel_id=1, source_target_pairs={{0,1},{1,0},{2,3},{3,2},{4,5},{5,4},{6,7},{7,6},{8,9},{9,8},{10,11... | collective-permute-start | bytes 1572872 | tf_op jit(solution)/shard_map/ppermute | solution.py:331
  15.2 9.4 %collective-permute-start.4 = (bf16[2,512,128]{2,1,0:T(8,128)(2,1)S(1)}, bf16[2,512,128]{2,1,0:T(8,128)(2,1)S(1)}, u32[]{:S(2)}, u32[]{:S(2)}) collective-permute-start(bf16[2,512,128]{2,1,0:T(8,128)(2,1)S(1)} %collective-permute-done.3.refs_1_), channel_id=1, source_target_pairs={{32,64},{40,72},{48,80},{56,88},{64,96},{72,104},{80,112},{88,120}... | collective-permute-start | bytes 786440 | tf_op jit(solution)/shard_map/ppermute | solution.py:252
  19.6 23.9 %collective-permute-start.12 = (bf16[2,512,128]{2,1,0:T(8,128)(2,1)S(1)}, bf16[2,512,128]{2,1,0:T(8,128)(2,1)S(1)}, u32[]{:S(2)}, u32[]{:S(2)}) collective-permute-start(bf16[2,512,128]{2,1,0:T(8,128)(2,1)S(1)} %get-tuple-element.36.refs_0_), channel_id=1, source_target_pairs={{24,96},{25,97},{26,98},{27,99},{28,100},{29,101},{30,102},{31,103}} | collective-permute-start | bytes 786440 | tf_op jit(solution)/shard_map/ppermute | solution.py:256
  20.2 16.0 %collective-permute-start.5 = (bf16[2,512,128]{2,1,0:T(8,128)(2,1)S(1)}, bf16[2,512,128]{2,1,0:T(8,128)(2,1)S(1)}, u32[]{:S(2)}, u32[]{:S(2)}) collective-permute-start(bf16[2,512,128]{2,1,0:T(8,128)(2,1)S(1)} %get-tuple-element.36.refs_0_), channel_id=1, source_target_pairs={{0,8},{8,16},{16,24},{24,0},{32,40},{40,48},{48,56},{56,32},{64,72... | collective-permute-start | bytes 786440 | tf_op jit(solution)/shard_map/ppermute | solution.py:247
  22.2 16.0 %collective-permute-start.9 = (bf16[2,512,128]{2,1,0:T(8,128)(2,1)S(1)}, bf16[2,512,128]{2,1,0:T(8,128)(2,1)S(1)}, u32[]{:S(2)}, u32[]{:S(2)}) collective-permute-start(bf16[2,512,128]{2,1,0:T(8,128)(2,1)S(1)} %collective-permute-done.3.refs_1_), channel_id=1, source_target_pairs={{0,24},{8,0},{16,8},{24,16},{32,56},{40,32},{48,40},{56,48},{64,88... | collective-permute-start | bytes 786440 | tf_op jit(solution)/shard_map/ppermute | solution.py:247
  24.6 8.5 %collective-permute-start.13 = (bf16[2,512,128]{2,1,0:T(8,128)(2,1)S(1)}, bf16[2,512,128]{2,1,0:T(8,128)(2,1)S(1)}, u32[]{:S(2)}, u32[]{:S(2)}) collective-permute-start(bf16[2,512,128]{2,1,0:T(8,128)(2,1)S(1)} %get-tuple-element.35), channel_id=1, source_target_pairs={{0,32},{8,40},{16,48},{24,56},{32,64},{40,72},{48,80},{56,88},{64,... | collective-permute-start | bytes 786440 | tf_op jit(solution)/shard_map/ppermute | solution.py:252
  27.7 10.7 %collective-permute-start.7 = (bf16[2,512,128]{2,1,0:T(8,128)(2,1)S(1)}, bf16[2,512,128]{2,1,0:T(8,128)(2,1)S(1)}, u32[]{:S(2)}, u32[]{:S(2)}) collective-permute-start(bf16[2,512,128]{2,1,0:T(8,128)(2,1)S(1)} %collective-permute-done.4.refs_2_), channel_id=1, source_target_pairs={{0,8},{8,16},{16,24},{24,0},{32,40},{40,48},{48,56},{56,32},{64,72... | collective-permute-start | bytes 786440 | tf_op jit(solution)/shard_map/ppermute | solution.py:247
  33.1 8.3 %collective-permute-start.14 = (bf16[2,512,128]{2,1,0:T(8,128)(2,1)S(1)}, bf16[2,512,128]{2,1,0:T(8,128)(2,1)S(1)}, u32[]{:S(2)}, u32[]{:S(2)}) collective-permute-start(bf16[2,512,128]{2,1,0:T(8,128)(2,1)S(1)} %collective-permute-done.13), channel_id=1, source_target_pairs={{32,64},{40,72},{48,80},{56,88},{64,96},{72,104},{80,112},{88,120}... | collective-permute-start | bytes 786440 | tf_op jit(solution)/shard_map/ppermute | solution.py:252
  36.2 8.2 %collective-permute-start.6 = (bf16[2,512,128]{2,1,0:T(8,128)(2,1)S(1)}, bf16[2,512,128]{2,1,0:T(8,128)(2,1)S(1)}, u32[]{:S(2)}, u32[]{:S(2)}) collective-permute-start(bf16[2,512,128]{2,1,0:T(8,128)(2,1)S(1)} %collective-permute-done.3.refs_1_), channel_id=1, source_target_pairs={{0,8},{8,16},{16,24},{24,0},{32,40},{40,48},{48,56},{56,32},{64,72... | collective-permute-start | bytes 786440 | tf_op jit(solution)/shard_map/ppermute | solution.py:247
  38.2 10.8 %collective-permute-start.8 = (bf16[2,512,128]{2,1,0:T(8,128)(2,1)S(1)}, bf16[2,512,128]{2,1,0:T(8,128)(2,1)S(1)}, u32[]{:S(2)}, u32[]{:S(2)}) collective-permute-start(bf16[2,512,128]{2,1,0:T(8,128)(2,1)S(1)} %broadcast_select_fusion.5), channel_id=1, source_target_pairs={{0,24},{8,0},{16,8},{24,16},{32,56},{40,32},{48,40},{56,48},{64,88... | collective-permute-start | bytes 786440 | tf_op jit(solution)/shard_map/ppermute | solution.py:247
  38.3 10.7 %collective-permute-start.11 = (bf16[2,512,128]{2,1,0:T(8,128)(2,1)S(1)}, bf16[2,512,128]{2,1,0:T(8,128)(2,1)S(1)}, u32[]{:S(2)}, u32[]{:S(2)}) collective-permute-start(bf16[2,512,128]{2,1,0:T(8,128)(2,1)S(1)} %collective-permute-done.9.refs_7_), channel_id=1, source_target_pairs={{0,24},{8,0},{16,8},{24,16},{32,56},{40,32},{48,40},{56,48},{64,88... | collective-permute-start | bytes 786440 | tf_op jit(solution)/shard_map/ppermute | solution.py:247
  41.3 7.7 %collective-permute-start.10 = (bf16[2,512,128]{2,1,0:T(8,128)(2,1)S(1)}, bf16[2,512,128]{2,1,0:T(8,128)(2,1)S(1)}, u32[]{:S(2)}, u32[]{:S(2)}) collective-permute-start(bf16[2,512,128]{2,1,0:T(8,128)(2,1)S(1)} %broadcast_select_fusion.4), channel_id=1, source_target_pairs={{0,8},{8,16},{16,24},{24,0},{32,40},{40,48},{48,56},{56,32},{64,72... | collective-permute-start | bytes 786440 | tf_op jit(solution)/shard_map/ppermute | solution.py:247
  62.9 4.7 %collective-permute-start.15 = (bf16[512,512]{1,0:T(8,128)(2,1)S(1)}, bf16[512,512]{1,0:T(8,128)(2,1)}, u32[]{:S(2)}, u32[]{:S(2)}) collective-permute-start(bf16[512,512]{1,0:T(8,128)(2,1)S(1)} %attend.3), channel_id=1, source_target_pairs={{0,1},{1,0},{2,3},{3,2},{4,5},{5,4},{6,7},{7,6},{8,9},{9,8},{10,11... | collective-permute-start | bytes 1572872 | tf_op jit(solution)/shard_map/ppermute | solution.py:331
  63.1 29.3 %collective-permute-start.26 = (bf16[2,512,128]{2,1,0:T(8,128)(2,1)S(1)}, bf16[2,512,128]{2,1,0:T(8,128)(2,1)S(1)}, u32[]{:S(2)}, u32[]{:S(2)}) collective-permute-start(bf16[2,512,128]{2,1,0:T(8,128)(2,1)S(1)} %get-tuple-element.35), channel_id=1, source_target_pairs={{24,96},{25,97},{26,98},{27,99},{28,100},{29,101},{30,102},{31,103}} | collective-permute-start | bytes 786440 | tf_op jit(solution)/shard_map/ppermute | solution.py:256
  63.7 16.2 %collective-permute-start.23 = (bf16[2,2,512,128]{3,2,1,0:T(8,128)(2,1)S(1)}, bf16[2,2,512,128]{3,2,1,0:T(8,128)(2,1)S(1)}, u32[]{:S(2)}, u32[]{:S(2)}) collective-permute-start(bf16[2,2,512,128]{3,2,1,0:T(8,128)(2,1)S(1)} %pad_maximum_fusion.2), channel_id=1, source_target_pairs={{0,24},{8,0},{16,8},{24,16},{32,56},{40,32},{48,40},{56,48},{64,88... | collective-permute-start | bytes 1572872 | tf_op jit(solution)/shard_map/ppermute | solution.py:247
  64.5 24.7 %collective-permute-start.22 = (bf16[3,2,512,128]{3,2,1,0:T(8,128)(2,1)S(1)}, bf16[3,2,512,128]{3,2,1,0:T(8,128)(2,1)S(1)}, u32[]{:S(2)}, u32[]{:S(2)}) collective-permute-start(bf16[3,2,512,128]{3,2,1,0:T(8,128)(2,1)S(1)} %pad_maximum_fusion.1.refs_0_), channel_id=1, source_target_pairs={{0,8},{8,16},{16,24},{24,0},{32,40},{40,48},{48,56},{56,32},{64,72... | collective-permute-start | bytes 2359304 | tf_op jit(solution)/shard_map/ppermute | solution.py:247
  89.3 8.1 %collective-permute-start.25 = (bf16[2,512,128]{2,1,0:T(8,128)(2,1)S(1)}, bf16[2,512,128]{2,1,0:T(8,128)(2,1)S(1)}, u32[]{:S(2)}, u32[]{:S(2)}) collective-permute-start(bf16[2,512,128]{2,1,0:T(8,128)(2,1)S(1)} %slice_bitcast_fusion), channel_id=1, source_target_pairs={{0,24},{8,0},{16,8},{24,16},{32,56},{40,32},{48,40},{56,48},{64,88... | collective-permute-start | bytes 786440 | tf_op jit(solution)/shard_map/ppermute | solution.py:247
  92.4 7.2 %collective-permute-start.24 = (bf16[2,512,128]{2,1,0:T(8,128)(2,1)S(1)}, bf16[2,512,128]{2,1,0:T(8,128)(2,1)S(1)}, u32[]{:S(2)}, u32[]{:S(2)}) collective-permute-start(bf16[2,512,128]{2,1,0:T(8,128)(2,1)S(1)} %select_bitcast_fusion), channel_id=1, source_target_pairs={{0,8},{8,16},{16,24},{24,0},{32,40},{40,48},{48,56},{56,32},{64,72... | collective-permute-start | bytes 786440 | tf_op jit(solution)/shard_map/ppermute | solution.py:247
  119.7 3.2 %collective-permute-start.27 = (bf16[512,512]{1,0:T(8,128)(2,1)S(1)}, bf16[512,512]{1,0:T(8,128)(2,1)S(1)}, u32[]{:S(2)}, u32[]{:S(2)}) collective-permute-start(bf16[512,512]{1,0:T(8,128)(2,1)S(1)} %pad_maximum_fusion.3), channel_id=1, source_target_pairs={{0,1},{1,0},{2,3},{3,2},{4,5},{5,4},{6,7},{7,6},{8,9},{9,8},{10,11... | collective-permute-start | bytes 1572872 | tf_op jit(solution)/shard_map/ppermute | solution.py:331
  119.8 15.4 %collective-permute-start.17 = (bf16[128,2048]{1,0:T(8,128)(2,1)S(1)}, bf16[128,2048]{1,0:T(8,128)(2,1)S(1)}, u32[]{:S(2)}, u32[]{:S(2)}) collective-permute-start(bf16[128,2048]{1,0:T(8,128)(2,1)S(1)} %get-tuple-element.65), channel_id=1, source_target_pairs={{0,6},{2,0},{4,2},{6,4},{1,7},{3,1},{5,3},{7,5},{8,14},{10,8},{12,... | collective-permute-start | bytes 1572872 | tf_op jit(solution)/shard_map/ppermute | solution.py:311
  122.9 16.0 %collective-permute-start.16 = (bf16[128,2048]{1,0:T(8,128)(2,1)S(1)}, bf16[128,2048]{1,0:T(8,128)(2,1)S(1)}, u32[]{:S(2)}, u32[]{:S(2)}) collective-permute-start(bf16[128,2048]{1,0:T(8,128)(2,1)S(1)} %get-tuple-element.66), channel_id=1, source_target_pairs={{0,2},{2,4},{4,6},{6,0},{1,3},{3,5},{5,7},{7,1},{8,10},{10,12},{12... | collective-permute-start | bytes 1572872 | tf_op jit(solution)/shard_map/ppermute | solution.py:311
  127.8 18.7 %collective-permute-start.29 = (bf16[128,2048]{1,0:T(8,128)(2,1)S(1)}, bf16[128,2048]{1,0:T(8,128)(2,1)S(1)}, u32[]{:S(2)}, u32[]{:S(2)}) collective-permute-start(bf16[128,2048]{1,0:T(8,128)(2,1)S(1)} %get-tuple-element.63), channel_id=1, source_target_pairs={{0,6},{2,0},{4,2},{6,4},{1,7},{3,1},{5,3},{7,5},{8,14},{10,8},{12,... | collective-permute-start | bytes 1572872 | tf_op jit(solution)/shard_map/ppermute | solution.py:311
  131.1 19.1 %collective-permute-start.28 = (bf16[128,2048]{1,0:T(8,128)(2,1)S(1)}, bf16[128,2048]{1,0:T(8,128)(2,1)S(1)}, u32[]{:S(2)}, u32[]{:S(2)}) collective-permute-start(bf16[128,2048]{1,0:T(8,128)(2,1)S(1)} %get-tuple-element.64), channel_id=1, source_target_pairs={{0,2},{2,4},{4,6},{6,0},{1,3},{3,5},{5,7},{7,1},{8,10},{10,12},{12... | collective-permute-start | bytes 1572872 | tf_op jit(solution)/shard_map/ppermute | solution.py:311
  139.0 22.4 %collective-permute-start.18 = (bf16[128,2048]{1,0:T(8,128)(2,1)S(1)}, bf16[128,2048]{1,0:T(8,128)(2,1)S(1)}, u32[]{:S(2)}, u32[]{:S(2)}) collective-permute-start(bf16[128,2048]{1,0:T(8,128)(2,1)S(1)} %get-tuple-element.47), channel_id=1, source_target_pairs={{0,2},{2,4},{4,6},{6,0},{1,3},{3,5},{5,7},{7,1},{8,10},{10,12},{12... | collective-permute-start | bytes 1572872 | tf_op jit(solution)/shard_map/ppermute | solution.py:311
  139.1 22.3 %collective-permute-start.19 = (bf16[128,2048]{1,0:T(8,128)(2,1)S(1)}, bf16[128,2048]{1,0:T(8,128)(2,1)S(1)}, u32[]{:S(2)}, u32[]{:S(2)}) collective-permute-start(bf16[128,2048]{1,0:T(8,128)(2,1)S(1)} %get-tuple-element.48), channel_id=1, source_target_pairs={{0,6},{2,0},{4,2},{6,4},{1,7},{3,1},{5,3},{7,5},{8,14},{10,8},{12,... | collective-permute-start | bytes 1572872 | tf_op jit(solution)/shard_map/ppermute | solution.py:311
  150.2 22.3 %collective-permute-start.30 = (bf16[128,2048]{1,0:T(8,128)(2,1)S(1)}, bf16[128,2048]{1,0:T(8,128)(2,1)S(1)}, u32[]{:S(2)}, u32[]{:S(2)}) collective-permute-start(bf16[128,2048]{1,0:T(8,128)(2,1)S(1)} %get-tuple-element.57), channel_id=1, source_target_pairs={{0,2},{2,4},{4,6},{6,0},{1,3},{3,5},{5,7},{7,1},{8,10},{10,12},{12... | collective-permute-start | bytes 1572872 | tf_op jit(solution)/shard_map/ppermute | solution.py:311
  150.3 22.3 %collective-permute-start.31 = (bf16[128,2048]{1,0:T(8,128)(2,1)S(1)}, bf16[128,2048]{1,0:T(8,128)(2,1)S(1)}, u32[]{:S(2)}, u32[]{:S(2)}) collective-permute-start(bf16[128,2048]{1,0:T(8,128)(2,1)S(1)} %get-tuple-element.58), channel_id=1, source_target_pairs={{0,6},{2,0},{4,2},{6,4},{1,7},{3,1},{5,3},{7,5},{8,14},{10,8},{12,... | collective-permute-start | bytes 1572872 | tf_op jit(solution)/shard_map/ppermute | solution.py:311
  161.5 22.3 %collective-permute-start.20 = (bf16[128,2048]{1,0:T(8,128)(2,1)S(1)}, bf16[128,2048]{1,0:T(8,128)(2,1)S(1)}, u32[]{:S(2)}, u32[]{:S(2)}) collective-permute-start(bf16[128,2048]{1,0:T(8,128)(2,1)S(1)} %get-tuple-element.49), channel_id=1, source_target_pairs={{0,2},{2,4},{4,6},{6,0},{1,3},{3,5},{5,7},{7,1},{8,10},{10,12},{12... | collective-permute-start | bytes 1572872 | tf_op jit(solution)/shard_map/ppermute | solution.py:311
  161.6 22.2 %collective-permute-start.21 = (bf16[128,2048]{1,0:T(8,128)(2,1)S(1)}, bf16[128,2048]{1,0:T(8,128)(2,1)S(1)}, u32[]{:S(2)}, u32[]{:S(2)}) collective-permute-start(bf16[128,2048]{1,0:T(8,128)(2,1)S(1)} %get-tuple-element.50), channel_id=1, source_target_pairs={{0,6},{2,0},{4,2},{6,4},{1,7},{3,1},{5,3},{7,5},{8,14},{10,8},{12,... | collective-permute-start | bytes 1572872 | tf_op jit(solution)/shard_map/ppermute | solution.py:311
  172.7 21.5 %collective-permute-start.32 = (bf16[128,2048]{1,0:T(8,128)(2,1)S(1)}, bf16[128,2048]{1,0:T(8,128)(2,1)S(1)}, u32[]{:S(2)}, u32[]{:S(2)}) collective-permute-start(bf16[128,2048]{1,0:T(8,128)(2,1)S(1)} %get-tuple-element.59), channel_id=1, source_target_pairs={{0,2},{2,4},{4,6},{6,0},{1,3},{3,5},{5,7},{7,1},{8,10},{10,12},{12... | collective-permute-start | bytes 1572872 | tf_op jit(solution)/shard_map/ppermute | solution.py:311
  172.8 21.4 %collective-permute-start.33 = (bf16[128,2048]{1,0:T(8,128)(2,1)S(1)}, bf16[128,2048]{1,0:T(8,128)(2,1)S(1)}, u32[]{:S(2)}, u32[]{:S(2)}) collective-permute-start(bf16[128,2048]{1,0:T(8,128)(2,1)S(1)} %get-tuple-element.60), channel_id=1, source_target_pairs={{0,6},{2,0},{4,2},{6,4},{1,7},{3,1},{5,3},{7,5},{8,14},{10,8},{12,... | collective-permute-start | bytes 1572872 | tf_op jit(solution)/shard_map/ppermute | solution.py:311
  (6 other events, 57.7 us)
where the time goes:
time: 198 us
  waiting for transfers between devices  91 us (46%)
  starting transfers between devices  51 us (26%)
  Pallas kernels  34.7 us (18%)
  matrix products  13 us (7%)
  local copies, waits for them, and re-layouts  7.2 us (4%)
    ppermute x12, waiting for transfers between devices, around(): return lax.ppermute(v, 'head', [(i, (i + step) % n) for i in range(n)])  49.2 us
    pallas_call x3, Pallas kernels, attention(): pl.pallas_call(functools.partial(attn_kernel, spec, n, span), name='atten...  33.8 us
    ppermute x11, waiting for transfers between devices, along_z(): return lax.ppermute(v, 'seq', pairs)  26.1 us
    ppermute x12, starting transfers between devices, around(): return lax.ppermute(v, 'head', [(i, (i + step) % n) for i in range(n)])  19.6 us
    ppermute x11, starting transfers between devices, along_z(): return lax.ppermute(v, 'seq', pairs)  17.3 us
    ppermute x4, waiting for transfers between devices, along_x(): return lax.ppermute(v, 'seq', pairs)  13.3 us
    dot_general x2, matrix products, project(): jnp.dot(both, out_weight, preferred_element_type=jnp.float32)  13 us
    ppermute x4, starting transfers between devices, along_x(): return lax.ppermute(v, 'seq', pairs)  12.4 us
  transfers between devices with their start and end apart: 34, of which 20 were waited for; matrix products, arithmetic and copies ran while one was open for 7% of the time, Pallas kernels for 0%

commit v1 on v0

--- a/solution.py
+++ b/solution.py
@@ -18,6 +18,7 @@
 BPD = TOK // BLK
 REACH = 9
 SLOTS = REACH + 1
+STREAMS = 2
 SCALE = math.log2(math.e) / math.sqrt(HD)
 NEG = -1e30
 
@@ -247,8 +248,8 @@
     return lax.ppermute(v, "seq", pairs)
 
 
-def along_x(v, first_row):
-    pairs = [(ZN * x + z, ZN * (x + 1) + z) for x in range(first_row, XN - 1) for z in range(ZN)]
+def along_x(v, step):
+    pairs = [(ZN * x + z, ZN * (x + step) + z) for x in range(XN - step) for z in range(ZN)]
     return lax.ppermute(v, "seq", pairs)
 
 
@@ -257,10 +258,10 @@
 
 
 def gather_apart(own, z):
-    x1 = along_x(own, 0)
+    x1 = along_x(own, 1)
+    x2 = along_x(own, 2)
     below_own = along_z(own, 1)
     corner = from_corner(own)
-    x2 = along_x(x1, 1)
     below_x1 = along_z(x1, 1)
     above_x1 = along_z(x1, -1)
     below_x2 = along_z(x2, 1)
@@ -282,19 +283,21 @@
     ]
 
 
-def add_kernel(turn, ra_ref, rb_ref, p_ref, na_ref, nb_ref):
-    rows, half = ra_ref.shape
+def add_kernel(turn, first_col, ra_ref, rb_ref, p_ref, na_ref, nb_ref):
+    rows, width = ra_ref.shape
     n = lax.axis_size("head")
     me = lax.axis_index("head")
+    half = p_ref.shape[1] // 2
     ka = pl.multiple_of((me + 2 * n - 2 - turn) % n * rows, rows)
     kb = pl.multiple_of((me + 2 + turn) % n * rows, rows)
-    na_ref[...] = ra_ref[...] + p_ref[pl.ds(ka, rows), :half]
-    nb_ref[...] = rb_ref[...] + p_ref[pl.ds(kb, rows), half:]
-
-
-def ring_add(turn, ra, rb, partial):
+    c = first_col
+    na_ref[...] = ra_ref[...] + p_ref[pl.ds(ka, rows), c : c + width]
+    nb_ref[...] = rb_ref[...] + p_ref[pl.ds(kb, rows), half + c : half + c + width]
+
+
+def ring_add(turn, first_col, ra, rb, partial):
     return pl.pallas_call(
-        functools.partial(add_kernel, turn),
+        functools.partial(add_kernel, turn, first_col),
         name="ring_add",
         out_shape=[jax.ShapeDtypeStruct(ra.shape, ra.dtype)] * 2,
         in_specs=[pl.BlockSpec(memory_space=pltpu.VMEM)] * 3,
@@ -311,20 +314,49 @@
     return lax.ppermute(v, "head", [(i, (i + step) % n) for i in range(n)])
 
 
-def first_blocks(partial):
+def first_kernel(own_ref, other_ref, w_ref, a_ref, b_ref):
+    n = lax.axis_size("head")
     me = lax.axis_index("head")
-    n = lax.axis_size("head")
-    rows = partial.shape[0] // n
-    half = partial.shape[1] // 2
-    a = lax.dynamic_slice(partial, ((me + n - 1) % n * rows, 0), (rows, half))
-    b = lax.dynamic_slice(partial, ((me + 1) % n * rows, half), (rows, half))
-    return a, b
-
-
-def ring_step(turn, a, b, partial):
+    core = lax.axis_index("batch")
+    depth = own_ref.shape[1]
+    rows, half = a_ref.shape
+    mine = pl.ds(pl.multiple_of(core * depth, depth), depth)
+    theirs = pl.ds(pl.multiple_of((1 - core) * depth, depth), depth)
+    tile = 512
+    for out_ref, block, base in ((a_ref, (me + n - 1) % n, 0), (b_ref, (me + 1) % n, half)):
+        at = pl.ds(pl.multiple_of(block * rows, rows), rows)
+        own, other = own_ref[at], other_ref[at]
+
+        @pl.loop(0, half // tile)
+        def _(i):
+            start = pl.multiple_of(i * tile, tile)
+            cols = pl.ds(pl.multiple_of(base + i * tile, tile), tile)
+            out_ref[:, pl.ds(start, tile)] = (
+                jnp.dot(own, w_ref[mine, cols], preferred_element_type=jnp.float32)
+                + jnp.dot(other, w_ref[theirs, cols], preferred_element_type=jnp.float32)
+            ).astype(out_ref.dtype)
+
+
+def first_blocks(own, other, weight):
+    rows = own.shape[0] // lax.axis_size("head")
+    half = weight.shape[1] // 2
+    return pl.pallas_call(
+        first_kernel,
+        name="first_blocks",
+        out_shape=[jax.ShapeDtypeStruct((rows, half), jnp.bfloat16)] * 2,
+        in_specs=[pl.BlockSpec(memory_space=pltpu.VMEM)] * 3,
+        out_specs=[pl.BlockSpec(memory_space=pltpu.VMEM)] * 2,
+        compiler_params=pltpu.CompilerParams(vmem_limit_bytes=24 << 20),
+        cost_estimate=pl.CostEstimate(
+            flops=4 * rows * half * weight.shape[0], bytes_accessed=12 << 20, transcendentals=0
+        ),
+    )(own, other, weight)
+
+
+def ring_step(turn, a, b, partial, first_col=0):
     a = around(a, 1)
     b = around(b, -1)
-    return ring_add(turn, a, b, partial)
+    return ring_add(turn, first_col, a, b, partial)
 
 
 def swapped(v):
@@ -348,8 +380,7 @@
     def of(sequence, mine, theirs):
         return jnp.where(core == sequence, mine, theirs)
 
-    def project(attended):
-        other = swapped(attended)
+    def project(attended, other):
         both = jnp.where(
             first,
             jnp.concatenate([attended, other], axis=1),
@@ -361,20 +392,22 @@
     z = lax.axis_index("seq") % ZN
     units0 = gather_apart(of(0, kv_mine, kv_theirs), z)
 
-    own1, units0[2] = tie((of(1, kv_mine, kv_theirs), units0[2]))
-    y1 = along_x(own1, 0)
-    y2 = along_x(y1, 1)
+    own1 = of(1, kv_mine, kv_theirs)
+    y1 = along_x(own1, 1)
+    y2 = along_x(own1, 2)
+    corner1 = from_corner(own1)
+    units0, (own1, y1, y2) = tie((units0, (own1, y1, y2)))
     stack1 = jnp.stack([own1, y1, y2])
     up1 = jnp.stack([jnp.where(z == 0, own1, y2), y1])
-    units0, stack1, up1 = tie((units0, stack1, up1))
     below1 = along_z(stack1, 1)
     above1 = along_z(up1, -1)
-    corner1 = from_corner(own1)
     attended0 = attention(
         of(0, block_doc, doc_theirs), of(0, q_mine, q_theirs), units0, APART, (0, BPD)
     )
-    partial0 = project(attended0)
-    a0, b0 = first_blocks(partial0)
+    other0 = swapped(attended0)
+    a0, b0 = first_blocks(attended0, other0, out_weight)
+    _, (attended0, other0) = tie(((a0, b0), (attended0, other0)))
+    partial0 = project(attended0, other0)
 
     (below1, above1), _ = tie(((below1, above1), (a0, b0)))
     far_mixed1 = along_z(jnp.where((z == 1) | (z == 2), below1[0], below1[2]), 1)
@@ -386,13 +419,23 @@
     a0, b0 = ring_step(1, a0, b0, partial0)
     lower = attention(doc1, q1, units1, STACKED, (BPD // 2, BPD))
     a0, b0 = ring_step(2, a0, b0, partial0)
-    partial1 = project(jnp.concatenate([upper, lower], axis=0))
-    a1, b1 = first_blocks(partial1)
-    for turn in range(3):
-        a1, b1 = ring_step(turn, a1, b1, partial1)
+    attended1 = jnp.concatenate([upper, lower], axis=0)
+    other1 = swapped(attended1)
+    a1, b1 = first_blocks(attended1, other1, out_weight)
+    _, (attended1, other1) = tie(((a1, b1), (attended1, other1)))
+    partial1 = project(attended1, other1)
+    width = a1.shape[1] // STREAMS
+    tails = []
+    for i in range(STREAMS):
+        cols = slice(i * width, (i + 1) * width)
+        a, b = a1[:, cols], b1[:, cols]
+        for turn in range(3):
+            a, b = ring_step(turn, a, b, partial1, i * width)
+        tails.append((a, b))
     sum0 = jnp.concatenate([a0, b0], axis=1)
-    sum1 = jnp.concatenate([a1, b1], axis=1)
-    return jnp.stack([sum0, sum1], axis=1)
+    sum1 = jnp.concatenate([t[0] for t in tails] + [t[1] for t in tails], axis=1)
+    spot = lax.broadcasted_iota(jnp.int32, (1, 2, 1), 1)
+    return jnp.where(spot == 0, sum0[:, None], sum1[:, None])
 
 
 def solution(mesh):

time: 198 us -> 185 us (0.934)
  the two profiles are of different devices: /device:TPU:36 before, /device:TPU:4 now
where the time goes in v1:
time: 185 us
  waiting for transfers between devices  70.3 us (38%)
  starting transfers between devices  60.1 us (32%)
  Pallas kernels  36.5 us (20%)
  matrix products  9.53 us (5%)
  other arithmetic  4.62 us (2%)
  local copies, waits for them, and re-layouts  3.48 us (2%)
    ppermute x18, waiting for transfers between devices, around(): return lax.ppermute(v, 'head', [(i, (i + step) % n) for i in range(n)])  34.5 us
    pallas_call x3, Pallas kernels, attention(): pl.pallas_call(functools.partial(attn_kernel, spec, n, span), name='atten...  30.6 us
    ppermute x11, starting transfers between devices, along_z(): return lax.ppermute(v, 'seq', pairs)  26.6 us
    ppermute x11, waiting for transfers between devices, along_z(): return lax.ppermute(v, 'seq', pairs)  23.9 us
    ppermute x18, starting transfers between devices, around(): return lax.ppermute(v, 'head', [(i, (i + step) % n) for i in range(n)])  23.4 us
    ppermute x4, waiting for transfers between devices, along_x(): return lax.ppermute(v, 'seq', pairs)  10.4 us
    dot_general x2, matrix products, project(): jnp.dot(both, out_weight, preferred_element_type=jnp.float32)  9.53 us
    ppermute x4, starting transfers between devices, along_x(): return lax.ppermute(v, 'seq', pairs)  8.11 us
  transfers between devices with their start and end apart: 40, of which 19 were waited for; matrix products, arithmetic and copies ran while one was open for 6% of the time, Pallas kernels for 20%

profile of v1, /device:TPU:4, one launch (start us, length us, event | category | flops | bytes accessed | tf_op | source)
XLA Modules:
  0.0 185.0 jit_solution(3073866560418988399)
XLA Ops:
  6.7 2.0 %collective-permute-start.5 = (bf16[2,512,128]{2,1,0:T(8,128)(2,1)S(1)}, bf16[2,512,128]{2,1,0:T(8,128)(2,1)S(1)}, u32[]{:S(2)}, u32[]{:S(2)}) collective-permute-start(bf16[2,512,128]{2,1,0:T(8,128)(2,1)S(1)} %get-tuple-element.47.refs_0_), channel_id=1, source_target_pairs={{0,8},{8,16},{16,24},{24,0},{32,40},{40,48},{48,56},{56,32},{64,72... | collective-permute-start | bytes 786440 | tf_op jit(solution)/shard_map/ppermute | solution.py:248
  8.7 3.1 %collective-permute-start.3 = (bf16[2,512,128]{2,1,0:T(8,128)(2,1)S(1)}, bf16[2,512,128]{2,1,0:T(8,128)(2,1)S(1)}, u32[]{:S(2)}, u32[]{:S(2)}) collective-permute-start(bf16[2,512,128]{2,1,0:T(8,128)(2,1)S(1)} %get-tuple-element.47.refs_0_), channel_id=1, source_target_pairs={{0,32},{8,40},{16,48},{24,56},{32,64},{40,72},{48,80},{56,88},{64,... | collective-permute-start | bytes 786440 | tf_op jit(solution)/shard_map/ppermute | solution.py:253
  12.0 5.3 %collective-permute-done.4.refs_2_ = bf16[2,512,128]{2,1,0:T(8,128)(2,1)S(1)} collective-permute-done((bf16[2,512,128]{2,1,0:T(8,128)(2,1)S(1)}, bf16[2,512,128]{2,1,0:T(8,128)(2,1)S(1)}, u32[]{:S(2)}, u32[]{:S(2)}) %collective-permute-start.4) | collective-permute-done | bytes 262176 | tf_op jit(solution)/shard_map/ppermute | solution.py:253
  17.3 1.9 %collective-permute-start.7 = (bf16[2,512,128]{2,1,0:T(8,128)(2,1)S(1)}, bf16[2,512,128]{2,1,0:T(8,128)(2,1)S(1)}, u32[]{:S(2)}, u32[]{:S(2)}) collective-permute-start(bf16[2,512,128]{2,1,0:T(8,128)(2,1)S(1)} %collective-permute-done.4.refs_2_), channel_id=1, source_target_pairs={{0,8},{8,16},{16,24},{24,0},{32,40},{40,48},{48,56},{56,32},{64,72... | collective-permute-start | bytes 786440 | tf_op jit(solution)/shard_map/ppermute | solution.py:248
  20.5 2.4 %collective-permute-start.13 = (bf16[2,512,128]{2,1,0:T(8,128)(2,1)S(1)}, bf16[2,512,128]{2,1,0:T(8,128)(2,1)S(1)}, u32[]{:S(2)}, u32[]{:S(2)}) collective-permute-start(bf16[2,512,128]{2,1,0:T(8,128)(2,1)S(1)} %get-tuple-element.68), channel_id=1, source_target_pairs={{0,32},{8,40},{16,48},{24,56},{32,64},{40,72},{48,80},{56,88},{64,... | collective-permute-start | bytes 786440 | tf_op jit(solution)/shard_map/ppermute | solution.py:253
  23.0 3.6 %collective-permute-start.9 = (bf16[2,512,128]{2,1,0:T(8,128)(2,1)S(1)}, bf16[2,512,128]{2,1,0:T(8,128)(2,1)S(1)}, u32[]{:S(2)}, u32[]{:S(2)}) collective-permute-start(bf16[2,512,128]{2,1,0:T(8,128)(2,1)S(1)} %collective-permute-done.3.refs_1_), channel_id=1, source_target_pairs={{0,24},{8,0},{16,8},{24,16},{32,56},{40,32},{48,40},{56,48},{64,88... | collective-permute-start | bytes 786440 | tf_op jit(solution)/shard_map/ppermute | solution.py:248
  27.3 4.5 %collective-permute-done.14 = bf16[2,512,128]{2,1,0:T(8,128)(2,1)S(1)} collective-permute-done((bf16[2,512,128]{2,1,0:T(8,128)(2,1)S(1)}, bf16[2,512,128]{2,1,0:T(8,128)(2,1)S(1)}, u32[]{:S(2)}, u32[]{:S(2)}) %collective-permute-start.14) | collective-permute-done | bytes 262176 | tf_op jit(solution)/shard_map/ppermute | solution.py:253
  31.8 2.4 %collective-permute-start.8 = (bf16[2,512,128]{2,1,0:T(8,128)(2,1)S(1)}, bf16[2,512,128]{2,1,0:T(8,128)(2,1)S(1)}, u32[]{:S(2)}, u32[]{:S(2)}) collective-permute-start(bf16[2,512,128]{2,1,0:T(8,128)(2,1)S(1)} %broadcast_select_fusion.7), channel_id=1, source_target_pairs={{0,24},{8,0},{16,8},{24,16},{32,56},{40,32},{48,40},{56,48},{64,88... | collective-permute-start | bytes 786440 | tf_op jit(solution)/shard_map/ppermute | solution.py:248
  34.8 1.9 %collective-permute-start.6 = (bf16[2,512,128]{2,1,0:T(8,128)(2,1)S(1)}, bf16[2,512,128]{2,1,0:T(8,128)(2,1)S(1)}, u32[]{:S(2)}, u32[]{:S(2)}) collective-permute-start(bf16[2,512,128]{2,1,0:T(8,128)(2,1)S(1)} %collective-permute-done.3.refs_1_), channel_id=1, source_target_pairs={{0,8},{8,16},{16,24},{24,0},{32,40},{40,48},{48,56},{56,32},{64,72... | collective-permute-start | bytes 786440 | tf_op jit(solution)/shard_map/ppermute | solution.py:248
  40.1 5.1 %collective-permute-done.6.refs_4_ = bf16[2,512,128]{2,1,0:T(8,128)(2,1)S(1)} collective-permute-done((bf16[2,512,128]{2,1,0:T(8,128)(2,1)S(1)}, bf16[2,512,128]{2,1,0:T(8,128)(2,1)S(1)}, u32[]{:S(2)}, u32[]{:S(2)}) %collective-permute-start.6) | collective-permute-done | bytes 262176 | tf_op jit(solution)/shard_map/ppermute | solution.py:248
  45.2 4.7 %collective-permute-done.10.refs_8_ = bf16[2,512,128]{2,1,0:T(8,128)(2,1)S(1)} collective-permute-done((bf16[2,512,128]{2,1,0:T(8,128)(2,1)S(1)}, bf16[2,512,128]{2,1,0:T(8,128)(2,1)S(1)}, u32[]{:S(2)}, u32[]{:S(2)}) %collective-permute-start.10) | collective-permute-done | bytes 262176 | tf_op jit(solution)/shard_map/ppermute | solution.py:248
  50.7 12.6 %attend.3.own_ref = bf16[512,512]{1,0:T(8,128)(2,1)S(1)} custom-call(s32[1,64]{1,0:T(1,128)S(1)} %get-tuple-element.101.doc_ref, bf16[512,512]{1,0:T(8,128)(2,1)S(1)} %get-tuple-element.89.q_ref, bf16[2,512,128]{2,1,0:T(8,128)(2,1)S(1)} %get-tuple-element.47.refs_0_, bf16[2,512,128]{2,1,0:T(8,128)(2,1)S(1)} %collective-permute-done.3.refs_1_, ...), custom_call_target="tpu_custom_call" | custom-call | flops 6000000000 | bytes 4000000 | tf_op jit(solution)/shard_map/attend/pallas_call | solution.py:213
  63.5 7.1 %collective-permute-start.23 = (bf16[2,2,512,128]{3,2,1,0:T(8,128)(2,1)S(1)}, bf16[2,2,512,128]{3,2,1,0:T(8,128)(2,1)S(1)}, u32[]{:S(2)}, u32[]{:S(2)}) collective-permute-start(bf16[2,2,512,128]{3,2,1,0:T(8,128)(2,1)S(1)} %pad_maximum_fusion.3), channel_id=1, source_target_pairs={{0,24},{8,0},{16,8},{24,16},{32,56},{40,32},{48,40},{56,48},{64,88... | collective-permute-start | bytes 1572872 | tf_op jit(solution)/shard_map/ppermute | solution.py:248
  71.3 2.6 %first_blocks.2 = (bf16[128,2048]{1,0:T(8,128)(2,1)S(1)}, bf16[128,2048]{1,0:T(8,128)(2,1)S(1)}) custom-call(bf16[512,512]{1,0:T(8,128)(2,1)S(1)} %attend.3.own_ref, bf16[512,512]{1,0:T(8,128)(2,1)S(1)} %collective-permute-done.15.other_ref, bf16[1024,4096]{1,0:T(8,128)(2,1)S(1)} %bitcast.25), custom_call_target="tpu_custom_call" | custom-call | flops 1073741824 | bytes 12582912 | tf_op jit(solution)/shard_map/first_blocks/pallas_call | solution.py:343
  73.9 8.5 %collective-permute-done.23.refs_2_ = bf16[2,2,512,128]{3,2,1,0:T(8,128)(2,1)S(1)} collective-permute-done((bf16[2,2,512,128]{3,2,1,0:T(8,128)(2,1)S(1)}, bf16[2,2,512,128]{3,2,1,0:T(8,128)(2,1)S(1)}, u32[]{:S(2)}, u32[]{:S(2)}) %collective-permute-start.23) | collective-permute-done | bytes 524320 | tf_op jit(solution)/shard_map/ppermute | solution.py:248
  82.5 3.8 %collective-permute-start.25 = (bf16[2,512,128]{2,1,0:T(8,128)(2,1)S(1)}, bf16[2,512,128]{2,1,0:T(8,128)(2,1)S(1)}, u32[]{:S(2)}, u32[]{:S(2)}) collective-permute-start(bf16[2,512,128]{2,1,0:T(8,128)(2,1)S(1)} %slice_bitcast_fusion), channel_id=1, source_target_pairs={{0,24},{8,0},{16,8},{24,16},{32,56},{40,32},{48,40},{56,48},{64,88... | collective-permute-start | bytes 786440 | tf_op jit(solution)/shard_map/ppermute | solution.py:248
  89.5 2.1 %collective-permute-done.25.refs_4_ = bf16[2,512,128]{2,1,0:T(8,128)(2,1)S(1)} collective-permute-done((bf16[2,512,128]{2,1,0:T(8,128)(2,1)S(1)}, bf16[2,512,128]{2,1,0:T(8,128)(2,1)S(1)}, u32[]{:S(2)}, u32[]{:S(2)}) %collective-permute-start.25) | collective-permute-done | bytes 262176 | tf_op jit(solution)/shard_map/ppermute | solution.py:248
  91.6 3.4 %collective-permute-done.24.refs_3_ = bf16[2,512,128]{2,1,0:T(8,128)(2,1)S(1)} collective-permute-done((bf16[2,512,128]{2,1,0:T(8,128)(2,1)S(1)}, bf16[2,512,128]{2,1,0:T(8,128)(2,1)S(1)}, u32[]{:S(2)}, u32[]{:S(2)}) %collective-permute-start.24) | collective-permute-done | bytes 262176 | tf_op jit(solution)/shard_map/ppermute | solution.py:248
  95.0 9.0 %attend.5 = bf16[256,512]{1,0:T(8,128)(2,1)S(1)} custom-call(s32[1,64]{1,0:T(1,128)S(1)} %get-tuple-element.102.doc_ref, bf16[512,512]{1,0:T(8,128)(2,1)S(1)} %get-tuple-element.90.q_ref, bf16[3,2,512,128]{3,2,1,0:T(8,128)(2,1)S(1)} %pad_maximum_fusion.2.refs_0_, bf16[3,2,512,128]{3,2,1,0:T(8,128)(2,1)S(1)} %collective-permute-done.22.refs_1_, ...), custom_call_target="tpu_custom_call" | custom-call | flops 3000000000 | bytes 4000000 | tf_op jit(solution)/shard_map/attend/pallas_call | solution.py:213
  104.0 9.0 %attend.4 = bf16[256,512]{1,0:T(8,128)(2,1)S(1)} custom-call(s32[1,64]{1,0:T(1,128)S(1)} %get-tuple-element.102.doc_ref, bf16[512,512]{1,0:T(8,128)(2,1)S(1)} %get-tuple-element.90.q_ref, bf16[3,2,512,128]{3,2,1,0:T(8,128)(2,1)S(1)} %pad_maximum_fusion.2.refs_0_, bf16[3,2,512,128]{3,2,1,0:T(8,128)(2,1)S(1)} %collective-permute-done.22.refs_1_, ...), custom_call_target="tpu_custom_call" | custom-call | flops 3000000000 | bytes 4000000 | tf_op jit(solution)/shard_map/attend/pallas_call | solution.py:213
  113.2 4.8 %convolution_convert_fusion.1.p_ref = bf16[512,4096]{1,0:T(8,128)(2,1)S(1)} fusion(bf16[1024,4096]{1,0:T(8,128)(2,1)S(1)} %bitcast.25, bf16[512,512]{1,0:T(8,128)(2,1)S(1)} %collective-permute-done.15.other_ref, bf16[512,512]{1,0:T(8,128)(2,1)S(1)} %attend.3.own_ref, pred[]{:T(512)S(6)} %eq.34), kind=kOutput, calls=%fused_computation.1 | convolution fusion | flops 4301783040 | bytes 13631489 | tf_op jit(solution)/shard_map/dot_general | solution.py:389
  121.4 2.6 %first_blocks.3 = (bf16[128,2048]{1,0:T(8,128)(2,1)S(1)}, bf16[128,2048]{1,0:T(8,128)(2,1)S(1)}) custom-call(bf16[512,512]{1,0:T(8,128)(2,1)S(1)} %pad_maximum_fusion.4.own_ref, bf16[512,512]{1,0:T(8,128)(2,1)S(1)} %collective-permute-done.27.other_ref, bf16[1024,4096]{1,0:T(8,128)(2,1)S(1)} %bitcast.25), custom_call_target="tpu_custom_call" | custom-call | flops 1073741824 | bytes 12582912 | tf_op jit(solution)/shard_map/first_blocks/pallas_call | solution.py:343
  127.8 4.8 %convolution_convert_fusion.p_ref = bf16[512,4096]{1,0:T(8,128)(2,1)S(1)} fusion(bf16[1024,4096]{1,0:T(8,128)(2,1)S(1)} %bitcast.25, bf16[512,512]{1,0:T(8,128)(2,1)S(1)} %collective-permute-done.27.other_ref, bf16[512,512]{1,0:T(8,128)(2,1)S(1)} %pad_maximum_fusion.4.own_ref, pred[]{:T(512)S(6)} %eq.34), kind=kOutput, calls=%fused_computation | convolution fusion | flops 4301783040 | bytes 13631489 | tf_op jit(solution)/shard_map/dot_general | solution.py:389
  132.6 7.3 %collective-permute-done.28.ra_ref = bf16[128,1024]{1,0:T(8,128)(2,1)S(1)} collective-permute-done((bf16[128,1024]{1,0:T(8,128)(2,1)S(1)}, bf16[128,1024]{1,0:T(8,128)(2,1)S(1)}, u32[]{:S(2)}, u32[]{:S(2)}) %collective-permute-start.28) | collective-permute-done | bytes 262176 | tf_op jit(solution)/shard_map/ppermute | solution.py:314
  142.6 2.8 %collective-permute-start.21 = (bf16[128,2048]{1,0:T(8,128)(2,1)S(1)}, bf16[128,2048]{1,0:T(8,128)(2,1)S(1)}, u32[]{:S(2)}, u32[]{:S(2)}) collective-permute-start(bf16[128,2048]{1,0:T(8,128)(2,1)S(1)} %get-tuple-element.65), channel_id=1, source_target_pairs={{0,6},{2,0},{4,2},{6,4},{1,7},{3,1},{5,3},{7,5},{8,14},{10,8},{12,... | collective-permute-start | bytes 1572872 | tf_op jit(solution)/shard_map/ppermute | solution.py:314
  149.4 2.7 %collective-permute-done.30.ra_ref = bf16[128,1024]{1,0:T(8,128)(2,1)S(1)} collective-permute-done((bf16[128,1024]{1,0:T(8,128)(2,1)S(1)}, bf16[128,1024]{1,0:T(8,128)(2,1)S(1)}, u32[]{:S(2)}, u32[]{:S(2)}) %collective-permute-start.30) | collective-permute-done | bytes 262176 | tf_op jit(solution)/shard_map/ppermute | solution.py:314
  152.9 13.0 %collective-permute-done.31.rb_ref = bf16[128,1024]{1,0:T(8,128)(2,1)S(1)} collective-permute-done((bf16[128,1024]{1,0:T(8,128)(2,1)S(1)}, bf16[128,1024]{1,0:T(8,128)(2,1)S(1)}, u32[]{:S(2)}, u32[]{:S(2)}) %collective-permute-start.31) | collective-permute-done | bytes 262176 | tf_op jit(solution)/shard_map/ppermute | solution.py:314
  166.3 2.2 %collective-permute-done.36.ra_ref = bf16[128,1024]{1,0:T(8,128)(2,1)S(1)} collective-permute-done((bf16[128,1024]{1,0:T(8,128)(2,1)S(1)}, bf16[128,1024]{1,0:T(8,128)(2,1)S(1)}, u32[]{:S(2)}, u32[]{:S(2)}) %collective-permute-start.36) | collective-permute-done | bytes 262176 | tf_op jit(solution)/shard_map/ppermute | solution.py:314
  171.0 3.2 %collective-permute-start.39 = (bf16[128,1024]{1,0:T(8,128)(2,1)S(1)}, bf16[128,1024]{1,0:T(8,128)(2,1)S(1)}, u32[]{:S(2)}, u32[]{:S(2)}) collective-permute-start(bf16[128,1024]{1,0:T(8,128)(2,1)S(1)} %get-tuple-element.85), channel_id=1, source_target_pairs={{0,6},{2,0},{4,2},{6,4},{1,7},{3,1},{5,3},{7,5},{8,14},{10,8},{12,... | collective-permute-start | bytes 786440 | tf_op jit(solution)/shard_map/ppermute | solution.py:314
  174.6 3.1 %collective-permute-done.33.rb_ref = bf16[128,1024]{1,0:T(8,128)(2,1)S(1)} collective-permute-done((bf16[128,1024]{1,0:T(8,128)(2,1)S(1)}, bf16[128,1024]{1,0:T(8,128)(2,1)S(1)}, u32[]{:S(2)}, u32[]{:S(2)}) %collective-permute-start.33) | collective-permute-done | bytes 262176 | tf_op jit(solution)/shard_map/ppermute | solution.py:314
  179.2 1.8 collective-permute-done.39.rb_ref
  181.1 3.9 %broadcast_select_fusion = bf16[128,2,4096]{2,1,0:T(2,128)(2,1)} fusion(pred[2]{0:T(512)(128)(4,1)S(1)} %iota_compare_fusion, bf16[128,4096]{1,0:T(8,128)(2,1)S(1)} %pad_maximum_fusion.1, bf16[128,4096]{1,0:T(8,128)(2,1)S(1)} %pad_maximum_fusion), kind=kLoop, calls=%fused_computation.2 | loop fusion | flops 1048576 | bytes 4194306 | tf_op jit(solution)/shard_map/jit(_where)/select_n | solution.py:438
  (97 shorter events, 37.5 us)
Async XLA Ops:
  4.9 12.4 %collective-permute-start.4 = (bf16[2,512,128]{2,1,0:T(8,128)(2,1)S(1)}, bf16[2,512,128]{2,1,0:T(8,128)(2,1)S(1)}, u32[]{:S(2)}, u32[]{:S(2)}) collective-permute-start(bf16[2,512,128]{2,1,0:T(8,128)(2,1)S(1)} %get-tuple-element.47.refs_0_), channel_id=1, source_target_pairs={{0,64},{8,72},{16,80},{24,88},{32,96},{40,104},{48,112},{56,120},{... | collective-permute-start | bytes 786440 | tf_op jit(solution)/shard_map/ppermute | solution.py:253
  6.2 13.0 %collective-permute-start = (s32[1,64]{1,0:T(1,128)S(1)}, s32[1,64]{1,0:T(1,128)S(1)}, u32[]{:S(2)}, u32[]{:S(2)}) collective-permute-start(s32[1,64]{1,0:T(1,128)S(1)} %copy-done.1), channel_id=1, source_target_pairs={{0,1},{1,0},{2,3},{3,2},{4,5},{5,4},{6,7},{7,6},{8,9},{9,8},{10,11... | collective-permute-start | bytes 776 | tf_op jit(solution)/shard_map/ppermute | solution.py:363
  6.7 13.8 %collective-permute-start.5 = (bf16[2,512,128]{2,1,0:T(8,128)(2,1)S(1)}, bf16[2,512,128]{2,1,0:T(8,128)(2,1)S(1)}, u32[]{:S(2)}, u32[]{:S(2)}) collective-permute-start(bf16[2,512,128]{2,1,0:T(8,128)(2,1)S(1)} %get-tuple-element.47.refs_0_), channel_id=1, source_target_pairs={{0,8},{8,16},{16,24},{24,0},{32,40},{40,48},{48,56},{56,32},{64,72... | collective-permute-start | bytes 786440 | tf_op jit(solution)/shard_map/ppermute | solution.py:248
  8.7 14.3 %collective-permute-start.3 = (bf16[2,512,128]{2,1,0:T(8,128)(2,1)S(1)}, bf16[2,512,128]{2,1,0:T(8,128)(2,1)S(1)}, u32[]{:S(2)}, u32[]{:S(2)}) collective-permute-start(bf16[2,512,128]{2,1,0:T(8,128)(2,1)S(1)} %get-tuple-element.47.refs_0_), channel_id=1, source_target_pairs={{0,32},{8,40},{16,48},{24,56},{32,64},{40,72},{48,80},{56,88},{64,... | collective-permute-start | bytes 786440 | tf_op jit(solution)/shard_map/ppermute | solution.py:253
  11.8 24.9 %collective-permute-start.1 = (bf16[512,512]{1,0:T(8,128)(2,1)S(1)}, bf16[512,512]{1,0:T(8,128)(2,1)S(1)}, u32[]{:S(2)}, u32[]{:S(2)}) collective-permute-start(bf16[512,512]{1,0:T(8,128)(2,1)S(1)} %broadcast_select_fusion.3), channel_id=1, source_target_pairs={{0,1},{1,0},{2,3},{3,2},{4,5},{5,4},{6,7},{7,6},{8,9},{9,8},{10,11... | collective-permute-start | bytes 1572872 | tf_op jit(solution)/shard_map/ppermute | solution.py:363
  17.3 9.3 %collective-permute-start.7 = (bf16[2,512,128]{2,1,0:T(8,128)(2,1)S(1)}, bf16[2,512,128]{2,1,0:T(8,128)(2,1)S(1)}, u32[]{:S(2)}, u32[]{:S(2)}) collective-permute-start(bf16[2,512,128]{2,1,0:T(8,128)(2,1)S(1)} %collective-permute-done.4.refs_2_), channel_id=1, source_target_pairs={{0,8},{8,16},{16,24},{24,0},{32,40},{40,48},{48,56},{56,32},{64,72... | collective-permute-start | bytes 786440 | tf_op jit(solution)/shard_map/ppermute | solution.py:248
  19.2 12.6 %collective-permute-start.14 = (bf16[2,512,128]{2,1,0:T(8,128)(2,1)S(1)}, bf16[2,512,128]{2,1,0:T(8,128)(2,1)S(1)}, u32[]{:S(2)}, u32[]{:S(2)}) collective-permute-start(bf16[2,512,128]{2,1,0:T(8,128)(2,1)S(1)} %get-tuple-element.68), channel_id=1, source_target_pairs={{0,64},{8,72},{16,80},{24,88},{32,96},{40,104},{48,112},{56,120},{... | collective-permute-start | bytes 786440 | tf_op jit(solution)/shard_map/ppermute | solution.py:253
  20.5 14.3 %collective-permute-start.13 = (bf16[2,512,128]{2,1,0:T(8,128)(2,1)S(1)}, bf16[2,512,128]{2,1,0:T(8,128)(2,1)S(1)}, u32[]{:S(2)}, u32[]{:S(2)}) collective-permute-start(bf16[2,512,128]{2,1,0:T(8,128)(2,1)S(1)} %get-tuple-element.68), channel_id=1, source_target_pairs={{0,32},{8,40},{16,48},{24,56},{32,64},{40,72},{48,80},{56,88},{64,... | collective-permute-start | bytes 786440 | tf_op jit(solution)/shard_map/ppermute | solution.py:253
  23.0 15.4 %collective-permute-start.9 = (bf16[2,512,128]{2,1,0:T(8,128)(2,1)S(1)}, bf16[2,512,128]{2,1,0:T(8,128)(2,1)S(1)}, u32[]{:S(2)}, u32[]{:S(2)}) collective-permute-start(bf16[2,512,128]{2,1,0:T(8,128)(2,1)S(1)} %collective-permute-done.3.refs_1_), channel_id=1, source_target_pairs={{0,24},{8,0},{16,8},{24,16},{32,56},{40,32},{48,40},{56,48},{64,88... | collective-permute-start | bytes 786440 | tf_op jit(solution)/shard_map/ppermute | solution.py:248
  26.6 13.4 %collective-permute-start.12 = (bf16[2,512,128]{2,1,0:T(8,128)(2,1)S(1)}, bf16[2,512,128]{2,1,0:T(8,128)(2,1)S(1)}, u32[]{:S(2)}, u32[]{:S(2)}) collective-permute-start(bf16[2,512,128]{2,1,0:T(8,128)(2,1)S(1)} %get-tuple-element.47.refs_0_), channel_id=1, source_target_pairs={{24,96},{25,97},{26,98},{27,99},{28,100},{29,101},{30,102},{31,103}} | collective-permute-start | bytes 786440 | tf_op jit(solution)/shard_map/ppermute | solution.py:257
  34.8 10.4 %collective-permute-start.6 = (bf16[2,512,128]{2,1,0:T(8,128)(2,1)S(1)}, bf16[2,512,128]{2,1,0:T(8,128)(2,1)S(1)}, u32[]{:S(2)}, u32[]{:S(2)}) collective-permute-start(bf16[2,512,128]{2,1,0:T(8,128)(2,1)S(1)} %collective-permute-done.3.refs_1_), channel_id=1, source_target_pairs={{0,8},{8,16},{16,24},{24,0},{32,40},{40,48},{48,56},{56,32},{64,72... | collective-permute-start | bytes 786440 | tf_op jit(solution)/shard_map/ppermute | solution.py:248
  36.7 13.1 %collective-permute-start.10 = (bf16[2,512,128]{2,1,0:T(8,128)(2,1)S(1)}, bf16[2,512,128]{2,1,0:T(8,128)(2,1)S(1)}, u32[]{:S(2)}, u32[]{:S(2)}) collective-permute-start(bf16[2,512,128]{2,1,0:T(8,128)(2,1)S(1)} %broadcast_select_fusion.6), channel_id=1, source_target_pairs={{0,8},{8,16},{16,24},{24,0},{32,40},{40,48},{48,56},{56,32},{64,72... | collective-permute-start | bytes 786440 | tf_op jit(solution)/shard_map/ppermute | solution.py:248
  38.4 11.5 %collective-permute-start.11 = (bf16[2,512,128]{2,1,0:T(8,128)(2,1)S(1)}, bf16[2,512,128]{2,1,0:T(8,128)(2,1)S(1)}, u32[]{:S(2)}, u32[]{:S(2)}) collective-permute-start(bf16[2,512,128]{2,1,0:T(8,128)(2,1)S(1)} %collective-permute-done.9.refs_7_), channel_id=1, source_target_pairs={{0,24},{8,0},{16,8},{24,16},{32,56},{40,32},{48,40},{56,48},{64,88... | collective-permute-start | bytes 786440 | tf_op jit(solution)/shard_map/ppermute | solution.py:248
  49.9 32.5 %collective-permute-start.22 = (bf16[3,2,512,128]{3,2,1,0:T(8,128)(2,1)S(1)}, bf16[3,2,512,128]{3,2,1,0:T(8,128)(2,1)S(1)}, u32[]{:S(2)}, u32[]{:S(2)}) collective-permute-start(bf16[3,2,512,128]{3,2,1,0:T(8,128)(2,1)S(1)} %pad_maximum_fusion.2.refs_0_), channel_id=1, source_target_pairs={{0,8},{8,16},{16,24},{24,0},{32,40},{40,48},{48,56},{56,32},{64,72... | collective-permute-start | bytes 2359304 | tf_op jit(solution)/shard_map/ppermute | solution.py:248
  63.5 19.0 %collective-permute-start.23 = (bf16[2,2,512,128]{3,2,1,0:T(8,128)(2,1)S(1)}, bf16[2,2,512,128]{3,2,1,0:T(8,128)(2,1)S(1)}, u32[]{:S(2)}, u32[]{:S(2)}) collective-permute-start(bf16[2,2,512,128]{3,2,1,0:T(8,128)(2,1)S(1)} %pad_maximum_fusion.3), channel_id=1, source_target_pairs={{0,24},{8,0},{16,8},{24,16},{32,56},{40,32},{48,40},{56,48},{64,88... | collective-permute-start | bytes 1572872 | tf_op jit(solution)/shard_map/ppermute | solution.py:248
  70.6 18.9 %collective-permute-start.26 = (bf16[2,512,128]{2,1,0:T(8,128)(2,1)S(1)}, bf16[2,512,128]{2,1,0:T(8,128)(2,1)S(1)}, u32[]{:S(2)}, u32[]{:S(2)}) collective-permute-start(bf16[2,512,128]{2,1,0:T(8,128)(2,1)S(1)} %get-tuple-element.68), channel_id=1, source_target_pairs={{24,96},{25,97},{26,98},{27,99},{28,100},{29,101},{30,102},{31,103}} | collective-permute-start | bytes 786440 | tf_op jit(solution)/shard_map/ppermute | solution.py:257
  86.3 31.7 %collective-permute-start.16 = (bf16[128,2048]{1,0:T(8,128)(2,1)S(1)}, bf16[128,2048]{1,0:T(8,128)(2,1)S(1)}, u32[]{:S(2)}, u32[]{:S(2)}) collective-permute-start(bf16[128,2048]{1,0:T(8,128)(2,1)S(1)} %get-tuple-element.58), channel_id=1, source_target_pairs={{0,2},{2,4},{4,6},{6,0},{1,3},{3,5},{5,7},{7,1},{8,10},{10,12},{12... | collective-permute-start | bytes 1572872 | tf_op jit(solution)/shard_map/ppermute | solution.py:314
  87.8 30.2 %collective-permute-start.17 = (bf16[128,2048]{1,0:T(8,128)(2,1)S(1)}, bf16[128,2048]{1,0:T(8,128)(2,1)S(1)}, u32[]{:S(2)}, u32[]{:S(2)}) collective-permute-start(bf16[128,2048]{1,0:T(8,128)(2,1)S(1)} %get-tuple-element.59), channel_id=1, source_target_pairs={{0,6},{2,0},{4,2},{6,4},{1,7},{3,1},{5,3},{7,5},{8,14},{10,8},{12,... | collective-permute-start | bytes 1572872 | tf_op jit(solution)/shard_map/ppermute | solution.py:314
  118.1 23.9 %collective-permute-start.18 = (bf16[128,2048]{1,0:T(8,128)(2,1)S(1)}, bf16[128,2048]{1,0:T(8,128)(2,1)S(1)}, u32[]{:S(2)}, u32[]{:S(2)}) collective-permute-start(bf16[128,2048]{1,0:T(8,128)(2,1)S(1)} %get-tuple-element.62), channel_id=1, source_target_pairs={{0,2},{2,4},{4,6},{6,0},{1,3},{3,5},{5,7},{7,1},{8,10},{10,12},{12... | collective-permute-start | bytes 1572872 | tf_op jit(solution)/shard_map/ppermute | solution.py:314
  119.8 22.2 %collective-permute-start.19 = (bf16[128,2048]{1,0:T(8,128)(2,1)S(1)}, bf16[128,2048]{1,0:T(8,128)(2,1)S(1)}, u32[]{:S(2)}, u32[]{:S(2)}) collective-permute-start(bf16[128,2048]{1,0:T(8,128)(2,1)S(1)} %get-tuple-element.63), channel_id=1, source_target_pairs={{0,6},{2,0},{4,2},{6,4},{1,7},{3,1},{5,3},{7,5},{8,14},{10,8},{12,... | collective-permute-start | bytes 1572872 | tf_op jit(solution)/shard_map/ppermute | solution.py:314
  124.1 15.7 %collective-permute-start.28 = (bf16[128,1024]{1,0:T(8,128)(2,1)S(1)}, bf16[128,1024]{1,0:T(8,128)(2,1)S(1)}, u32[]{:S(2)}, u32[]{:S(2)}) collective-permute-start(bf16[128,1024]{1,0:T(8,128)(2,1)S(1)} %get-tuple-element.95), channel_id=1, source_target_pairs={{0,2},{2,4},{4,6},{6,0},{1,3},{3,5},{5,7},{7,1},{8,10},{10,12},{12... | collective-permute-start | bytes 786440 | tf_op jit(solution)/shard_map/ppermute | solution.py:314
  124.5 20.9 %collective-permute-start.34 = (bf16[128,1024]{1,0:T(8,128)(2,1)S(1)}, bf16[128,1024]{1,0:T(8,128)(2,1)S(1)}, u32[]{:S(2)}, u32[]{:S(2)}) collective-permute-start(bf16[128,1024]{1,0:T(8,128)(2,1)S(1)} %get-tuple-element.96), channel_id=1, source_target_pairs={{0,2},{2,4},{4,6},{6,0},{1,3},{3,5},{5,7},{7,1},{8,10},{10,12},{12... | collective-permute-start | bytes 786440 | tf_op jit(solution)/shard_map/ppermute | solution.py:314
  126.1 15.5 %collective-permute-start.29 = (bf16[128,1024]{1,0:T(8,128)(2,1)S(1)}, bf16[128,1024]{1,0:T(8,128)(2,1)S(1)}, u32[]{:S(2)}, u32[]{:S(2)}) collective-permute-start(bf16[128,1024]{1,0:T(8,128)(2,1)S(1)} %get-tuple-element.93), channel_id=1, source_target_pairs={{0,6},{2,0},{4,2},{6,4},{1,7},{3,1},{5,3},{7,5},{8,14},{10,8},{12,... | collective-permute-start | bytes 786440 | tf_op jit(solution)/shard_map/ppermute | solution.py:314
  139.8 9.2 %collective-permute-start.35 = (bf16[128,1024]{1,0:T(8,128)(2,1)S(1)}, bf16[128,1024]{1,0:T(8,128)(2,1)S(1)}, u32[]{:S(2)}, u32[]{:S(2)}) collective-permute-start(bf16[128,1024]{1,0:T(8,128)(2,1)S(1)} %get-tuple-element.94), channel_id=1, source_target_pairs={{0,6},{2,0},{4,2},{6,4},{1,7},{3,1},{5,3},{7,5},{8,14},{10,8},{12,... | collective-permute-start | bytes 786440 | tf_op jit(solution)/shard_map/ppermute | solution.py:314
  141.7 10.5 %collective-permute-start.30 = (bf16[128,1024]{1,0:T(8,128)(2,1)S(1)}, bf16[128,1024]{1,0:T(8,128)(2,1)S(1)}, u32[]{:S(2)}, u32[]{:S(2)}) collective-permute-start(bf16[128,1024]{1,0:T(8,128)(2,1)S(1)} %get-tuple-element.77), channel_id=1, source_target_pairs={{0,2},{2,4},{4,6},{6,0},{1,3},{3,5},{5,7},{7,1},{8,10},{10,12},{12... | collective-permute-start | bytes 786440 | tf_op jit(solution)/shard_map/ppermute | solution.py:314
  142.1 28.9 %collective-permute-start.20 = (bf16[128,2048]{1,0:T(8,128)(2,1)S(1)}, bf16[128,2048]{1,0:T(8,128)(2,1)S(1)}, u32[]{:S(2)}, u32[]{:S(2)}) collective-permute-start(bf16[128,2048]{1,0:T(8,128)(2,1)S(1)} %get-tuple-element.64), channel_id=1, source_target_pairs={{0,2},{2,4},{4,6},{6,0},{1,3},{3,5},{5,7},{7,1},{8,10},{10,12},{12... | collective-permute-start | bytes 1572872 | tf_op jit(solution)/shard_map/ppermute | solution.py:314
  142.6 31.6 %collective-permute-start.21 = (bf16[128,2048]{1,0:T(8,128)(2,1)S(1)}, bf16[128,2048]{1,0:T(8,128)(2,1)S(1)}, u32[]{:S(2)}, u32[]{:S(2)}) collective-permute-start(bf16[128,2048]{1,0:T(8,128)(2,1)S(1)} %get-tuple-element.65), channel_id=1, source_target_pairs={{0,6},{2,0},{4,2},{6,4},{1,7},{3,1},{5,3},{7,5},{8,14},{10,8},{12,... | collective-permute-start | bytes 1572872 | tf_op jit(solution)/shard_map/ppermute | solution.py:314
  145.4 20.4 %collective-permute-start.31 = (bf16[128,1024]{1,0:T(8,128)(2,1)S(1)}, bf16[128,1024]{1,0:T(8,128)(2,1)S(1)}, u32[]{:S(2)}, u32[]{:S(2)}) collective-permute-start(bf16[128,1024]{1,0:T(8,128)(2,1)S(1)} %get-tuple-element.78), channel_id=1, source_target_pairs={{0,6},{2,0},{4,2},{6,4},{1,7},{3,1},{5,3},{7,5},{8,14},{10,8},{12,... | collective-permute-start | bytes 786440 | tf_op jit(solution)/shard_map/ppermute | solution.py:314
  149.0 19.4 %collective-permute-start.36 = (bf16[128,1024]{1,0:T(8,128)(2,1)S(1)}, bf16[128,1024]{1,0:T(8,128)(2,1)S(1)}, u32[]{:S(2)}, u32[]{:S(2)}) collective-permute-start(bf16[128,1024]{1,0:T(8,128)(2,1)S(1)} %get-tuple-element.82), channel_id=1, source_target_pairs={{0,2},{2,4},{4,6},{6,0},{1,3},{3,5},{5,7},{7,1},{8,10},{10,12},{12... | collective-permute-start | bytes 786440 | tf_op jit(solution)/shard_map/ppermute | solution.py:314
  152.1 18.7 %collective-permute-start.37 = (bf16[128,1024]{1,0:T(8,128)(2,1)S(1)}, bf16[128,1024]{1,0:T(8,128)(2,1)S(1)}, u32[]{:S(2)}, u32[]{:S(2)}) collective-permute-start(bf16[128,1024]{1,0:T(8,128)(2,1)S(1)} %get-tuple-element.83), channel_id=1, source_target_pairs={{0,6},{2,0},{4,2},{6,4},{1,7},{3,1},{5,3},{7,5},{8,14},{10,8},{12,... | collective-permute-start | bytes 786440 | tf_op jit(solution)/shard_map/ppermute | solution.py:314
  168.5 9.2 %collective-permute-start.33 = (bf16[128,1024]{1,0:T(8,128)(2,1)S(1)}, bf16[128,1024]{1,0:T(8,128)(2,1)S(1)}, u32[]{:S(2)}, u32[]{:S(2)}) collective-permute-start(bf16[128,1024]{1,0:T(8,128)(2,1)S(1)} %get-tuple-element.80), channel_id=1, source_target_pairs={{0,6},{2,0},{4,2},{6,4},{1,7},{3,1},{5,3},{7,5},{8,14},{10,8},{12,... | collective-permute-start | bytes 786440 | tf_op jit(solution)/shard_map/ppermute | solution.py:314
  171.0 10.0 %collective-permute-start.39 = (bf16[128,1024]{1,0:T(8,128)(2,1)S(1)}, bf16[128,1024]{1,0:T(8,128)(2,1)S(1)}, u32[]{:S(2)}, u32[]{:S(2)}) collective-permute-start(bf16[128,1024]{1,0:T(8,128)(2,1)S(1)} %get-tuple-element.85), channel_id=1, source_target_pairs={{0,6},{2,0},{4,2},{6,4},{1,7},{3,1},{5,3},{7,5},{8,14},{10,8},{12,... | collective-permute-start | bytes 786440 | tf_op jit(solution)/shard_map/ppermute | solution.py:314
  (12 other events, 108.7 us)

commit v2 on v1

--- a/solution.py
+++ b/solution.py
@@ -72,7 +72,13 @@
 )
 
 
-def attn_kernel(spec, n, span, doc_ref, q_ref, *refs):
+def turn_block(pair, step, head):
+    if pair == 0:
+        return (head + BPD - 1 + 2 * step) % BPD
+    return (head + BPD // 2 * (1 - step)) % BPD
+
+
+def attn_kernel(spec, n, pair, doc_ref, q_ref, *refs):
     unit_refs = refs[:n]
     o_ref = refs[n]
     kv, qs, m_ref, l_ref, acc_ref, s_a, s_b, p_a, p_b, a_a, a_b, sems = refs[n + 1 :]
@@ -135,8 +141,11 @@
         pv = jnp.dot(p_src[...], kv[slot, 1], preferred_element_type=jnp.float32)
         acc_ref[...] = acc_ref[...] * a_src[...] + pv
 
-    @pl.loop(span[0], span[1])
-    def _(j):
+    head = lax.axis_index("head")
+
+    @pl.loop(0, 2)
+    def _(step):
+        j = turn_block(pair, step, head)
         for h in range(GRP):
             qs[h * BLK : (h + 1) * BLK] = q_ref[
                 pl.ds(pl.multiple_of(j * BLK, BLK), BLK), h * HD : (h + 1) * HD
@@ -162,27 +171,29 @@
                 hidden = hidden + (doc_ref[0, BPD * unit + b] < doc_q).astype(jnp.int32)
             return hidden * BLK
 
-        score(s_b, 0, (key_pos <= row_pos) & (key_pos >= hidden_keys(s_idx)))
-        soften(s_b, p_b, a_b)
-
         edge = jnp.minimum(full + 1, REACH)
-
-        @pl.when(some > full)
-        def _():
-            score(s_a, edge, key_pos >= hidden_keys(jnp.maximum(s_idx - edge, 0)))
-            mix(p_b, a_b, 0)
+        odd = full % 2
+        has_edge = (some > full).astype(jnp.int32)
+
+        def single_slot(k):
+            return jnp.where(k == 0, 0, jnp.where((k == 1) & (has_edge == 1), edge, 1))
+
+        singles = 1 + has_edge + odd
+
+        @pl.loop(0, singles)
+        def _(k):
+            slot = single_slot(k)
+            low = hidden_keys(jnp.maximum(s_idx - slot, 0))
+            high = jnp.where(k == 0, 0, TOK)
+            score(s_a, slot, (key_pos <= row_pos + high) & (key_pos >= low))
+
+            @pl.when(k > 0)
+            def _():
+                mix(p_b, a_b, single_slot(k - 1))
+
             soften(s_a, p_b, a_b)
 
-        pend = jnp.where(some > full, edge, 0)
-        odd = full % 2
-
-        @pl.when(odd == 1)
-        def _():
-            score(s_a, 1)
-            mix(p_b, a_b, pend)
-            soften(s_a, p_b, a_b)
-
-        pend = jnp.where(odd == 1, 1, pend)
+        pend = single_slot(singles - 1)
 
         @pl.when(full > 1)
         def _():
@@ -203,17 +214,17 @@
         for h in range(GRP):
             rows = slice(h * BLK, (h + 1) * BLK)
             total = jnp.sum(l_ref[rows], axis=1, keepdims=True)
-            o_ref[pl.ds(pl.multiple_of((j - span[0]) * BLK, BLK), BLK), h * HD : (h + 1) * HD] = (
+            o_ref[pl.ds(pl.multiple_of(step * BLK, BLK), BLK), h * HD : (h + 1) * HD] = (
                 acc_ref[rows] / total
             ).astype(o_ref.dtype)
 
 
-def attention(doc, q, units, spec, span):
+def attention(doc, q, units, spec, pair):
     n = len(units)
     return pl.pallas_call(
-        functools.partial(attn_kernel, spec, n, span),
+        functools.partial(attn_kernel, spec, n, pair),
         name="attend",
-        out_shape=jax.ShapeDtypeStruct(((span[1] - span[0]) * BLK, GRP * HD), jnp.bfloat16),
+        out_shape=jax.ShapeDtypeStruct((2 * BLK, GRP * HD), jnp.bfloat16),
         in_specs=[
             pl.BlockSpec(memory_space=pltpu.SMEM),
             pl.BlockSpec(memory_space=pltpu.VMEM),
@@ -236,9 +247,9 @@
         ],
         compiler_params=pltpu.CompilerParams(vmem_limit_bytes=16 << 20),
         cost_estimate=pl.CostEstimate(
-            flops=(span[1] - span[0]) * 1_500_000_000,
+            flops=3_000_000_000,
             bytes_accessed=4_000_000,
-            transcendentals=(span[1] - span[0]) * 2_000_000,
+            transcendentals=4_000_000,
         ),
     )(doc, q, *units)
 
@@ -253,15 +264,21 @@
     return lax.ppermute(v, "seq", pairs)
 
 
-def from_corner(own):
-    return lax.ppermute(own, "seq", [(ZN - 1, ZN * (XN - 1))])
+def up_row(v):
+    pairs = [(ZN * x + z, ZN * x + z + 1) for x in range(XN) for z in range(ZN - 1)]
+    pairs.append((ZN - 1, 0))
+    return lax.ppermute(v, "seq", pairs)
+
+
+def from_corner(v):
+    return lax.ppermute(v, "seq", [(0, ZN * (XN - 1))])
 
 
 def gather_apart(own, z):
     x1 = along_x(own, 1)
     x2 = along_x(own, 2)
-    below_own = along_z(own, 1)
-    corner = from_corner(own)
+    below_own = up_row(own)
+    corner = from_corner(below_own)
     below_x1 = along_z(x1, 1)
     above_x1 = along_z(x1, -1)
     below_x2 = along_z(x2, 1)
@@ -283,30 +300,39 @@
     ]
 
 
-def add_kernel(turn, first_col, ra_ref, rb_ref, p_ref, na_ref, nb_ref):
-    rows, width = ra_ref.shape
-    n = lax.axis_size("head")
-    me = lax.axis_index("head")
+TURNS = ((1, 0, 0), (0, 1, 0), (1, 1, 1))
+
+
+def add_kernel(turn, first_col, last_col, ra_ref, rb_ref, p_ref, na_ref, nb_ref):
+    rows = ra_ref.shape[0]
     half = p_ref.shape[1] // 2
-    ka = pl.multiple_of((me + 2 * n - 2 - turn) % n * rows, rows)
-    kb = pl.multiple_of((me + 2 + turn) % n * rows, rows)
-    c = first_col
-    na_ref[...] = ra_ref[...] + p_ref[pl.ds(ka, rows), c : c + width]
-    nb_ref[...] = rb_ref[...] + p_ref[pl.ds(kb, rows), half + c : half + c + width]
-
-
-def ring_add(turn, first_col, ra, rb, partial):
+    _, ka, kb = TURNS[turn]
+    skip = ra_ref.shape[1] != last_col - first_col
+    took = slice(first_col, last_col) if skip else slice(None)
+    step = 32
+
+    @pl.loop(0, rows // step)
+    def _(i):
+        at = pl.ds(pl.multiple_of(i * step, step), step)
+        pa = pl.ds(pl.multiple_of(ka * rows + i * step, step), step)
+        pb = pl.ds(pl.multiple_of(kb * rows + i * step, step), step)
+        na_ref[at] = ra_ref[at, took] + p_ref[pa, first_col:last_col]
+        nb_ref[at] = rb_ref[at, took] + p_ref[pb, half + first_col : half + last_col]
+
+
+def ring_add(turn, first_col, last_col, ra, rb, partials):
+    shape = (ra.shape[0], last_col - first_col)
     return pl.pallas_call(
-        functools.partial(add_kernel, turn, first_col),
+        functools.partial(add_kernel, turn, first_col, last_col),
         name="ring_add",
-        out_shape=[jax.ShapeDtypeStruct(ra.shape, ra.dtype)] * 2,
+        out_shape=[jax.ShapeDtypeStruct(shape, ra.dtype)] * 2,
         in_specs=[pl.BlockSpec(memory_space=pltpu.VMEM)] * 3,
         out_specs=[pl.BlockSpec(memory_space=pltpu.VMEM)] * 2,
         compiler_params=pltpu.CompilerParams(vmem_limit_bytes=16 << 20),
         cost_estimate=pl.CostEstimate(
             flops=100_000_000, bytes_accessed=12 * ra.size, transcendentals=0
         ),
-    )(ra, rb, partial)
+    )(ra, rb, partials[TURNS[turn][0]])
 
 
 def around(v, step):
@@ -315,22 +341,19 @@
 
 
 def first_kernel(own_ref, other_ref, w_ref, a_ref, b_ref):
-    n = lax.axis_size("head")
-    me = lax.axis_index("head")
     core = lax.axis_index("batch")
     depth = own_ref.shape[1]
     rows, half = a_ref.shape
     mine = pl.ds(pl.multiple_of(core * depth, depth), depth)
     theirs = pl.ds(pl.multiple_of((1 - core) * depth, depth), depth)
     tile = 512
-    for out_ref, block, base in ((a_ref, (me + n - 1) % n, 0), (b_ref, (me + 1) % n, half)):
-        at = pl.ds(pl.multiple_of(block * rows, rows), rows)
-        own, other = own_ref[at], other_ref[at]
+    for i, out_ref in enumerate((a_ref, b_ref)):
+        own, other = own_ref[i * rows : (i + 1) * rows], other_ref[i * rows : (i + 1) * rows]
 
         @pl.loop(0, half // tile)
-        def _(i):
-            start = pl.multiple_of(i * tile, tile)
-            cols = pl.ds(pl.multiple_of(base + i * tile, tile), tile)
+        def _(t):
+            start = pl.multiple_of(t * tile, tile)
+            cols = pl.ds(pl.multiple_of(i * half + t * tile, tile), tile)
             out_ref[:, pl.ds(start, tile)] = (
                 jnp.dot(own, w_ref[mine, cols], preferred_element_type=jnp.float32)
                 + jnp.dot(other, w_ref[theirs, cols], preferred_element_type=jnp.float32)
@@ -338,7 +361,7 @@
 
 
 def first_blocks(own, other, weight):
-    rows = own.shape[0] // lax.axis_size("head")
+    rows = own.shape[0] // 2
     half = weight.shape[1] // 2
     return pl.pallas_call(
         first_kernel,
@@ -354,9 +377,14 @@
 
 
 def ring_step(turn, a, b, partial, first_col=0):
+    a, b = ring_send(a, b)
+    return ring_add(turn, first_col, first_col + a.shape[1], a, b, partial)
+
+
+def ring_send(a, b):
     a = around(a, 1)
     b = around(b, -1)
-    return ring_add(turn, first_col, a, b, partial)
+    return a, b
 
 
 def swapped(v):
@@ -393,21 +421,25 @@
     units0 = gather_apart(of(0, kv_mine, kv_theirs), z)
 
     own1 = of(1, kv_mine, kv_theirs)
+    edge1 = lax.ppermute(own1, "seq", [(ZN - 1, 0)])
+    corner1 = from_corner(edge1)
     y1 = along_x(own1, 1)
     y2 = along_x(own1, 2)
-    corner1 = from_corner(own1)
     units0, (own1, y1, y2) = tie((units0, (own1, y1, y2)))
     stack1 = jnp.stack([own1, y1, y2])
     up1 = jnp.stack([jnp.where(z == 0, own1, y2), y1])
     below1 = along_z(stack1, 1)
     above1 = along_z(up1, -1)
-    attended0 = attention(
-        of(0, block_doc, doc_theirs), of(0, q_mine, q_theirs), units0, APART, (0, BPD)
-    )
-    other0 = swapped(attended0)
-    a0, b0 = first_blocks(attended0, other0, out_weight)
-    _, (attended0, other0) = tie(((a0, b0), (attended0, other0)))
-    partial0 = project(attended0, other0)
+    doc0, q0 = of(0, block_doc, doc_theirs), of(0, q_mine, q_theirs)
+    early0 = attention(doc0, q0, units0, APART, 0)
+    early0_other = swapped(early0)
+    a0, b0 = first_blocks(early0, early0_other, out_weight)
+    (q0, doc0, early0, early0_other), _ = tie(((q0, doc0, early0, early0_other), (a0, b0)))
+    late0 = attention(doc0, q0, units0, APART, 1)
+    late0_other = swapped(late0)
+    late0_sum = project(late0, late0_other)
+    early0_sum = project(early0, early0_other)
+    partial0 = (early0_sum, late0_sum)
 
     (below1, above1), _ = tie(((below1, above1), (a0, b0)))
     far_mixed1 = along_z(jnp.where((z == 1) | (z == 2), below1[0], below1[2]), 1)
@@ -415,21 +447,23 @@
     units1 = [stack1, below1, above1, far_mixed1, far_x1, corner1]
     doc1, q1 = of(1, block_doc, doc_theirs), of(1, q_mine, q_theirs)
     a0, b0 = ring_step(0, a0, b0, partial0)
-    upper = attention(doc1, q1, units1, STACKED, (0, BPD // 2))
+    early1 = attention(doc1, q1, units1, STACKED, 0)
+    early1_other = swapped(early1)
+    a1, b1 = first_blocks(early1, early1_other, out_weight)
     a0, b0 = ring_step(1, a0, b0, partial0)
-    lower = attention(doc1, q1, units1, STACKED, (BPD // 2, BPD))
+    late1 = attention(doc1, q1, units1, STACKED, 1)
     a0, b0 = ring_step(2, a0, b0, partial0)
-    attended1 = jnp.concatenate([upper, lower], axis=0)
-    other1 = swapped(attended1)
-    a1, b1 = first_blocks(attended1, other1, out_weight)
-    _, (attended1, other1) = tie(((a1, b1), (attended1, other1)))
-    partial1 = project(attended1, other1)
+    late1_other = swapped(late1)
+    (early1, early1_other), _ = tie(((early1, early1_other), (a1, b1)))
+    late1_sum = project(late1, late1_other)
+    early1_sum = project(early1, early1_other)
+    partial1 = (early1_sum, late1_sum)
     width = a1.shape[1] // STREAMS
+    a1, b1 = ring_send(a1, b1)
     tails = []
     for i in range(STREAMS):
-        cols = slice(i * width, (i + 1) * width)
-        a, b = a1[:, cols], b1[:, cols]
-        for turn in range(3):
+        a, b = ring_add(0, i * width, (i + 1) * width, a1, b1, partial1)
+        for turn in (1, 2):
             a, b = ring_step(turn, a, b, partial1, i * width)
         tails.append((a, b))
     sum0 = jnp.concatenate([a0, b0], axis=1)

time: 185 us -> 171 us (0.924)
  the two profiles are of different devices: /device:TPU:4 before, /device:TPU:36 now
where the time goes in v2:
time: 171 us
  starting transfers between devices  56.7 us (33%)
  waiting for transfers between devices  49.5 us (29%)
  Pallas kernels  46.6 us (27%)
  matrix products  9.34 us (5%)
  other arithmetic  4.55 us (3%)
  local copies, waits for them, and re-layouts  3.4 us (2%)
    pallas_call x4, Pallas kernels, attention(): pl.pallas_call(functools.partial(attn_kernel, spec, n, pair), name='atten...  40.7 us
    ppermute x16, waiting for transfers between devices, around(): return lax.ppermute(v, 'head', [(i, (i + step) % n) for i in range(n)])  26 us
    ppermute x16, starting transfers between devices, around(): return lax.ppermute(v, 'head', [(i, (i + step) % n) for i in range(n)])  24.1 us
    ppermute x10, starting transfers between devices, along_z(): return lax.ppermute(v, 'seq', pairs)  16.4 us
    ppermute x10, waiting for transfers between devices, along_z(): return lax.ppermute(v, 'seq', pairs)  11.8 us
    ppermute x4, waiting for transfers between devices, along_x(): return lax.ppermute(v, 'seq', pairs)  10.1 us
    dot_general x4, matrix products, project(): jnp.dot(both, out_weight, preferred_element_type=jnp.float32)  9.34 us
    ppermute x4, starting transfers between devices, along_x(): return lax.ppermute(v, 'seq', pairs)  8.76 us
  transfers between devices with their start and end apart: 41, of which 15 were waited for; matrix products, arithmetic and copies ran while one was open for 6% of the time, Pallas kernels for 27%

profile of v2, /device:TPU:36, one launch (start us, length us, event | category | flops | bytes accessed | tf_op | source)
XLA Modules:
  0.0 170.6 jit_solution(9636335201297511035)
XLA Ops:
  6.7 3.8 %collective-permute-start.5 = (bf16[2,512,128]{2,1,0:T(8,128)(2,1)S(1)}, bf16[2,512,128]{2,1,0:T(8,128)(2,1)S(1)}, u32[]{:S(2)}, u32[]{:S(2)}) collective-permute-start(bf16[2,512,128]{2,1,0:T(8,128)(2,1)S(1)} %get-tuple-element.49.refs_0_), channel_id=1, source_target_pairs={{0,8},{8,16},{16,24},{32,40},{40,48},{48,56},{64,72},{72,80},{80,8... | collective-permute-start | bytes 786440 | tf_op jit(solution)/shard_map/ppermute | solution.py:270
  10.5 3.1 %collective-permute-start.3 = (bf16[2,512,128]{2,1,0:T(8,128)(2,1)S(1)}, bf16[2,512,128]{2,1,0:T(8,128)(2,1)S(1)}, u32[]{:S(2)}, u32[]{:S(2)}) collective-permute-start(bf16[2,512,128]{2,1,0:T(8,128)(2,1)S(1)} %get-tuple-element.49.refs_0_), channel_id=1, source_target_pairs={{0,32},{8,40},{16,48},{24,56},{32,64},{40,72},{48,80},{56,88},{64,... | collective-permute-start | bytes 786440 | tf_op jit(solution)/shard_map/ppermute | solution.py:264
  13.8 2.8 %collective-permute-done.4.refs_2_ = bf16[2,512,128]{2,1,0:T(8,128)(2,1)S(1)} collective-permute-done((bf16[2,512,128]{2,1,0:T(8,128)(2,1)S(1)}, bf16[2,512,128]{2,1,0:T(8,128)(2,1)S(1)}, u32[]{:S(2)}, u32[]{:S(2)}) %collective-permute-start.4) | collective-permute-done | bytes 262176 | tf_op jit(solution)/shard_map/ppermute | solution.py:264
  19.9 3.1 %collective-permute-start.13 = (bf16[2,512,128]{2,1,0:T(8,128)(2,1)S(1)}, bf16[2,512,128]{2,1,0:T(8,128)(2,1)S(1)}, u32[]{:S(2)}, u32[]{:S(2)}) collective-permute-start(bf16[2,512,128]{2,1,0:T(8,128)(2,1)S(1)} %get-tuple-element.72), channel_id=1, source_target_pairs={{0,32},{8,40},{16,48},{24,56},{32,64},{40,72},{48,80},{56,88},{64,... | collective-permute-start | bytes 786440 | tf_op jit(solution)/shard_map/ppermute | solution.py:264
  24.1 2.7 %collective-permute-start.8 = (bf16[2,512,128]{2,1,0:T(8,128)(2,1)S(1)}, bf16[2,512,128]{2,1,0:T(8,128)(2,1)S(1)}, u32[]{:S(2)}, u32[]{:S(2)}) collective-permute-start(bf16[2,512,128]{2,1,0:T(8,128)(2,1)S(1)} %broadcast_select_fusion.7), channel_id=1, source_target_pairs={{0,24},{8,0},{16,8},{24,16},{32,56},{40,32},{48,40},{56,48},{64,88... | collective-permute-start | bytes 786440 | tf_op jit(solution)/shard_map/ppermute | solution.py:259
  26.9 4.3 %collective-permute-done.14 = bf16[2,512,128]{2,1,0:T(8,128)(2,1)S(1)} collective-permute-done((bf16[2,512,128]{2,1,0:T(8,128)(2,1)S(1)}, bf16[2,512,128]{2,1,0:T(8,128)(2,1)S(1)}, u32[]{:S(2)}, u32[]{:S(2)}) %collective-permute-start.14) | collective-permute-done | bytes 262176 | tf_op jit(solution)/shard_map/ppermute | solution.py:264
  31.9 2.9 %collective-permute-done.13 = bf16[2,512,128]{2,1,0:T(8,128)(2,1)S(1)} collective-permute-done((bf16[2,512,128]{2,1,0:T(8,128)(2,1)S(1)}, bf16[2,512,128]{2,1,0:T(8,128)(2,1)S(1)}, u32[]{:S(2)}, u32[]{:S(2)}) %collective-permute-start.13) | collective-permute-done | bytes 262176 | tf_op jit(solution)/shard_map/ppermute | solution.py:264
  39.4 4.6 %collective-permute-done.6.refs_4_ = bf16[2,512,128]{2,1,0:T(8,128)(2,1)S(1)} collective-permute-done((bf16[2,512,128]{2,1,0:T(8,128)(2,1)S(1)}, bf16[2,512,128]{2,1,0:T(8,128)(2,1)S(1)}, u32[]{:S(2)}, u32[]{:S(2)}) %collective-permute-start.6) | collective-permute-done | bytes 262176 | tf_op jit(solution)/shard_map/ppermute | solution.py:259
  44.0 4.7 %collective-permute-done.10.refs_8_ = bf16[2,512,128]{2,1,0:T(8,128)(2,1)S(1)} collective-permute-done((bf16[2,512,128]{2,1,0:T(8,128)(2,1)S(1)}, bf16[2,512,128]{2,1,0:T(8,128)(2,1)S(1)}, u32[]{:S(2)}, u32[]{:S(2)}) %collective-permute-start.10) | collective-permute-done | bytes 262176 | tf_op jit(solution)/shard_map/ppermute | solution.py:259
  50.4 8.4 %attend.4.own_ref = bf16[256,512]{1,0:T(8,128)(2,1)S(1)} custom-call(s32[1,64]{1,0:T(1,128)S(1)} %get-tuple-element.62.doc_ref, bf16[512,512]{1,0:T(8,128)(2,1)S(1)} %get-tuple-element.63.q_ref, bf16[2,512,128]{2,1,0:T(8,128)(2,1)S(1)} %get-tuple-element.49.refs_0_, bf16[2,512,128]{2,1,0:T(8,128)(2,1)S(1)} %collective-permute-done.3.refs_1_, ...), custom_call_target="tpu_custom_call" | custom-call | flops 3000000000 | bytes 4000000 | tf_op jit(solution)/shard_map/attend/pallas_call | solution.py:224
  60.4 2.6 %first_blocks.2 = (bf16[128,2048]{1,0:T(8,128)(2,1)S(1)}, bf16[128,2048]{1,0:T(8,128)(2,1)S(1)}) custom-call(bf16[256,512]{1,0:T(8,128)(2,1)S(1)} %attend.4.own_ref, bf16[256,512]{1,0:T(8,128)(2,1)S(1)} %collective-permute-done.15.other_ref, bf16[1024,4096]{1,0:T(8,128)(2,1)S(1)} %bitcast.27), custom_call_target="tpu_custom_call" | custom-call | flops 1073741824 | bytes 12582912 | tf_op jit(solution)/shard_map/first_blocks/pallas_call | solution.py:366
  66.3 8.6 %attend.5 = bf16[256,512]{1,0:T(8,128)(2,1)S(1)} custom-call(s32[1,64]{1,0:T(1,128)S(1)} %get-tuple-element.62.doc_ref, bf16[512,512]{1,0:T(8,128)(2,1)S(1)} %get-tuple-element.63.q_ref, bf16[2,512,128]{2,1,0:T(8,128)(2,1)S(1)} %get-tuple-element.49.refs_0_, bf16[2,512,128]{2,1,0:T(8,128)(2,1)S(1)} %collective-permute-done.3.refs_1_, ...), custom_call_target="tpu_custom_call" | custom-call | flops 3000000000 | bytes 4000000 | tf_op jit(solution)/shard_map/attend/pallas_call | solution.py:224
  75.1 4.2 %collective-permute-start.26 = (bf16[2,512,128]{2,1,0:T(8,128)(2,1)S(1)}, bf16[2,512,128]{2,1,0:T(8,128)(2,1)S(1)}, u32[]{:S(2)}, u32[]{:S(2)}) collective-permute-start(bf16[2,512,128]{2,1,0:T(8,128)(2,1)S(1)} %slice_bitcast_fusion), channel_id=1, source_target_pairs={{0,24},{8,0},{16,8},{24,16},{32,56},{40,32},{48,40},{56,48},{64,88... | collective-permute-start | bytes 786440 | tf_op jit(solution)/shard_map/ppermute | solution.py:259
  80.8 2.3 %convolution_convert_fusion.3.p_ref = bf16[256,4096]{1,0:T(8,128)(2,1)S(1)} fusion(bf16[1024,4096]{1,0:T(8,128)(2,1)S(1)} %bitcast.27, bf16[256,512]{1,0:T(8,128)(2,1)S(1)} %collective-permute-done.18, bf16[256,512]{1,0:T(8,128)(2,1)S(1)} %attend.5, pred[]{:T(512)S(6)} %eq.34), kind=kOutput, calls=%fused_computation.3 | convolution fusion | flops 2150891520 | bytes 11010049 | tf_op jit(solution)/shard_map/dot_general | solution.py:417
  83.7 2.9 %collective-permute-start.20 = (bf16[128,2048]{1,0:T(8,128)(2,1)S(1)}, bf16[128,2048]{1,0:T(8,128)(2,1)S(1)}, u32[]{:S(2)}, u32[]{:S(2)}) collective-permute-start(bf16[128,2048]{1,0:T(8,128)(2,1)S(1)} %get-tuple-element.65), channel_id=1, source_target_pairs={{0,6},{2,0},{4,2},{6,4},{1,7},{3,1},{5,3},{7,5},{8,14},{10,8},{12,... | collective-permute-start | bytes 1572872 | tf_op jit(solution)/shard_map/ppermute | solution.py:340
  88.2 11.9 %attend.7 = bf16[256,512]{1,0:T(8,128)(2,1)S(1)} custom-call(s32[1,64]{1,0:T(1,128)S(1)} %get-tuple-element.102.doc_ref, bf16[512,512]{1,0:T(8,128)(2,1)S(1)} %get-tuple-element.94.q_ref, bf16[3,2,512,128]{3,2,1,0:T(8,128)(2,1)S(1)} %pad_maximum_fusion.2.refs_0_, bf16[3,2,512,128]{3,2,1,0:T(8,128)(2,1)S(1)} %collective-permute-done.23.refs_1_, ...), custom_call_target="tpu_custom_call" | custom-call | flops 3000000000 | bytes 4000000 | tf_op jit(solution)/shard_map/attend/pallas_call | solution.py:224
  100.2 11.8 %attend.6.own_ref = bf16[256,512]{1,0:T(8,128)(2,1)S(1)} custom-call(s32[1,64]{1,0:T(1,128)S(1)} %get-tuple-element.102.doc_ref, bf16[512,512]{1,0:T(8,128)(2,1)S(1)} %get-tuple-element.94.q_ref, bf16[3,2,512,128]{3,2,1,0:T(8,128)(2,1)S(1)} %pad_maximum_fusion.2.refs_0_, bf16[3,2,512,128]{3,2,1,0:T(8,128)(2,1)S(1)} %collective-permute-done.23.refs_1_, ...), custom_call_target="tpu_custom_call" | custom-call | flops 3000000000 | bytes 4000000 | tf_op jit(solution)/shard_map/attend/pallas_call | solution.py:224
  112.8 2.3 %convolution_convert_fusion.2.p_ref = bf16[256,4096]{1,0:T(8,128)(2,1)S(1)} fusion(bf16[1024,4096]{1,0:T(8,128)(2,1)S(1)} %bitcast.27, bf16[256,512]{1,0:T(8,128)(2,1)S(1)} %collective-permute-done.15.other_ref, bf16[256,512]{1,0:T(8,128)(2,1)S(1)} %attend.4.own_ref, pred[]{:T(512)S(6)} %eq.34), kind=kOutput, calls=%fused_computation.2 | convolution fusion | flops 2150891520 | bytes 11010049 | tf_op jit(solution)/shard_map/dot_general | solution.py:417
  115.1 2.6 %first_blocks.3 = (bf16[128,2048]{1,0:T(8,128)(2,1)S(1)}, bf16[128,2048]{1,0:T(8,128)(2,1)S(1)}) custom-call(bf16[256,512]{1,0:T(8,128)(2,1)S(1)} %attend.6.own_ref, bf16[256,512]{1,0:T(8,128)(2,1)S(1)} %collective-permute-done.29.other_ref, bf16[1024,4096]{1,0:T(8,128)(2,1)S(1)} %bitcast.27), custom_call_target="tpu_custom_call" | custom-call | flops 1073741824 | bytes 12582912 | tf_op jit(solution)/shard_map/first_blocks/pallas_call | solution.py:366
  118.2 2.9 %collective-permute-start.31 = (bf16[128,2048]{1,0:T(8,128)(2,1)S(1)}, bf16[128,2048]{1,0:T(8,128)(2,1)S(1)}, u32[]{:S(2)}, u32[]{:S(2)}) collective-permute-start(bf16[128,2048]{1,0:T(8,128)(2,1)S(1)} %get-tuple-element.78), channel_id=1, source_target_pairs={{0,6},{2,0},{4,2},{6,4},{1,7},{3,1},{5,3},{7,5},{8,14},{10,8},{12,... | collective-permute-start | bytes 1572872 | tf_op jit(solution)/shard_map/ppermute | solution.py:340
  121.3 2.3 %convolution_convert_fusion.1.p_ref = bf16[256,4096]{1,0:T(8,128)(2,1)S(1)} fusion(bf16[1024,4096]{1,0:T(8,128)(2,1)S(1)} %bitcast.27, bf16[256,512]{1,0:T(8,128)(2,1)S(1)} %collective-permute-done.32, bf16[256,512]{1,0:T(8,128)(2,1)S(1)} %attend.7, pred[]{:T(512)S(6)} %eq.34), kind=kOutput, calls=%fused_computation.1 | convolution fusion | flops 2150891520 | bytes 11010049 | tf_op jit(solution)/shard_map/dot_general | solution.py:417
  123.6 3.3 %collective-permute-start.22 = (bf16[128,2048]{1,0:T(8,128)(2,1)S(1)}, bf16[128,2048]{1,0:T(8,128)(2,1)S(1)}, u32[]{:S(2)}, u32[]{:S(2)}) collective-permute-start(bf16[128,2048]{1,0:T(8,128)(2,1)S(1)} %get-tuple-element.69), channel_id=1, source_target_pairs={{0,6},{2,0},{4,2},{6,4},{1,7},{3,1},{5,3},{7,5},{8,14},{10,8},{12,... | collective-permute-start | bytes 1572872 | tf_op jit(solution)/shard_map/ppermute | solution.py:340
  126.9 6.9 %collective-permute-done.30.ra_ref = bf16[128,2048]{1,0:T(8,128)(2,1)S(1)} collective-permute-done((bf16[128,2048]{1,0:T(8,128)(2,1)S(1)}, bf16[128,2048]{1,0:T(8,128)(2,1)S(1)}, u32[]{:S(2)}, u32[]{:S(2)}) %collective-permute-start.30) | collective-permute-done | bytes 524320 | tf_op jit(solution)/shard_map/ppermute | solution.py:340
  134.7 2.6 %collective-permute-start.38 = (bf16[128,1024]{1,0:T(8,128)(2,1)S(1)}, bf16[128,1024]{1,0:T(8,128)(2,1)S(1)}, u32[]{:S(2)}, u32[]{:S(2)}) collective-permute-start(bf16[128,1024]{1,0:T(8,128)(2,1)S(1)} %get-tuple-element.87), channel_id=1, source_target_pairs={{0,6},{2,0},{4,2},{6,4},{1,7},{3,1},{5,3},{7,5},{8,14},{10,8},{12,... | collective-permute-start | bytes 786440 | tf_op jit(solution)/shard_map/ppermute | solution.py:340
  137.4 7.6 %collective-permute-done.21.ra_ref = bf16[128,2048]{1,0:T(8,128)(2,1)S(1)} collective-permute-done((bf16[128,2048]{1,0:T(8,128)(2,1)S(1)}, bf16[128,2048]{1,0:T(8,128)(2,1)S(1)}, u32[]{:S(2)}, u32[]{:S(2)}) %collective-permute-start.21) | collective-permute-done | bytes 524320 | tf_op jit(solution)/shard_map/ppermute | solution.py:340
  145.6 2.3 %convolution_convert_fusion.p_ref = bf16[256,4096]{1,0:T(8,128)(2,1)S(1)} fusion(bf16[1024,4096]{1,0:T(8,128)(2,1)S(1)} %bitcast.27, bf16[256,512]{1,0:T(8,128)(2,1)S(1)} %collective-permute-done.29.other_ref, bf16[256,512]{1,0:T(8,128)(2,1)S(1)} %attend.6.own_ref, pred[]{:T(512)S(6)} %eq.34), kind=kOutput, calls=%fused_computation | convolution fusion | flops 2150891520 | bytes 11010049 | tf_op jit(solution)/shard_map/dot_general | solution.py:417
  148.1 2.6 %collective-permute-done.37.ra_ref = bf16[128,1024]{1,0:T(8,128)(2,1)S(1)} collective-permute-done((bf16[128,1024]{1,0:T(8,128)(2,1)S(1)}, bf16[128,1024]{1,0:T(8,128)(2,1)S(1)}, u32[]{:S(2)}, u32[]{:S(2)}) %collective-permute-start.37) | collective-permute-done | bytes 262176 | tf_op jit(solution)/shard_map/ppermute | solution.py:340
  151.5 2.6 %collective-permute-start.40 = (bf16[128,1024]{1,0:T(8,128)(2,1)S(1)}, bf16[128,1024]{1,0:T(8,128)(2,1)S(1)}, u32[]{:S(2)}, u32[]{:S(2)}) collective-permute-start(bf16[128,1024]{1,0:T(8,128)(2,1)S(1)} %get-tuple-element.89), channel_id=1, source_target_pairs={{0,6},{2,0},{4,2},{6,4},{1,7},{3,1},{5,3},{7,5},{8,14},{10,8},{12,... | collective-permute-start | bytes 786440 | tf_op jit(solution)/shard_map/ppermute | solution.py:340
  154.1 2.2 %collective-permute-done.33.ra_ref = bf16[128,1024]{1,0:T(8,128)(2,1)S(1)} collective-permute-done((bf16[128,1024]{1,0:T(8,128)(2,1)S(1)}, bf16[128,1024]{1,0:T(8,128)(2,1)S(1)}, u32[]{:S(2)}, u32[]{:S(2)}) %collective-permute-start.33) | collective-permute-done | bytes 262176 | tf_op jit(solution)/shard_map/ppermute | solution.py:340
  157.1 2.6 %collective-permute-start.36 = (bf16[128,1024]{1,0:T(8,128)(2,1)S(1)}, bf16[128,1024]{1,0:T(8,128)(2,1)S(1)}, u32[]{:S(2)}, u32[]{:S(2)}) collective-permute-start(bf16[128,1024]{1,0:T(8,128)(2,1)S(1)} %get-tuple-element.84), channel_id=1, source_target_pairs={{0,6},{2,0},{4,2},{6,4},{1,7},{3,1},{5,3},{7,5},{8,14},{10,8},{12,... | collective-permute-start | bytes 786440 | tf_op jit(solution)/shard_map/ppermute | solution.py:340
  162.0 4.6 %collective-permute-done.35.ra_ref = bf16[128,1024]{1,0:T(8,128)(2,1)S(1)} collective-permute-done((bf16[128,1024]{1,0:T(8,128)(2,1)S(1)}, bf16[128,1024]{1,0:T(8,128)(2,1)S(1)}, u32[]{:S(2)}, u32[]{:S(2)}) %collective-permute-start.35) | collective-permute-done | bytes 262176 | tf_op jit(solution)/shard_map/ppermute | solution.py:340
  166.7 3.9 %broadcast_select_fusion = bf16[128,2,4096]{2,1,0:T(2,128)(2,1)} fusion(pred[2]{0:T(512)(128)(4,1)S(1)} %iota_compare_fusion, bf16[128,4096]{1,0:T(8,128)(2,1)S(1)} %pad_maximum_fusion.1, bf16[128,4096]{1,0:T(8,128)(2,1)S(1)} %pad_maximum_fusion), kind=kLoop, calls=%fused_computation.4 | loop fusion | flops 1048576 | bytes 4194306 | tf_op jit(solution)/shard_map/jit(_where)/select_n | solution.py:472
  (99 shorter events, 34.0 us)
Async XLA Ops:
  4.9 11.7 %collective-permute-start.4 = (bf16[2,512,128]{2,1,0:T(8,128)(2,1)S(1)}, bf16[2,512,128]{2,1,0:T(8,128)(2,1)S(1)}, u32[]{:S(2)}, u32[]{:S(2)}) collective-permute-start(bf16[2,512,128]{2,1,0:T(8,128)(2,1)S(1)} %get-tuple-element.49.refs_0_), channel_id=1, source_target_pairs={{0,64},{8,72},{16,80},{24,88},{32,96},{40,104},{48,112},{56,120},{... | collective-permute-start | bytes 786440 | tf_op jit(solution)/shard_map/ppermute | solution.py:264
  6.2 12.4 %collective-permute-start = (s32[1,64]{1,0:T(1,128)S(1)}, s32[1,64]{1,0:T(1,128)S(1)}, u32[]{:S(2)}, u32[]{:S(2)}) collective-permute-start(s32[1,64]{1,0:T(1,128)S(1)} %copy-done.1), channel_id=1, source_target_pairs={{0,1},{1,0},{2,3},{3,2},{4,5},{5,4},{6,7},{7,6},{8,9},{9,8},{10,11... | collective-permute-start | bytes 776 | tf_op jit(solution)/shard_map/ppermute | solution.py:391
  6.7 13.2 %collective-permute-start.5 = (bf16[2,512,128]{2,1,0:T(8,128)(2,1)S(1)}, bf16[2,512,128]{2,1,0:T(8,128)(2,1)S(1)}, u32[]{:S(2)}, u32[]{:S(2)}) collective-permute-start(bf16[2,512,128]{2,1,0:T(8,128)(2,1)S(1)} %get-tuple-element.49.refs_0_), channel_id=1, source_target_pairs={{0,8},{8,16},{16,24},{32,40},{40,48},{48,56},{64,72},{72,80},{80,8... | collective-permute-start | bytes 786440 | tf_op jit(solution)/shard_map/ppermute | solution.py:270
  10.5 12.4 %collective-permute-start.3 = (bf16[2,512,128]{2,1,0:T(8,128)(2,1)S(1)}, bf16[2,512,128]{2,1,0:T(8,128)(2,1)S(1)}, u32[]{:S(2)}, u32[]{:S(2)}) collective-permute-start(bf16[2,512,128]{2,1,0:T(8,128)(2,1)S(1)} %get-tuple-element.49.refs_0_), channel_id=1, source_target_pairs={{0,32},{8,40},{16,48},{24,56},{32,64},{40,72},{48,80},{56,88},{64,... | collective-permute-start | bytes 786440 | tf_op jit(solution)/shard_map/ppermute | solution.py:264
  13.7 22.7 %collective-permute-start.1 = (bf16[512,512]{1,0:T(8,128)(2,1)S(1)}, bf16[512,512]{1,0:T(8,128)(2,1)S(1)}, u32[]{:S(2)}, u32[]{:S(2)}) collective-permute-start(bf16[512,512]{1,0:T(8,128)(2,1)S(1)} %broadcast_select_fusion.3), channel_id=1, source_target_pairs={{0,1},{1,0},{2,3},{3,2},{4,5},{5,4},{6,7},{7,6},{8,9},{9,8},{10,11... | collective-permute-start | bytes 1572872 | tf_op jit(solution)/shard_map/ppermute | solution.py:391
  18.6 12.6 %collective-permute-start.14 = (bf16[2,512,128]{2,1,0:T(8,128)(2,1)S(1)}, bf16[2,512,128]{2,1,0:T(8,128)(2,1)S(1)}, u32[]{:S(2)}, u32[]{:S(2)}) collective-permute-start(bf16[2,512,128]{2,1,0:T(8,128)(2,1)S(1)} %get-tuple-element.72), channel_id=1, source_target_pairs={{0,64},{8,72},{16,80},{24,88},{32,96},{40,104},{48,112},{56,120},{... | collective-permute-start | bytes 786440 | tf_op jit(solution)/shard_map/ppermute | solution.py:264
  19.9 14.9 %collective-permute-start.13 = (bf16[2,512,128]{2,1,0:T(8,128)(2,1)S(1)}, bf16[2,512,128]{2,1,0:T(8,128)(2,1)S(1)}, u32[]{:S(2)}, u32[]{:S(2)}) collective-permute-start(bf16[2,512,128]{2,1,0:T(8,128)(2,1)S(1)} %get-tuple-element.72), channel_id=1, source_target_pairs={{0,32},{8,40},{16,48},{24,56},{32,64},{40,72},{48,80},{56,88},{64,... | collective-permute-start | bytes 786440 | tf_op jit(solution)/shard_map/ppermute | solution.py:264
  23.0 14.1 %collective-permute-start.9 = (bf16[2,512,128]{2,1,0:T(8,128)(2,1)S(1)}, bf16[2,512,128]{2,1,0:T(8,128)(2,1)S(1)}, u32[]{:S(2)}, u32[]{:S(2)}) collective-permute-start(bf16[2,512,128]{2,1,0:T(8,128)(2,1)S(1)} %collective-permute-done.3.refs_1_), channel_id=1, source_target_pairs={{0,24},{8,0},{16,8},{24,16},{32,56},{40,32},{48,40},{56,48},{64,88... | collective-permute-start | bytes 786440 | tf_op jit(solution)/shard_map/ppermute | solution.py:259
  24.1 15.2 %collective-permute-start.8 = (bf16[2,512,128]{2,1,0:T(8,128)(2,1)S(1)}, bf16[2,512,128]{2,1,0:T(8,128)(2,1)S(1)}, u32[]{:S(2)}, u32[]{:S(2)}) collective-permute-start(bf16[2,512,128]{2,1,0:T(8,128)(2,1)S(1)} %broadcast_select_fusion.7), channel_id=1, source_target_pairs={{0,24},{8,0},{16,8},{24,16},{32,56},{40,32},{48,40},{56,48},{64,88... | collective-permute-start | bytes 786440 | tf_op jit(solution)/shard_map/ppermute | solution.py:259
  36.4 12.2 %collective-permute-start.10 = (bf16[2,512,128]{2,1,0:T(8,128)(2,1)S(1)}, bf16[2,512,128]{2,1,0:T(8,128)(2,1)S(1)}, u32[]{:S(2)}, u32[]{:S(2)}) collective-permute-start(bf16[2,512,128]{2,1,0:T(8,128)(2,1)S(1)} %broadcast_select_fusion.6), channel_id=1, source_target_pairs={{0,8},{8,16},{16,24},{24,0},{32,40},{40,48},{48,56},{56,32},{64,72... | collective-permute-start | bytes 786440 | tf_op jit(solution)/shard_map/ppermute | solution.py:259
  37.0 11.6 %collective-permute-start.11 = (bf16[2,512,128]{2,1,0:T(8,128)(2,1)S(1)}, bf16[2,512,128]{2,1,0:T(8,128)(2,1)S(1)}, u32[]{:S(2)}, u32[]{:S(2)}) collective-permute-start(bf16[2,512,128]{2,1,0:T(8,128)(2,1)S(1)} %collective-permute-done.9.refs_7_), channel_id=1, source_target_pairs={{0,24},{8,0},{16,8},{24,16},{32,56},{40,32},{48,40},{56,48},{64,88... | collective-permute-start | bytes 786440 | tf_op jit(solution)/shard_map/ppermute | solution.py:259
  38.5 21.1 %collective-permute-start.27 = (bf16[2,512,128]{2,1,0:T(8,128)(2,1)S(1)}, bf16[2,512,128]{2,1,0:T(8,128)(2,1)S(1)}, u32[]{:S(2)}, u32[]{:S(2)}) collective-permute-start(bf16[2,512,128]{2,1,0:T(8,128)(2,1)S(1)} %get-tuple-element.72), channel_id=1, source_target_pairs={{24,0},{25,1},{26,2},{27,3},{28,4},{29,5},{30,6},{31,7}} | collective-permute-start | bytes 786440 | tf_op jit(solution)/shard_map/ppermute | solution.py:424
  48.7 26.3 %collective-permute-start.23 = (bf16[3,2,512,128]{3,2,1,0:T(8,128)(2,1)S(1)}, bf16[3,2,512,128]{3,2,1,0:T(8,128)(2,1)S(1)}, u32[]{:S(2)}, u32[]{:S(2)}) collective-permute-start(bf16[3,2,512,128]{3,2,1,0:T(8,128)(2,1)S(1)} %pad_maximum_fusion.2.refs_0_), channel_id=1, source_target_pairs={{0,8},{8,16},{16,24},{24,0},{32,40},{40,48},{48,56},{56,32},{64,72... | collective-permute-start | bytes 2359304 | tf_op jit(solution)/shard_map/ppermute | solution.py:259
  59.0 15.9 %collective-permute-start.24 = (bf16[2,2,512,128]{3,2,1,0:T(8,128)(2,1)S(1)}, bf16[2,2,512,128]{3,2,1,0:T(8,128)(2,1)S(1)}, u32[]{:S(2)}, u32[]{:S(2)}) collective-permute-start(bf16[2,2,512,128]{3,2,1,0:T(8,128)(2,1)S(1)} %pad_maximum_fusion.3), channel_id=1, source_target_pairs={{0,24},{8,0},{16,8},{24,16},{32,56},{40,32},{48,40},{56,48},{64,88... | collective-permute-start | bytes 1572872 | tf_op jit(solution)/shard_map/ppermute | solution.py:259
  59.6 26.9 %collective-permute-start.28 = (bf16[2,512,128]{2,1,0:T(8,128)(2,1)S(1)}, bf16[2,512,128]{2,1,0:T(8,128)(2,1)S(1)}, u32[]{:S(2)}, u32[]{:S(2)}) collective-permute-start(bf16[2,512,128]{2,1,0:T(8,128)(2,1)S(1)} %collective-permute-done.27), channel_id=1, source_target_pairs={{0,96},{1,97},{2,98},{3,99},{4,100},{5,101},{6,102},{7,103}} | collective-permute-start | bytes 786440 | tf_op jit(solution)/shard_map/ppermute | solution.py:274
  63.0 20.1 %collective-permute-start.16 = (bf16[128,2048]{1,0:T(8,128)(2,1)S(1)}, bf16[128,2048]{1,0:T(8,128)(2,1)S(1)}, u32[]{:S(2)}, u32[]{:S(2)}) collective-permute-start(bf16[128,2048]{1,0:T(8,128)(2,1)S(1)} %get-tuple-element.60), channel_id=1, source_target_pairs={{0,2},{2,4},{4,6},{6,0},{1,3},{3,5},{5,7},{7,1},{8,10},{10,12},{12... | collective-permute-start | bytes 1572872 | tf_op jit(solution)/shard_map/ppermute | solution.py:340
  64.7 18.5 %collective-permute-start.17 = (bf16[128,2048]{1,0:T(8,128)(2,1)S(1)}, bf16[128,2048]{1,0:T(8,128)(2,1)S(1)}, u32[]{:S(2)}, u32[]{:S(2)}) collective-permute-start(bf16[128,2048]{1,0:T(8,128)(2,1)S(1)} %get-tuple-element.61), channel_id=1, source_target_pairs={{0,6},{2,0},{4,2},{6,4},{1,7},{3,1},{5,3},{7,5},{8,14},{10,8},{12,... | collective-permute-start | bytes 1572872 | tf_op jit(solution)/shard_map/ppermute | solution.py:340
  75.1 11.5 %collective-permute-start.26 = (bf16[2,512,128]{2,1,0:T(8,128)(2,1)S(1)}, bf16[2,512,128]{2,1,0:T(8,128)(2,1)S(1)}, u32[]{:S(2)}, u32[]{:S(2)}) collective-permute-start(bf16[2,512,128]{2,1,0:T(8,128)(2,1)S(1)} %slice_bitcast_fusion), channel_id=1, source_target_pairs={{0,24},{8,0},{16,8},{24,16},{32,56},{40,32},{48,40},{56,48},{64,88... | collective-permute-start | bytes 786440 | tf_op jit(solution)/shard_map/ppermute | solution.py:259
  83.3 37.8 %collective-permute-start.19 = (bf16[128,2048]{1,0:T(8,128)(2,1)S(1)}, bf16[128,2048]{1,0:T(8,128)(2,1)S(1)}, u32[]{:S(2)}, u32[]{:S(2)}) collective-permute-start(bf16[128,2048]{1,0:T(8,128)(2,1)S(1)} %get-tuple-element.64), channel_id=1, source_target_pairs={{0,2},{2,4},{4,6},{6,0},{1,3},{3,5},{5,7},{7,1},{8,10},{10,12},{12... | collective-permute-start | bytes 1572872 | tf_op jit(solution)/shard_map/ppermute | solution.py:340
  83.7 37.3 %collective-permute-start.20 = (bf16[128,2048]{1,0:T(8,128)(2,1)S(1)}, bf16[128,2048]{1,0:T(8,128)(2,1)S(1)}, u32[]{:S(2)}, u32[]{:S(2)}) collective-permute-start(bf16[128,2048]{1,0:T(8,128)(2,1)S(1)} %get-tuple-element.65), channel_id=1, source_target_pairs={{0,6},{2,0},{4,2},{6,4},{1,7},{3,1},{5,3},{7,5},{8,14},{10,8},{12,... | collective-permute-start | bytes 1572872 | tf_op jit(solution)/shard_map/ppermute | solution.py:340
  100.1 21.2 %collective-permute-start.32 = (bf16[256,512]{1,0:T(8,128)(2,1)S(1)}, bf16[256,512]{1,0:T(8,128)(2,1)S(1)}, u32[]{:S(2)}, u32[]{:S(2)}) collective-permute-start(bf16[256,512]{1,0:T(8,128)(2,1)S(1)} %attend.7), channel_id=1, source_target_pairs={{0,1},{1,0},{2,3},{3,2},{4,5},{5,4},{6,7},{7,6},{8,9},{9,8},{10,11... | collective-permute-start | bytes 786440 | tf_op jit(solution)/shard_map/ppermute | solution.py:391
  117.7 16.1 %collective-permute-start.30 = (bf16[128,2048]{1,0:T(8,128)(2,1)S(1)}, bf16[128,2048]{1,0:T(8,128)(2,1)S(1)}, u32[]{:S(2)}, u32[]{:S(2)}) collective-permute-start(bf16[128,2048]{1,0:T(8,128)(2,1)S(1)} %get-tuple-element.77), channel_id=1, source_target_pairs={{0,2},{2,4},{4,6},{6,0},{1,3},{3,5},{5,7},{7,1},{8,10},{10,12},{12... | collective-permute-start | bytes 1572872 | tf_op jit(solution)/shard_map/ppermute | solution.py:340
  118.2 15.7 %collective-permute-start.31 = (bf16[128,2048]{1,0:T(8,128)(2,1)S(1)}, bf16[128,2048]{1,0:T(8,128)(2,1)S(1)}, u32[]{:S(2)}, u32[]{:S(2)}) collective-permute-start(bf16[128,2048]{1,0:T(8,128)(2,1)S(1)} %get-tuple-element.78), channel_id=1, source_target_pairs={{0,6},{2,0},{4,2},{6,4},{1,7},{3,1},{5,3},{7,5},{8,14},{10,8},{12,... | collective-permute-start | bytes 1572872 | tf_op jit(solution)/shard_map/ppermute | solution.py:340
  121.2 23.9 %collective-permute-start.21 = (bf16[128,2048]{1,0:T(8,128)(2,1)S(1)}, bf16[128,2048]{1,0:T(8,128)(2,1)S(1)}, u32[]{:S(2)}, u32[]{:S(2)}) collective-permute-start(bf16[128,2048]{1,0:T(8,128)(2,1)S(1)} %get-tuple-element.68), channel_id=1, source_target_pairs={{0,2},{2,4},{4,6},{6,0},{1,3},{3,5},{5,7},{7,1},{8,10},{10,12},{12... | collective-permute-start | bytes 1572872 | tf_op jit(solution)/shard_map/ppermute | solution.py:340
  123.6 24.3 %collective-permute-start.22 = (bf16[128,2048]{1,0:T(8,128)(2,1)S(1)}, bf16[128,2048]{1,0:T(8,128)(2,1)S(1)}, u32[]{:S(2)}, u32[]{:S(2)}) collective-permute-start(bf16[128,2048]{1,0:T(8,128)(2,1)S(1)} %get-tuple-element.69), channel_id=1, source_target_pairs={{0,6},{2,0},{4,2},{6,4},{1,7},{3,1},{5,3},{7,5},{8,14},{10,8},{12,... | collective-permute-start | bytes 1572872 | tf_op jit(solution)/shard_map/ppermute | solution.py:340
  133.9 16.8 %collective-permute-start.37 = (bf16[128,1024]{1,0:T(8,128)(2,1)S(1)}, bf16[128,1024]{1,0:T(8,128)(2,1)S(1)}, u32[]{:S(2)}, u32[]{:S(2)}) collective-permute-start(bf16[128,1024]{1,0:T(8,128)(2,1)S(1)} %get-tuple-element.86), channel_id=1, source_target_pairs={{0,2},{2,4},{4,6},{6,0},{1,3},{3,5},{5,7},{7,1},{8,10},{10,12},{12... | collective-permute-start | bytes 786440 | tf_op jit(solution)/shard_map/ppermute | solution.py:340
  134.7 16.0 %collective-permute-start.38 = (bf16[128,1024]{1,0:T(8,128)(2,1)S(1)}, bf16[128,1024]{1,0:T(8,128)(2,1)S(1)}, u32[]{:S(2)}, u32[]{:S(2)}) collective-permute-start(bf16[128,1024]{1,0:T(8,128)(2,1)S(1)} %get-tuple-element.87), channel_id=1, source_target_pairs={{0,6},{2,0},{4,2},{6,4},{1,7},{3,1},{5,3},{7,5},{8,14},{10,8},{12,... | collective-permute-start | bytes 786440 | tf_op jit(solution)/shard_map/ppermute | solution.py:340
  137.3 18.9 %collective-permute-start.33 = (bf16[128,1024]{1,0:T(8,128)(2,1)S(1)}, bf16[128,1024]{1,0:T(8,128)(2,1)S(1)}, u32[]{:S(2)}, u32[]{:S(2)}) collective-permute-start(bf16[128,1024]{1,0:T(8,128)(2,1)S(1)} %get-tuple-element.79), channel_id=1, source_target_pairs={{0,2},{2,4},{4,6},{6,0},{1,3},{3,5},{5,7},{7,1},{8,10},{10,12},{12... | collective-permute-start | bytes 786440 | tf_op jit(solution)/shard_map/ppermute | solution.py:340
  145.0 11.2 %collective-permute-start.34 = (bf16[128,1024]{1,0:T(8,128)(2,1)S(1)}, bf16[128,1024]{1,0:T(8,128)(2,1)S(1)}, u32[]{:S(2)}, u32[]{:S(2)}) collective-permute-start(bf16[128,1024]{1,0:T(8,128)(2,1)S(1)} %get-tuple-element.80), channel_id=1, source_target_pairs={{0,6},{2,0},{4,2},{6,4},{1,7},{3,1},{5,3},{7,5},{8,14},{10,8},{12,... | collective-permute-start | bytes 786440 | tf_op jit(solution)/shard_map/ppermute | solution.py:340
  150.7 11.2 %collective-permute-start.39 = (bf16[128,1024]{1,0:T(8,128)(2,1)S(1)}, bf16[128,1024]{1,0:T(8,128)(2,1)S(1)}, u32[]{:S(2)}, u32[]{:S(2)}) collective-permute-start(bf16[128,1024]{1,0:T(8,128)(2,1)S(1)} %get-tuple-element.88), channel_id=1, source_target_pairs={{0,2},{2,4},{4,6},{6,0},{1,3},{3,5},{5,7},{7,1},{8,10},{10,12},{12... | collective-permute-start | bytes 786440 | tf_op jit(solution)/shard_map/ppermute | solution.py:340
  151.5 10.4 %collective-permute-start.40 = (bf16[128,1024]{1,0:T(8,128)(2,1)S(1)}, bf16[128,1024]{1,0:T(8,128)(2,1)S(1)}, u32[]{:S(2)}, u32[]{:S(2)}) collective-permute-start(bf16[128,1024]{1,0:T(8,128)(2,1)S(1)} %get-tuple-element.89), channel_id=1, source_target_pairs={{0,6},{2,0},{4,2},{6,4},{1,7},{3,1},{5,3},{7,5},{8,14},{10,8},{12,... | collective-permute-start | bytes 786440 | tf_op jit(solution)/shard_map/ppermute | solution.py:340
  156.4 10.2 %collective-permute-start.35 = (bf16[128,1024]{1,0:T(8,128)(2,1)S(1)}, bf16[128,1024]{1,0:T(8,128)(2,1)S(1)}, u32[]{:S(2)}, u32[]{:S(2)}) collective-permute-start(bf16[128,1024]{1,0:T(8,128)(2,1)S(1)} %get-tuple-element.83), channel_id=1, source_target_pairs={{0,2},{2,4},{4,6},{6,0},{1,3},{3,5},{5,7},{7,1},{8,10},{10,12},{12... | collective-permute-start | bytes 786440 | tf_op jit(solution)/shard_map/ppermute | solution.py:340
  (13 other events, 91.6 us)

commit v3 on v2

--- a/solution.py
+++ b/solution.py
@@ -260,7 +260,7 @@
 
 
 def along_x(v, step):
-    pairs = [(ZN * x + z, ZN * (x + step) + z) for x in range(XN - step) for z in range(ZN)]
+    pairs = [(ZN * x + z, ZN * ((x + step) % XN) + z) for x in range(XN) for z in range(ZN)]
     return lax.ppermute(v, "seq", pairs)
 
 
@@ -396,9 +396,8 @@
     first = core == 0
     q2 = queries[0].reshape(TOK, 2 * GRP * HD)
     halves_q = (q2[:, : GRP * HD], q2[:, GRP * HD :])
-    halves_kv = tuple(
-        jnp.stack([key_states[0, :, h], value_vectors[0, :, h]], axis=0) for h in range(2)
-    )
+    by_head = jnp.moveaxis(jnp.stack([key_states[0], value_vectors[0]]), 2, 0)
+    halves_kv = (by_head[0], by_head[1])
     kv_mine = jnp.where(first, halves_kv[0], halves_kv[1])
     kv_theirs = swapped(jnp.where(first, halves_kv[1], halves_kv[0]))
     q_mine = jnp.where(first, halves_q[0], halves_q[1])

time: 171 us -> 168 us (0.982)
  starting transfers between devices: 56.7 us -> 54.3 us
    ppermute x4, starting transfers between devices: 8.76 us -> 4.51 us  [along_x(): return lax.ppermute(v, 'seq', pairs)]
    slice x2 -> x0, local copies, waits for them, and re-layouts: 3.02 us -> none  [the longest x1 1.53 us: on_device(): value_vectors[0, :, h]]
    ppermute x10, starting transfers between devices: 16.4 us -> 18.6 us  [along_z(): return lax.ppermute(v, 'seq', pairs)]
    unnamed x9 -> x11, local copies, waits for them, and re-layouts: 0.29 us -> 2.34 us
  transfers between devices with their start and end apart: 41 -> 41, of which waited for: 15 -> 16; matrix products, arithmetic and copies ran while one was open for 6% -> 6% of each run, Pallas kernels for 27% -> 28%
where the time goes in v3:
time: 168 us
  starting transfers between devices  54.3 us (32%)
  waiting for transfers between devices  49.9 us (30%)
  Pallas kernels  46.7 us (28%)
  matrix products  9.34 us (6%)
  other arithmetic  4.58 us (3%)
  local copies, waits for them, and re-layouts  2.36 us (1%)
    pallas_call x4, Pallas kernels, attention(): pl.pallas_call(functools.partial(attn_kernel, spec, n, pair), name='atten...  40.7 us
    ppermute x16, waiting for transfers between devices, around(): return lax.ppermute(v, 'head', [(i, (i + step) % n) for i in range(n)])  25.9 us
    ppermute x16, starting transfers between devices, around(): return lax.ppermute(v, 'head', [(i, (i + step) % n) for i in range(n)])  24.1 us
    ppermute x10, starting transfers between devices, along_z(): return lax.ppermute(v, 'seq', pairs)  18.6 us
    ppermute x10, waiting for transfers between devices, along_z(): return lax.ppermute(v, 'seq', pairs)  11.6 us
    ppermute x4, waiting for transfers between devices, along_x(): return lax.ppermute(v, 'seq', pairs)  10.8 us
    dot_general x4, matrix products, project(): jnp.dot(both, out_weight, preferred_element_type=jnp.float32)  9.34 us
    pallas_call x2, Pallas kernels, first_blocks(): pl.pallas_call(first_kernel, name='first_blocks', out_shape=[jax.ShapeDty...  5.17 us
  transfers between devices with their start and end apart: 41, of which 16 were waited for; matrix products, arithmetic and copies ran while one was open for 6% of the time, Pallas kernels for 28%

profile of v3, /device:TPU:36, one launch (start us, length us, event | category | flops | bytes accessed | tf_op | source)
XLA Modules:
  0.0 167.6 jit_solution(1041578852205999205)
XLA Ops:
  4.7 3.8 %collective-permute-start.5 = (bf16[2,512,128]{2,1,0:T(8,128)(2,1)S(1)}, bf16[2,512,128]{2,1,0:T(8,128)(2,1)S(1)}, u32[]{:S(2)}, u32[]{:S(2)}) collective-permute-start(bf16[2,512,128]{2,1,0:T(8,128)(2,1)S(1)} %get-tuple-element.49.refs_0_), channel_id=1, source_target_pairs={{0,8},{8,16},{16,24},{32,40},{40,48},{48,56},{64,72},{72,80},{80,8... | collective-permute-start | bytes 786440 | tf_op jit(solution)/shard_map/ppermute | solution.py:270
  8.6 2.2 %collective-permute-start.3 = (bf16[2,512,128]{2,1,0:T(8,128)(2,1)S(1)}, bf16[2,512,128]{2,1,0:T(8,128)(2,1)S(1)}, u32[]{:S(2)}, u32[]{:S(2)}) collective-permute-start(bf16[2,512,128]{2,1,0:T(8,128)(2,1)S(1)} %get-tuple-element.49.refs_0_), channel_id=1, source_target_pairs={{0,32},{8,40},{16,48},{24,56},{32,64},{40,72},{48,80},{56,88},{64,... | collective-permute-start | bytes 786440 | tf_op jit(solution)/shard_map/ppermute | solution.py:264
  10.9 3.6 %collective-permute-done.4.refs_2_ = bf16[2,512,128]{2,1,0:T(8,128)(2,1)S(1)} collective-permute-done((bf16[2,512,128]{2,1,0:T(8,128)(2,1)S(1)}, bf16[2,512,128]{2,1,0:T(8,128)(2,1)S(1)}, u32[]{:S(2)}, u32[]{:S(2)}) %collective-permute-start.4) | collective-permute-done | bytes 262176 | tf_op jit(solution)/shard_map/ppermute | solution.py:264
  21.3 3.2 %collective-permute-start.8 = (bf16[2,512,128]{2,1,0:T(8,128)(2,1)S(1)}, bf16[2,512,128]{2,1,0:T(8,128)(2,1)S(1)}, u32[]{:S(2)}, u32[]{:S(2)}) collective-permute-start(bf16[2,512,128]{2,1,0:T(8,128)(2,1)S(1)} %broadcast_select_fusion.6), channel_id=1, source_target_pairs={{0,24},{8,0},{16,8},{24,16},{32,56},{40,32},{48,40},{56,48},{64,88... | collective-permute-start | bytes 786440 | tf_op jit(solution)/shard_map/ppermute | solution.py:259
  24.5 2.7 %collective-permute-done.14 = bf16[2,512,128]{2,1,0:T(8,128)(2,1)S(1)} collective-permute-done((bf16[2,512,128]{2,1,0:T(8,128)(2,1)S(1)}, bf16[2,512,128]{2,1,0:T(8,128)(2,1)S(1)}, u32[]{:S(2)}, u32[]{:S(2)}) %collective-permute-start.14) | collective-permute-done | bytes 262176 | tf_op jit(solution)/shard_map/ppermute | solution.py:264
  27.9 2.7 %collective-permute-done.13 = bf16[2,512,128]{2,1,0:T(8,128)(2,1)S(1)} collective-permute-done((bf16[2,512,128]{2,1,0:T(8,128)(2,1)S(1)}, bf16[2,512,128]{2,1,0:T(8,128)(2,1)S(1)}, u32[]{:S(2)}, u32[]{:S(2)}) %collective-permute-start.13) | collective-permute-done | bytes 262176 | tf_op jit(solution)/shard_map/ppermute | solution.py:264
  35.5 4.3 %collective-permute-done.6.refs_4_ = bf16[2,512,128]{2,1,0:T(8,128)(2,1)S(1)} collective-permute-done((bf16[2,512,128]{2,1,0:T(8,128)(2,1)S(1)}, bf16[2,512,128]{2,1,0:T(8,128)(2,1)S(1)}, u32[]{:S(2)}, u32[]{:S(2)}) %collective-permute-start.6) | collective-permute-done | bytes 262176 | tf_op jit(solution)/shard_map/ppermute | solution.py:259
  39.8 4.7 %collective-permute-done.10.refs_8_ = bf16[2,512,128]{2,1,0:T(8,128)(2,1)S(1)} collective-permute-done((bf16[2,512,128]{2,1,0:T(8,128)(2,1)S(1)}, bf16[2,512,128]{2,1,0:T(8,128)(2,1)S(1)}, u32[]{:S(2)}, u32[]{:S(2)}) %collective-permute-start.10) | collective-permute-done | bytes 262176 | tf_op jit(solution)/shard_map/ppermute | solution.py:259
  46.6 8.4 %attend.4.own_ref = bf16[256,512]{1,0:T(8,128)(2,1)S(1)} custom-call(s32[1,64]{1,0:T(1,128)S(1)} %get-tuple-element.62.doc_ref, bf16[512,512]{1,0:T(8,128)(2,1)S(1)} %get-tuple-element.63.q_ref, bf16[2,512,128]{2,1,0:T(8,128)(2,1)S(1)} %get-tuple-element.49.refs_0_, bf16[2,512,128]{2,1,0:T(8,128)(2,1)S(1)} %collective-permute-done.3.refs_1_, ...), custom_call_target="tpu_custom_call" | custom-call | flops 3000000000 | bytes 4000000 | tf_op jit(solution)/shard_map/attend/pallas_call | solution.py:224
  56.7 2.6 %first_blocks.2 = (bf16[128,2048]{1,0:T(8,128)(2,1)S(1)}, bf16[128,2048]{1,0:T(8,128)(2,1)S(1)}) custom-call(bf16[256,512]{1,0:T(8,128)(2,1)S(1)} %attend.4.own_ref, bf16[256,512]{1,0:T(8,128)(2,1)S(1)} %collective-permute-done.15.other_ref, bf16[1024,4096]{1,0:T(8,128)(2,1)S(1)} %bitcast.26), custom_call_target="tpu_custom_call" | custom-call | flops 1073741824 | bytes 12582912 | tf_op jit(solution)/shard_map/first_blocks/pallas_call | solution.py:366
  62.6 8.6 %attend.5 = bf16[256,512]{1,0:T(8,128)(2,1)S(1)} custom-call(s32[1,64]{1,0:T(1,128)S(1)} %get-tuple-element.62.doc_ref, bf16[512,512]{1,0:T(8,128)(2,1)S(1)} %get-tuple-element.63.q_ref, bf16[2,512,128]{2,1,0:T(8,128)(2,1)S(1)} %get-tuple-element.49.refs_0_, bf16[2,512,128]{2,1,0:T(8,128)(2,1)S(1)} %collective-permute-done.3.refs_1_, ...), custom_call_target="tpu_custom_call" | custom-call | flops 3000000000 | bytes 4000000 | tf_op jit(solution)/shard_map/attend/pallas_call | solution.py:224
  71.4 4.9 %collective-permute-start.26 = (bf16[2,512,128]{2,1,0:T(8,128)(2,1)S(1)}, bf16[2,512,128]{2,1,0:T(8,128)(2,1)S(1)}, u32[]{:S(2)}, u32[]{:S(2)}) collective-permute-start(bf16[2,512,128]{2,1,0:T(8,128)(2,1)S(1)} %slice_bitcast_fusion), channel_id=1, source_target_pairs={{0,24},{8,0},{16,8},{24,16},{32,56},{40,32},{48,40},{56,48},{64,88... | collective-permute-start | bytes 786440 | tf_op jit(solution)/shard_map/ppermute | solution.py:259
  78.0 2.3 %convolution_convert_fusion.3.p_ref = bf16[256,4096]{1,0:T(8,128)(2,1)S(1)} fusion(bf16[1024,4096]{1,0:T(8,128)(2,1)S(1)} %bitcast.26, bf16[256,512]{1,0:T(8,128)(2,1)S(1)} %collective-permute-done.18, bf16[256,512]{1,0:T(8,128)(2,1)S(1)} %attend.5, pred[]{:T(512)S(6)} %eq.34), kind=kOutput, calls=%fused_computation.3 | convolution fusion | flops 2150891520 | bytes 11010049 | tf_op jit(solution)/shard_map/dot_general | solution.py:416
  80.9 2.9 %collective-permute-start.20 = (bf16[128,2048]{1,0:T(8,128)(2,1)S(1)}, bf16[128,2048]{1,0:T(8,128)(2,1)S(1)}, u32[]{:S(2)}, u32[]{:S(2)}) collective-permute-start(bf16[128,2048]{1,0:T(8,128)(2,1)S(1)} %get-tuple-element.65), channel_id=1, source_target_pairs={{0,6},{2,0},{4,2},{6,4},{1,7},{3,1},{5,3},{7,5},{8,14},{10,8},{12,... | collective-permute-start | bytes 1572872 | tf_op jit(solution)/shard_map/ppermute | solution.py:340
  85.2 11.9 %attend.7 = bf16[256,512]{1,0:T(8,128)(2,1)S(1)} custom-call(s32[1,64]{1,0:T(1,128)S(1)} %get-tuple-element.98.doc_ref, bf16[512,512]{1,0:T(8,128)(2,1)S(1)} %get-tuple-element.94.q_ref, bf16[3,2,512,128]{3,2,1,0:T(8,128)(2,1)S(1)} %pad_maximum_fusion.2.refs_0_, bf16[3,2,512,128]{3,2,1,0:T(8,128)(2,1)S(1)} %collective-permute-done.23.refs_1_, ...), custom_call_target="tpu_custom_call" | custom-call | flops 3000000000 | bytes 4000000 | tf_op jit(solution)/shard_map/attend/pallas_call | solution.py:224
  97.2 11.8 %attend.6.own_ref = bf16[256,512]{1,0:T(8,128)(2,1)S(1)} custom-call(s32[1,64]{1,0:T(1,128)S(1)} %get-tuple-element.98.doc_ref, bf16[512,512]{1,0:T(8,128)(2,1)S(1)} %get-tuple-element.94.q_ref, bf16[3,2,512,128]{3,2,1,0:T(8,128)(2,1)S(1)} %pad_maximum_fusion.2.refs_0_, bf16[3,2,512,128]{3,2,1,0:T(8,128)(2,1)S(1)} %collective-permute-done.23.refs_1_, ...), custom_call_target="tpu_custom_call" | custom-call | flops 3000000000 | bytes 4000000 | tf_op jit(solution)/shard_map/attend/pallas_call | solution.py:224
  109.8 2.3 %convolution_convert_fusion.2.p_ref = bf16[256,4096]{1,0:T(8,128)(2,1)S(1)} fusion(bf16[1024,4096]{1,0:T(8,128)(2,1)S(1)} %bitcast.26, bf16[256,512]{1,0:T(8,128)(2,1)S(1)} %collective-permute-done.15.other_ref, bf16[256,512]{1,0:T(8,128)(2,1)S(1)} %attend.4.own_ref, pred[]{:T(512)S(6)} %eq.34), kind=kOutput, calls=%fused_computation.2 | convolution fusion | flops 2150891520 | bytes 11010049 | tf_op jit(solution)/shard_map/dot_general | solution.py:416
  112.2 2.6 %first_blocks.3 = (bf16[128,2048]{1,0:T(8,128)(2,1)S(1)}, bf16[128,2048]{1,0:T(8,128)(2,1)S(1)}) custom-call(bf16[256,512]{1,0:T(8,128)(2,1)S(1)} %attend.6.own_ref, bf16[256,512]{1,0:T(8,128)(2,1)S(1)} %collective-permute-done.29.other_ref, bf16[1024,4096]{1,0:T(8,128)(2,1)S(1)} %bitcast.26), custom_call_target="tpu_custom_call" | custom-call | flops 1073741824 | bytes 12582912 | tf_op jit(solution)/shard_map/first_blocks/pallas_call | solution.py:366
  115.2 2.9 %collective-permute-start.31 = (bf16[128,2048]{1,0:T(8,128)(2,1)S(1)}, bf16[128,2048]{1,0:T(8,128)(2,1)S(1)}, u32[]{:S(2)}, u32[]{:S(2)}) collective-permute-start(bf16[128,2048]{1,0:T(8,128)(2,1)S(1)} %get-tuple-element.78), channel_id=1, source_target_pairs={{0,6},{2,0},{4,2},{6,4},{1,7},{3,1},{5,3},{7,5},{8,14},{10,8},{12,... | collective-permute-start | bytes 1572872 | tf_op jit(solution)/shard_map/ppermute | solution.py:340
  118.3 2.3 %convolution_convert_fusion.1.p_ref = bf16[256,4096]{1,0:T(8,128)(2,1)S(1)} fusion(bf16[1024,4096]{1,0:T(8,128)(2,1)S(1)} %bitcast.26, bf16[256,512]{1,0:T(8,128)(2,1)S(1)} %collective-permute-done.32, bf16[256,512]{1,0:T(8,128)(2,1)S(1)} %attend.7, pred[]{:T(512)S(6)} %eq.34), kind=kOutput, calls=%fused_computation.1 | convolution fusion | flops 2150891520 | bytes 11010049 | tf_op jit(solution)/shard_map/dot_general | solution.py:416
  120.6 3.3 %collective-permute-start.22 = (bf16[128,2048]{1,0:T(8,128)(2,1)S(1)}, bf16[128,2048]{1,0:T(8,128)(2,1)S(1)}, u32[]{:S(2)}, u32[]{:S(2)}) collective-permute-start(bf16[128,2048]{1,0:T(8,128)(2,1)S(1)} %get-tuple-element.69), channel_id=1, source_target_pairs={{0,6},{2,0},{4,2},{6,4},{1,7},{3,1},{5,3},{7,5},{8,14},{10,8},{12,... | collective-permute-start | bytes 1572872 | tf_op jit(solution)/shard_map/ppermute | solution.py:340
  123.9 6.9 %collective-permute-done.30.ra_ref = bf16[128,2048]{1,0:T(8,128)(2,1)S(1)} collective-permute-done((bf16[128,2048]{1,0:T(8,128)(2,1)S(1)}, bf16[128,2048]{1,0:T(8,128)(2,1)S(1)}, u32[]{:S(2)}, u32[]{:S(2)}) %collective-permute-start.30) | collective-permute-done | bytes 524320 | tf_op jit(solution)/shard_map/ppermute | solution.py:340
  131.7 2.6 %collective-permute-start.38 = (bf16[128,1024]{1,0:T(8,128)(2,1)S(1)}, bf16[128,1024]{1,0:T(8,128)(2,1)S(1)}, u32[]{:S(2)}, u32[]{:S(2)}) collective-permute-start(bf16[128,1024]{1,0:T(8,128)(2,1)S(1)} %get-tuple-element.87), channel_id=1, source_target_pairs={{0,6},{2,0},{4,2},{6,4},{1,7},{3,1},{5,3},{7,5},{8,14},{10,8},{12,... | collective-permute-start | bytes 786440 | tf_op jit(solution)/shard_map/ppermute | solution.py:340
  134.5 7.6 %collective-permute-done.21.ra_ref = bf16[128,2048]{1,0:T(8,128)(2,1)S(1)} collective-permute-done((bf16[128,2048]{1,0:T(8,128)(2,1)S(1)}, bf16[128,2048]{1,0:T(8,128)(2,1)S(1)}, u32[]{:S(2)}, u32[]{:S(2)}) %collective-permute-start.21) | collective-permute-done | bytes 524320 | tf_op jit(solution)/shard_map/ppermute | solution.py:340
  142.7 2.3 %convolution_convert_fusion.p_ref = bf16[256,4096]{1,0:T(8,128)(2,1)S(1)} fusion(bf16[1024,4096]{1,0:T(8,128)(2,1)S(1)} %bitcast.26, bf16[256,512]{1,0:T(8,128)(2,1)S(1)} %collective-permute-done.29.other_ref, bf16[256,512]{1,0:T(8,128)(2,1)S(1)} %attend.6.own_ref, pred[]{:T(512)S(6)} %eq.34), kind=kOutput, calls=%fused_computation | convolution fusion | flops 2150891520 | bytes 11010049 | tf_op jit(solution)/shard_map/dot_general | solution.py:416
  145.1 2.6 %collective-permute-done.37.ra_ref = bf16[128,1024]{1,0:T(8,128)(2,1)S(1)} collective-permute-done((bf16[128,1024]{1,0:T(8,128)(2,1)S(1)}, bf16[128,1024]{1,0:T(8,128)(2,1)S(1)}, u32[]{:S(2)}, u32[]{:S(2)}) %collective-permute-start.37) | collective-permute-done | bytes 262176 | tf_op jit(solution)/shard_map/ppermute | solution.py:340
  148.6 2.6 %collective-permute-start.40 = (bf16[128,1024]{1,0:T(8,128)(2,1)S(1)}, bf16[128,1024]{1,0:T(8,128)(2,1)S(1)}, u32[]{:S(2)}, u32[]{:S(2)}) collective-permute-start(bf16[128,1024]{1,0:T(8,128)(2,1)S(1)} %get-tuple-element.89), channel_id=1, source_target_pairs={{0,6},{2,0},{4,2},{6,4},{1,7},{3,1},{5,3},{7,5},{8,14},{10,8},{12,... | collective-permute-start | bytes 786440 | tf_op jit(solution)/shard_map/ppermute | solution.py:340
  151.2 2.2 %collective-permute-done.33.ra_ref = bf16[128,1024]{1,0:T(8,128)(2,1)S(1)} collective-permute-done((bf16[128,1024]{1,0:T(8,128)(2,1)S(1)}, bf16[128,1024]{1,0:T(8,128)(2,1)S(1)}, u32[]{:S(2)}, u32[]{:S(2)}) %collective-permute-start.33) | collective-permute-done | bytes 262176 | tf_op jit(solution)/shard_map/ppermute | solution.py:340
  154.2 2.6 %collective-permute-start.36 = (bf16[128,1024]{1,0:T(8,128)(2,1)S(1)}, bf16[128,1024]{1,0:T(8,128)(2,1)S(1)}, u32[]{:S(2)}, u32[]{:S(2)}) collective-permute-start(bf16[128,1024]{1,0:T(8,128)(2,1)S(1)} %get-tuple-element.84), channel_id=1, source_target_pairs={{0,6},{2,0},{4,2},{6,4},{1,7},{3,1},{5,3},{7,5},{8,14},{10,8},{12,... | collective-permute-start | bytes 786440 | tf_op jit(solution)/shard_map/ppermute | solution.py:340
  156.9 2.1 %collective-permute-done.39.ra_ref = bf16[128,1024]{1,0:T(8,128)(2,1)S(1)} collective-permute-done((bf16[128,1024]{1,0:T(8,128)(2,1)S(1)}, bf16[128,1024]{1,0:T(8,128)(2,1)S(1)}, u32[]{:S(2)}, u32[]{:S(2)}) %collective-permute-start.39) | collective-permute-done | bytes 262176 | tf_op jit(solution)/shard_map/ppermute | solution.py:340
  159.0 4.6 %collective-permute-done.35.ra_ref = bf16[128,1024]{1,0:T(8,128)(2,1)S(1)} collective-permute-done((bf16[128,1024]{1,0:T(8,128)(2,1)S(1)}, bf16[128,1024]{1,0:T(8,128)(2,1)S(1)}, u32[]{:S(2)}, u32[]{:S(2)}) %collective-permute-start.35) | collective-permute-done | bytes 262176 | tf_op jit(solution)/shard_map/ppermute | solution.py:340
  163.8 3.9 %broadcast_select_fusion = bf16[128,2,4096]{2,1,0:T(2,128)(2,1)} fusion(pred[2]{0:T(512)(128)(4,1)S(1)} %iota_compare_fusion, bf16[128,4096]{1,0:T(8,128)(2,1)S(1)} %pad_maximum_fusion.1, bf16[128,4096]{1,0:T(8,128)(2,1)S(1)} %pad_maximum_fusion), kind=kLoop, calls=%fused_computation.4 | loop fusion | flops 1048576 | bytes 4194306 | tf_op jit(solution)/shard_map/jit(_where)/select_n | solution.py:471
  (98 shorter events, 33.2 us)
Async XLA Ops:
  3.8 10.7 %collective-permute-start.4 = (bf16[2,512,128]{2,1,0:T(8,128)(2,1)S(1)}, bf16[2,512,128]{2,1,0:T(8,128)(2,1)S(1)}, u32[]{:S(2)}, u32[]{:S(2)}) collective-permute-start(bf16[2,512,128]{2,1,0:T(8,128)(2,1)S(1)} %get-tuple-element.49.refs_0_), channel_id=1, source_target_pairs={{0,64},{8,72},{16,80},{24,88},{32,96},{40,104},{48,112},{56,120},{... | collective-permute-start | bytes 786440 | tf_op jit(solution)/shard_map/ppermute | solution.py:264
  4.4 12.1 %collective-permute-start = (s32[1,64]{1,0:T(1,128)S(1)}, s32[1,64]{1,0:T(1,128)S(1)}, u32[]{:S(2)}, u32[]{:S(2)}) collective-permute-start(s32[1,64]{1,0:T(1,128)S(1)} %copy-done.1), channel_id=1, source_target_pairs={{0,1},{1,0},{2,3},{3,2},{4,5},{5,4},{6,7},{7,6},{8,9},{9,8},{10,11... | collective-permute-start | bytes 776 | tf_op jit(solution)/shard_map/ppermute | solution.py:391
  4.7 11.8 %collective-permute-start.5 = (bf16[2,512,128]{2,1,0:T(8,128)(2,1)S(1)}, bf16[2,512,128]{2,1,0:T(8,128)(2,1)S(1)}, u32[]{:S(2)}, u32[]{:S(2)}) collective-permute-start(bf16[2,512,128]{2,1,0:T(8,128)(2,1)S(1)} %get-tuple-element.49.refs_0_), channel_id=1, source_target_pairs={{0,8},{8,16},{16,24},{32,40},{40,48},{48,56},{64,72},{72,80},{80,8... | collective-permute-start | bytes 786440 | tf_op jit(solution)/shard_map/ppermute | solution.py:270
  8.6 11.5 %collective-permute-start.3 = (bf16[2,512,128]{2,1,0:T(8,128)(2,1)S(1)}, bf16[2,512,128]{2,1,0:T(8,128)(2,1)S(1)}, u32[]{:S(2)}, u32[]{:S(2)}) collective-permute-start(bf16[2,512,128]{2,1,0:T(8,128)(2,1)S(1)} %get-tuple-element.49.refs_0_), channel_id=1, source_target_pairs={{0,32},{8,40},{16,48},{24,56},{32,64},{40,72},{48,80},{56,88},{64,... | collective-permute-start | bytes 786440 | tf_op jit(solution)/shard_map/ppermute | solution.py:264
  10.8 21.8 %collective-permute-start.1 = (bf16[512,512]{1,0:T(8,128)(2,1)S(1)}, bf16[512,512]{1,0:T(8,128)(2,1)S(1)}, u32[]{:S(2)}, u32[]{:S(2)}) collective-permute-start(bf16[512,512]{1,0:T(8,128)(2,1)S(1)} %broadcast_select_fusion.3), channel_id=1, source_target_pairs={{0,1},{1,0},{2,3},{3,2},{4,5},{5,4},{6,7},{7,6},{8,9},{9,8},{10,11... | collective-permute-start | bytes 1572872 | tf_op jit(solution)/shard_map/ppermute | solution.py:391
  16.5 10.7 %collective-permute-start.14 = (bf16[2,512,128]{2,1,0:T(8,128)(2,1)S(1)}, bf16[2,512,128]{2,1,0:T(8,128)(2,1)S(1)}, u32[]{:S(2)}, u32[]{:S(2)}) collective-permute-start(bf16[2,512,128]{2,1,0:T(8,128)(2,1)S(1)} %get-tuple-element.72), channel_id=1, source_target_pairs={{0,64},{8,72},{16,80},{24,88},{32,96},{40,104},{48,112},{56,120},{... | collective-permute-start | bytes 786440 | tf_op jit(solution)/shard_map/ppermute | solution.py:264
  16.5 14.1 %collective-permute-start.13 = (bf16[2,512,128]{2,1,0:T(8,128)(2,1)S(1)}, bf16[2,512,128]{2,1,0:T(8,128)(2,1)S(1)}, u32[]{:S(2)}, u32[]{:S(2)}) collective-permute-start(bf16[2,512,128]{2,1,0:T(8,128)(2,1)S(1)} %get-tuple-element.72), channel_id=1, source_target_pairs={{0,32},{8,40},{16,48},{24,56},{32,64},{40,72},{48,80},{56,88},{64,... | collective-permute-start | bytes 786440 | tf_op jit(solution)/shard_map/ppermute | solution.py:264
  20.0 14.1 %collective-permute-start.9 = (bf16[2,512,128]{2,1,0:T(8,128)(2,1)S(1)}, bf16[2,512,128]{2,1,0:T(8,128)(2,1)S(1)}, u32[]{:S(2)}, u32[]{:S(2)}) collective-permute-start(bf16[2,512,128]{2,1,0:T(8,128)(2,1)S(1)} %collective-permute-done.3.refs_1_), channel_id=1, source_target_pairs={{0,24},{8,0},{16,8},{24,16},{32,56},{40,32},{48,40},{56,48},{64,88... | collective-permute-start | bytes 786440 | tf_op jit(solution)/shard_map/ppermute | solution.py:259
  21.3 14.2 %collective-permute-start.8 = (bf16[2,512,128]{2,1,0:T(8,128)(2,1)S(1)}, bf16[2,512,128]{2,1,0:T(8,128)(2,1)S(1)}, u32[]{:S(2)}, u32[]{:S(2)}) collective-permute-start(bf16[2,512,128]{2,1,0:T(8,128)(2,1)S(1)} %broadcast_select_fusion.6), channel_id=1, source_target_pairs={{0,24},{8,0},{16,8},{24,16},{32,56},{40,32},{48,40},{56,48},{64,88... | collective-permute-start | bytes 786440 | tf_op jit(solution)/shard_map/ppermute | solution.py:259
  32.5 11.9 %collective-permute-start.10 = (bf16[2,512,128]{2,1,0:T(8,128)(2,1)S(1)}, bf16[2,512,128]{2,1,0:T(8,128)(2,1)S(1)}, u32[]{:S(2)}, u32[]{:S(2)}) collective-permute-start(bf16[2,512,128]{2,1,0:T(8,128)(2,1)S(1)} %broadcast_select_fusion.5), channel_id=1, source_target_pairs={{0,8},{8,16},{16,24},{24,0},{32,40},{40,48},{48,56},{56,32},{64,72... | collective-permute-start | bytes 786440 | tf_op jit(solution)/shard_map/ppermute | solution.py:259
  34.2 10.3 %collective-permute-start.11 = (bf16[2,512,128]{2,1,0:T(8,128)(2,1)S(1)}, bf16[2,512,128]{2,1,0:T(8,128)(2,1)S(1)}, u32[]{:S(2)}, u32[]{:S(2)}) collective-permute-start(bf16[2,512,128]{2,1,0:T(8,128)(2,1)S(1)} %collective-permute-done.9.refs_7_), channel_id=1, source_target_pairs={{0,24},{8,0},{16,8},{24,16},{32,56},{40,32},{48,40},{56,48},{64,88... | collective-permute-start | bytes 786440 | tf_op jit(solution)/shard_map/ppermute | solution.py:259
  34.7 21.3 %collective-permute-start.27 = (bf16[2,512,128]{2,1,0:T(8,128)(2,1)S(1)}, bf16[2,512,128]{2,1,0:T(8,128)(2,1)S(1)}, u32[]{:S(2)}, u32[]{:S(2)}) collective-permute-start(bf16[2,512,128]{2,1,0:T(8,128)(2,1)S(1)} %get-tuple-element.72), channel_id=1, source_target_pairs={{24,0},{25,1},{26,2},{27,3},{28,4},{29,5},{30,6},{31,7}} | collective-permute-start | bytes 786440 | tf_op jit(solution)/shard_map/ppermute | solution.py:423
  44.6 26.8 %collective-permute-start.23 = (bf16[3,2,512,128]{3,2,1,0:T(8,128)(2,1)S(1)}, bf16[3,2,512,128]{3,2,1,0:T(8,128)(2,1)S(1)}, u32[]{:S(2)}, u32[]{:S(2)}) collective-permute-start(bf16[3,2,512,128]{3,2,1,0:T(8,128)(2,1)S(1)} %pad_maximum_fusion.2.refs_0_), channel_id=1, source_target_pairs={{0,8},{8,16},{16,24},{24,0},{32,40},{40,48},{48,56},{56,32},{64,72... | collective-permute-start | bytes 2359304 | tf_op jit(solution)/shard_map/ppermute | solution.py:259
  55.2 16.1 %collective-permute-start.24 = (bf16[2,2,512,128]{3,2,1,0:T(8,128)(2,1)S(1)}, bf16[2,2,512,128]{3,2,1,0:T(8,128)(2,1)S(1)}, u32[]{:S(2)}, u32[]{:S(2)}) collective-permute-start(bf16[2,2,512,128]{3,2,1,0:T(8,128)(2,1)S(1)} %pad_maximum_fusion.3), channel_id=1, source_target_pairs={{0,24},{8,0},{16,8},{24,16},{32,56},{40,32},{48,40},{56,48},{64,88... | collective-permute-start | bytes 1572872 | tf_op jit(solution)/shard_map/ppermute | solution.py:259
  56.0 27.8 %collective-permute-start.28 = (bf16[2,512,128]{2,1,0:T(8,128)(2,1)S(1)}, bf16[2,512,128]{2,1,0:T(8,128)(2,1)S(1)}, u32[]{:S(2)}, u32[]{:S(2)}) collective-permute-start(bf16[2,512,128]{2,1,0:T(8,128)(2,1)S(1)} %collective-permute-done.27), channel_id=1, source_target_pairs={{0,96},{1,97},{2,98},{3,99},{4,100},{5,101},{6,102},{7,103}} | collective-permute-start | bytes 786440 | tf_op jit(solution)/shard_map/ppermute | solution.py:274
  59.3 21.0 %collective-permute-start.16 = (bf16[128,2048]{1,0:T(8,128)(2,1)S(1)}, bf16[128,2048]{1,0:T(8,128)(2,1)S(1)}, u32[]{:S(2)}, u32[]{:S(2)}) collective-permute-start(bf16[128,2048]{1,0:T(8,128)(2,1)S(1)} %get-tuple-element.60), channel_id=1, source_target_pairs={{0,2},{2,4},{4,6},{6,0},{1,3},{3,5},{5,7},{7,1},{8,10},{10,12},{12... | collective-permute-start | bytes 1572872 | tf_op jit(solution)/shard_map/ppermute | solution.py:340
  60.9 19.4 %collective-permute-start.17 = (bf16[128,2048]{1,0:T(8,128)(2,1)S(1)}, bf16[128,2048]{1,0:T(8,128)(2,1)S(1)}, u32[]{:S(2)}, u32[]{:S(2)}) collective-permute-start(bf16[128,2048]{1,0:T(8,128)(2,1)S(1)} %get-tuple-element.61), channel_id=1, source_target_pairs={{0,6},{2,0},{4,2},{6,4},{1,7},{3,1},{5,3},{7,5},{8,14},{10,8},{12,... | collective-permute-start | bytes 1572872 | tf_op jit(solution)/shard_map/ppermute | solution.py:340
  71.4 12.4 %collective-permute-start.26 = (bf16[2,512,128]{2,1,0:T(8,128)(2,1)S(1)}, bf16[2,512,128]{2,1,0:T(8,128)(2,1)S(1)}, u32[]{:S(2)}, u32[]{:S(2)}) collective-permute-start(bf16[2,512,128]{2,1,0:T(8,128)(2,1)S(1)} %slice_bitcast_fusion), channel_id=1, source_target_pairs={{0,24},{8,0},{16,8},{24,16},{32,56},{40,32},{48,40},{56,48},{64,88... | collective-permute-start | bytes 786440 | tf_op jit(solution)/shard_map/ppermute | solution.py:259
  80.5 37.6 %collective-permute-start.19 = (bf16[128,2048]{1,0:T(8,128)(2,1)S(1)}, bf16[128,2048]{1,0:T(8,128)(2,1)S(1)}, u32[]{:S(2)}, u32[]{:S(2)}) collective-permute-start(bf16[128,2048]{1,0:T(8,128)(2,1)S(1)} %get-tuple-element.64), channel_id=1, source_target_pairs={{0,2},{2,4},{4,6},{6,0},{1,3},{3,5},{5,7},{7,1},{8,10},{10,12},{12... | collective-permute-start | bytes 1572872 | tf_op jit(solution)/shard_map/ppermute | solution.py:340
  80.9 37.2 %collective-permute-start.20 = (bf16[128,2048]{1,0:T(8,128)(2,1)S(1)}, bf16[128,2048]{1,0:T(8,128)(2,1)S(1)}, u32[]{:S(2)}, u32[]{:S(2)}) collective-permute-start(bf16[128,2048]{1,0:T(8,128)(2,1)S(1)} %get-tuple-element.65), channel_id=1, source_target_pairs={{0,6},{2,0},{4,2},{6,4},{1,7},{3,1},{5,3},{7,5},{8,14},{10,8},{12,... | collective-permute-start | bytes 1572872 | tf_op jit(solution)/shard_map/ppermute | solution.py:340
  97.1 21.2 %collective-permute-start.32 = (bf16[256,512]{1,0:T(8,128)(2,1)S(1)}, bf16[256,512]{1,0:T(8,128)(2,1)S(1)}, u32[]{:S(2)}, u32[]{:S(2)}) collective-permute-start(bf16[256,512]{1,0:T(8,128)(2,1)S(1)} %attend.7), channel_id=1, source_target_pairs={{0,1},{1,0},{2,3},{3,2},{4,5},{5,4},{6,7},{7,6},{8,9},{9,8},{10,11... | collective-permute-start | bytes 786440 | tf_op jit(solution)/shard_map/ppermute | solution.py:391
  114.8 16.1 %collective-permute-start.30 = (bf16[128,2048]{1,0:T(8,128)(2,1)S(1)}, bf16[128,2048]{1,0:T(8,128)(2,1)S(1)}, u32[]{:S(2)}, u32[]{:S(2)}) collective-permute-start(bf16[128,2048]{1,0:T(8,128)(2,1)S(1)} %get-tuple-element.77), channel_id=1, source_target_pairs={{0,2},{2,4},{4,6},{6,0},{1,3},{3,5},{5,7},{7,1},{8,10},{10,12},{12... | collective-permute-start | bytes 1572872 | tf_op jit(solution)/shard_map/ppermute | solution.py:340
  115.2 15.6 %collective-permute-start.31 = (bf16[128,2048]{1,0:T(8,128)(2,1)S(1)}, bf16[128,2048]{1,0:T(8,128)(2,1)S(1)}, u32[]{:S(2)}, u32[]{:S(2)}) collective-permute-start(bf16[128,2048]{1,0:T(8,128)(2,1)S(1)} %get-tuple-element.78), channel_id=1, source_target_pairs={{0,6},{2,0},{4,2},{6,4},{1,7},{3,1},{5,3},{7,5},{8,14},{10,8},{12,... | collective-permute-start | bytes 1572872 | tf_op jit(solution)/shard_map/ppermute | solution.py:340
  118.2 23.9 %collective-permute-start.21 = (bf16[128,2048]{1,0:T(8,128)(2,1)S(1)}, bf16[128,2048]{1,0:T(8,128)(2,1)S(1)}, u32[]{:S(2)}, u32[]{:S(2)}) collective-permute-start(bf16[128,2048]{1,0:T(8,128)(2,1)S(1)} %get-tuple-element.68), channel_id=1, source_target_pairs={{0,2},{2,4},{4,6},{6,0},{1,3},{3,5},{5,7},{7,1},{8,10},{10,12},{12... | collective-permute-start | bytes 1572872 | tf_op jit(solution)/shard_map/ppermute | solution.py:340
  120.6 24.4 %collective-permute-start.22 = (bf16[128,2048]{1,0:T(8,128)(2,1)S(1)}, bf16[128,2048]{1,0:T(8,128)(2,1)S(1)}, u32[]{:S(2)}, u32[]{:S(2)}) collective-permute-start(bf16[128,2048]{1,0:T(8,128)(2,1)S(1)} %get-tuple-element.69), channel_id=1, source_target_pairs={{0,6},{2,0},{4,2},{6,4},{1,7},{3,1},{5,3},{7,5},{8,14},{10,8},{12,... | collective-permute-start | bytes 1572872 | tf_op jit(solution)/shard_map/ppermute | solution.py:340
  130.9 16.8 %collective-permute-start.37 = (bf16[128,1024]{1,0:T(8,128)(2,1)S(1)}, bf16[128,1024]{1,0:T(8,128)(2,1)S(1)}, u32[]{:S(2)}, u32[]{:S(2)}) collective-permute-start(bf16[128,1024]{1,0:T(8,128)(2,1)S(1)} %get-tuple-element.86), channel_id=1, source_target_pairs={{0,2},{2,4},{4,6},{6,0},{1,3},{3,5},{5,7},{7,1},{8,10},{10,12},{12... | collective-permute-start | bytes 786440 | tf_op jit(solution)/shard_map/ppermute | solution.py:340
  131.7 16.0 %collective-permute-start.38 = (bf16[128,1024]{1,0:T(8,128)(2,1)S(1)}, bf16[128,1024]{1,0:T(8,128)(2,1)S(1)}, u32[]{:S(2)}, u32[]{:S(2)}) collective-permute-start(bf16[128,1024]{1,0:T(8,128)(2,1)S(1)} %get-tuple-element.87), channel_id=1, source_target_pairs={{0,6},{2,0},{4,2},{6,4},{1,7},{3,1},{5,3},{7,5},{8,14},{10,8},{12,... | collective-permute-start | bytes 786440 | tf_op jit(solution)/shard_map/ppermute | solution.py:340
  134.4 18.9 %collective-permute-start.33 = (bf16[128,1024]{1,0:T(8,128)(2,1)S(1)}, bf16[128,1024]{1,0:T(8,128)(2,1)S(1)}, u32[]{:S(2)}, u32[]{:S(2)}) collective-permute-start(bf16[128,1024]{1,0:T(8,128)(2,1)S(1)} %get-tuple-element.79), channel_id=1, source_target_pairs={{0,2},{2,4},{4,6},{6,0},{1,3},{3,5},{5,7},{7,1},{8,10},{10,12},{12... | collective-permute-start | bytes 786440 | tf_op jit(solution)/shard_map/ppermute | solution.py:340
  142.1 11.2 %collective-permute-start.34 = (bf16[128,1024]{1,0:T(8,128)(2,1)S(1)}, bf16[128,1024]{1,0:T(8,128)(2,1)S(1)}, u32[]{:S(2)}, u32[]{:S(2)}) collective-permute-start(bf16[128,1024]{1,0:T(8,128)(2,1)S(1)} %get-tuple-element.80), channel_id=1, source_target_pairs={{0,6},{2,0},{4,2},{6,4},{1,7},{3,1},{5,3},{7,5},{8,14},{10,8},{12,... | collective-permute-start | bytes 786440 | tf_op jit(solution)/shard_map/ppermute | solution.py:340
  147.8 11.2 %collective-permute-start.39 = (bf16[128,1024]{1,0:T(8,128)(2,1)S(1)}, bf16[128,1024]{1,0:T(8,128)(2,1)S(1)}, u32[]{:S(2)}, u32[]{:S(2)}) collective-permute-start(bf16[128,1024]{1,0:T(8,128)(2,1)S(1)} %get-tuple-element.88), channel_id=1, source_target_pairs={{0,2},{2,4},{4,6},{6,0},{1,3},{3,5},{5,7},{7,1},{8,10},{10,12},{12... | collective-permute-start | bytes 786440 | tf_op jit(solution)/shard_map/ppermute | solution.py:340
  148.6 10.4 %collective-permute-start.40 = (bf16[128,1024]{1,0:T(8,128)(2,1)S(1)}, bf16[128,1024]{1,0:T(8,128)(2,1)S(1)}, u32[]{:S(2)}, u32[]{:S(2)}) collective-permute-start(bf16[128,1024]{1,0:T(8,128)(2,1)S(1)} %get-tuple-element.89), channel_id=1, source_target_pairs={{0,6},{2,0},{4,2},{6,4},{1,7},{3,1},{5,3},{7,5},{8,14},{10,8},{12,... | collective-permute-start | bytes 786440 | tf_op jit(solution)/shard_map/ppermute | solution.py:340
  153.4 10.2 %collective-permute-start.35 = (bf16[128,1024]{1,0:T(8,128)(2,1)S(1)}, bf16[128,1024]{1,0:T(8,128)(2,1)S(1)}, u32[]{:S(2)}, u32[]{:S(2)}) collective-permute-start(bf16[128,1024]{1,0:T(8,128)(2,1)S(1)} %get-tuple-element.83), channel_id=1, source_target_pairs={{0,2},{2,4},{4,6},{6,0},{1,3},{3,5},{5,7},{7,1},{8,10},{10,12},{12... | collective-permute-start | bytes 786440 | tf_op jit(solution)/shard_map/ppermute | solution.py:340
  (13 other events, 94.3 us)
